TPU v7x, 128 devices: a whole 4x4x4 slice. The times are simulated.
128 devices in a mesh: leaf: 32 (over y, x, core), rhs: 4 (over z).
Axes of the slice: x: 4, y: 4, z: 4, core: 2. Of those that a mesh axis runs over, the one named last changes fastest.
Arguments:
- rhs_cols: bfloat16 [262144, 512], P('leaf', 'rhs'), may hold values from -6 to 6
- leaf_inv: bfloat16 [512, 512, 512], P('leaf', 'rhs')
- leaf_basis: bfloat16 [512, 512, 128], P('leaf'), may hold values from -0.25 to 0.25
- leaf_back: bfloat16 [512, 512, 128], P('leaf'), may hold values from -0.5 to 0.5
- leaf_coarse: float32 [512, 128, 128], P('leaf')
- mid_inv: float32 [480, 256, 256], P('leaf')
- mid_basis: float32 [480, 256, 128], P('leaf'), may hold values from -0.375 to 0.375
- mid_back: float32 [480, 256, 128], P('leaf'), may hold values from -0.5 to 0.5
- mid_coarse: float32 [480, 128, 128], P('leaf')
- top_inv: float32 [32, 256, 256], P('leaf')
- top_basis: float32 [32, 256, 128], P('leaf'), may hold values from -0.375 to 0.375
- top_back: float32 [32, 256, 128], P('leaf'), may hold values from -0.5 to 0.5
- top_coarse: float32 [32, 128, 128], P('leaf')
Outputs:
- solution: float32 [262144, 512], P('leaf', 'rhs')
All inputs are finite; a program needn't handle non-finite values.
Results may differ from a plain program's by a relative error of at most 0.004.
Values may be sent and summed in bfloat16 or wider, within the bound.
No kernel may reach another device: no remote copies, remote signals or barrier semaphores. Data moves between devices by JAX's collectives and lax.ppermute only.
A program may use at most 192 MiB of HBM per device.

v0:
```python
import math

import jax
import jax.numpy as jnp
from jax import lax
from jax.sharding import PartitionSpec as P

exact_mode = lax.Precision.HIGHEST


def swapped(array, axis, bit):
    return lax.ppermute(array, axis, [(i, i ^ 1 << bit) for i in range(lax.axis_size(axis))])


def sent_together(arrays, axis, dim, along):
    widths = [math.prod(a.shape[along:]) for a in arrays]
    both = jnp.concatenate(
        [a.reshape(*a.shape[:along], w) for a, w in zip(arrays, widths)], axis=along
    )
    result = lax.all_gather(both, axis, axis=dim, tiled=True)
    tiles = jnp.split(result, [sum(widths[:k]) for k in range(1, len(widths))], axis=along)
    return tuple(
        (b.reshape(*result.shape[:along], *a.shape[along:]) for a, b in zip(arrays, tiles))
    )


def node_up(inverse, basis_mat, coarse, stacked):
    solved = jnp.einsum("nij,njc->nic", inverse, stacked, precision=exact_mode)
    reduced = jnp.einsum("nik,nic->nkc", basis_mat, solved, precision=exact_mode)
    upward = jnp.einsum("nkl,nlc->nkc", coarse, reduced, precision=exact_mode)
    return (solved, reduced, upward)


def node_down(solved, reduced, back_mat, parent_part):
    return solved - jnp.einsum(
        "nik,nkc->nic", back_mat, reduced - parent_part, precision=exact_mode
    )


def top_doubling(current, every_inv, every_basis, every_back, every_coarse, tree_depth, position):
    basis_rank = current.shape[1]
    stored = []
    for height in range(1, tree_depth + 1):
        level_bit = height - 1
        partner = swapped(current, "leaf", level_bit)
        is_left = (position >> level_bit) % 2 == 0
        left_part = jnp.where(is_left, current, partner)
        right_part = jnp.where(is_left, partner, current)
        stacked = jnp.concatenate([left_part, right_part], axis=1)
        entry = (position >> height) * (1 << height) + (1 << height - 1)
        node_inv = lax.dynamic_slice_in_dim(every_inv, entry, 1, 0)
        node_basis = lax.dynamic_slice_in_dim(every_basis, entry, 1, 0)
        node_back = lax.dynamic_slice_in_dim(every_back, entry, 1, 0)
        node_coarse = lax.dynamic_slice_in_dim(every_coarse, entry, 1, 0)
        solved, reduced, current = node_up(node_inv, node_basis, node_coarse, stacked)
        stored.append((solved, reduced, node_back, is_left))
    parent_part = None
    for height in range(tree_depth, 0, -1):
        solved, reduced, node_back, is_left = stored[height - 1]
        if parent_part is None:
            halves = solved
        else:
            halves = node_down(solved, reduced, node_back, parent_part)
        parent_part = jnp.where(is_left, halves[:, :basis_rank], halves[:, basis_rank:])
    return parent_part


def per_device(
    rhs_cols,
    leaf_inv,
    leaf_basis,
    leaf_back,
    leaf_coarse,
    mid_inv,
    mid_basis,
    mid_back,
    mid_coarse,
    top_inv,
    top_basis,
    top_back,
    top_coarse,
):
    leaf_count = leaf_inv.shape[0]
    leaf_width = leaf_inv.shape[2]
    basis_rank = leaf_basis.shape[2]
    columns = rhs_cols.shape[1]
    blocks = rhs_cols.reshape(leaf_count, leaf_width, columns)
    leaf_vals = jnp.einsum(
        "nij,njc->nic",
        lax.all_gather(leaf_inv, "rhs", axis=1, tiled=True),
        blocks,
        preferred_element_type=jnp.float32,
    ).astype(jnp.bfloat16)
    leaf_proj = jnp.einsum(
        "nik,nic->nkc", leaf_basis, leaf_vals, preferred_element_type=jnp.float32
    )
    current = jnp.einsum("nkl,nlc->nkc", leaf_coarse, leaf_proj, precision=exact_mode)
    local_levels = leaf_count.bit_length() - 1
    stored = []
    for height in range(1, local_levels + 1):
        offset = leaf_count - (leaf_count >> height - 1)
        node_count = leaf_count >> height
        stacked = current.reshape(node_count, 2 * basis_rank, columns)
        solved, reduced, current = node_up(
            mid_inv[offset : offset + node_count],
            mid_basis[offset : offset + node_count],
            mid_coarse[offset : offset + node_count],
            stacked,
        )
        stored.append((solved, reduced, mid_back[offset : offset + node_count]))
    leaf_total = lax.axis_size("leaf")
    tree_depth = leaf_total.bit_length() - 1
    position = lax.axis_index("leaf")
    every_inv, every_basis, every_back, every_coarse = sent_together(
        (top_inv, top_basis, top_back, top_coarse), "leaf", 0, 1
    )
    parent_part = top_doubling(
        current, every_inv, every_basis, every_back, every_coarse, tree_depth, position
    )
    for solved, reduced, back_part in reversed(stored):
        halves = node_down(solved, reduced, back_part, parent_part)
        parent_part = halves.reshape(2 * halves.shape[0], basis_rank, columns)
    difference = (leaf_proj - parent_part).astype(jnp.bfloat16)
    result = leaf_vals.astype(jnp.float32) - jnp.einsum(
        "nik,nkc->nic", leaf_back, difference, preferred_element_type=jnp.float32
    )
    return result.reshape(leaf_count * leaf_width, columns)


def solution(mesh):
    return jax.shard_map(
        per_device,
        mesh=mesh,
        in_specs=(
            P("leaf", "rhs"),
            P("leaf", "rhs", None),
            P("leaf", None, None),
            P("leaf", None, None),
            P("leaf", None, None),
            P("leaf", None, None),
            P("leaf", None, None),
            P("leaf", None, None),
            P("leaf", None, None),
            P("leaf", None, None),
            P("leaf", None, None),
            P("leaf", None, None),
            P("leaf", None, None),
        ),
        out_specs=P("leaf", "rhs"),
        check_vma=False,
    )
```

profile of v0, /device:TPU:0, one launch (start us, length us, event | category | flops | bytes accessed | tf_op | source)
XLA Modules:
  0.0 298.7 jit_solution(11918203498356709517)
XLA Ops:
  8.5 5.1 %maximum_bitcast_fusion = f32[1,1,147456]{2,1,0:T(1,128)} fusion(f32[1,16384]{1,0:T(1,128)} %bitcast.266, f32[1,32768]{1,0:T(1,128)} %bitcast.264, f32[1,32768]{1,0:T(1,128)} %bitcast.265, f32[1,65536]{1,0:T(1,128)S(1)} %bitcast.260), kind=kLoop, calls=%fused_computation.37 | loop fusion | flops 442368 | bytes 1179648
  13.7 81.1 %all-gather.4.cloned.1.call-done = bf16[16,512,512]{2,1,0:T(8,128)(2,1)} async-done(((bf16[16,128,512]{2,1,0:T(8,128)(2,1)}), bf16[16,512,512]{2,1,0:T(8,128)(2,1)}) %all-gather.4.cloned.1.call-update) | async-done | bytes 8388624 | tf_op jit(solution)/shard_map/all_gather | solution.py:90
  94.8 5.9 %convolution_convert_fusion = bf16[16,512,128]{2,1,0:T(8,128)(2,1)S(1)} fusion(bf16[16,512,512]{2,1,0:T(8,128)(2,1)} %all-gather.4.cloned.1.call-done, bf16[16,512,128]{2,1,0:T(8,128)(2,1)S(1)} %bitcast.232), kind=kOutput, calls=%fused_computation.7 | convolution fusion | flops 1074790400 | bytes 12582912 | tf_op jit(solution)/shard_map/nij,njc->nic/dot_general | solution.py:88
  102.7 2.3 fusion.146
  105.0 2.3 fusion
  117.8 57.3 %all-gather.6.cloned.1.call-done = f32[32,1,147456]{2,1,0:T(1,128)} async-done(((f32[1,1,147456]{2,1,0:T(1,128)}), f32[32,1,147456]{2,1,0:T(1,128)}) %all-gather.6.cloned.1.call-update) | async-done | bytes 18874384 | tf_op jit(solution)/shard_map/all_gather | solution.py:20
  175.1 17.0 %copy.68 = f32[32,1,147456]{2,0,1:T(8,128)S(1)} copy(f32[32,1,147456]{2,1,0:T(1,128)} %all-gather.6.cloned.1.call-done) | data formatting | bytes 37748736
  193.6 3.8 %split.16 = f32[32,65536]{1,0:T(8,128)} slice(f32[32,147456]{1,0:T(8,128)S(1)} %bitcast.234), slice={[0:32], [0:65536]} | slice | bytes 16777216 | tf_op jit(solution)/shard_map/split | solution.py:21
  197.4 4.0 %slice_bitcast_fusion = (f32[4,8,256,128]{3,1,2,0:T(8,128)}, f32[4,8,256,128]{3,1,2,0:T(8,128)}) fusion(f32[32,147456]{1,0:T(8,128)S(1)} %bitcast.235), kind=kLoop, calls=%fused_computation.1 | loop fusion | bytes 16777216
  204.3 2.9 copy.65
  209.2 2.6 copy.63
  211.8 3.3 %copy-done.4 = f32[4,8,256,256]{3,2,1,0:T(8,128)} copy-done((f32[4,8,256,256]{3,2,1,0:T(8,128)}, f32[4,8,256,256]{3,2,1,0:T(8,128)S(1)}, u32[]{:S(2)}) %copy-start.4) | copy-done | bytes 8388632
  219.1 3.1 %collective-permute-done.1 = f32[1,128,128]{2,1,0:T(8,128)} collective-permute-done((f32[1,128,128]{2,1,0:T(8,128)}, f32[1,128,128]{2,1,0:T(8,128)}, u32[]{:S(2)}, u32[]{:S(2)}) %collective-permute-start.1) | collective-permute-done | bytes 65568 | tf_op jit(solution)/shard_map/ppermute | solution.py:12
  228.7 3.0 collective-permute-start.2
  231.6 3.1 %collective-permute-done.2 = f32[1,128,128]{2,1,0:T(8,128)} collective-permute-done((f32[1,128,128]{2,1,0:T(8,128)}, f32[1,128,128]{2,1,0:T(8,128)}, u32[]{:S(2)}, u32[]{:S(2)}) %collective-permute-start.2) | collective-permute-done | bytes 65568 | tf_op jit(solution)/shard_map/ppermute | solution.py:12
  242.3 3.5 %collective-permute-done.3 = f32[1,128,128]{2,1,0:T(8,128)} collective-permute-done((f32[1,128,128]{2,1,0:T(8,128)}, f32[1,128,128]{2,1,0:T(8,128)}, u32[]{:S(2)}, u32[]{:S(2)}) %collective-permute-start.3) | collective-permute-done | bytes 65568 | tf_op jit(solution)/shard_map/ppermute | solution.py:12
  252.3 2.6 collective-permute-start.4
  255.6 3.0 %copy.64 = f32[4,8,256,128]{3,2,1,0:T(8,128)S(1)} copy(f32[4,8,256,128]{3,1,2,0:T(8,128)} %get-tuple-element.6) | data formatting | bytes 8388608
  267.4 2.2 fusion.4
  273.1 2.5 fusion.3
  277.9 3.4 %fusion.2 = f32[8,256,128]{1,2,0:T(8,128)} fusion(f32[8,128,256]{2,1,0:T(8,128)S(1)} %fusion, f32[15,256,128]{2,1,0:T(8,128)} %param.20, f32[8,128,128]{1,2,0:T(8,128)} %copy.50, f32[8,128,128]{2,1,0:T(8,128)S(1)} %fusion.14), kind=kOutput, calls=%fused_computation.9 | convolution fusion | flops 403046400 | bytes 4194304 | tf_op jit(solution)/shard_map/nik,nkc->nic/dot_general | solution.py:35
  281.3 2.5 copy.51
  283.8 2.7 copy.52
  286.5 5.3 %bitcast_subtract_fusion = f32[16,512,128]{2,1,0:T(8,128)} fusion(bf16[16,512,128]{2,1,0:T(8,128)(2,1)} %copy-done.5, bf16[16,512,128]{2,1,0:T(8,128)(2,1)} %param.16, f32[16,128,128]{1,2,0:T(8,128)} %copy.52, f32[16,128,128]{2,1,0:T(8,128)S(1)} %fusion.145), kind=kOutput, calls=%fused_computation.3 | convolution fusion | flops 271056896 | bytes 10485760 | tf_op jit(solution)/shard_map/nik,nkc->nic/dot_general | solution.py:124
  (125 shorter events, 60.0 us)
Async XLA Ops:
  6.5 88.3 %copy-start = (bf16[8192,128]{1,0:T(8,128)(2,1)S(1)}, bf16[8192,128]{1,0:T(8,128)(2,1)}, u32[]{:S(2)}) copy-start(bf16[8192,128]{1,0:T(8,128)(2,1)} %param.13) | copy-start | bytes 6291460
  6.5 88.3 %all-gather.4.cloned.1.call-start = ((), (), s32[]{:S(2)}) async-start(), calls=%async_computation | async-start | bytes 10485760 | tf_op jit(solution)/shard_map/all_gather | solution.py:90
  7.3 167.9 %all-gather.6.cloned.1.call-start = ((), (), s32[]{:S(2)}) async-start(), calls=%async_computation.1 | async-start | bytes 19464192 | tf_op jit(solution)/shard_map/all_gather | solution.py:20
  94.8 5.9 %copy-start.9 = (bf16[16,512,128]{2,1,0:T(8,128)(2,1)S(1)}, bf16[16,512,128]{2,1,0:T(8,128)(2,1)}, u32[]{:S(2)}) copy-start(bf16[16,512,128]{2,1,0:T(8,128)(2,1)} %param.15) | copy-start | bytes 6291460
  115.9 1.3 collective-permute-start
  203.6 13.2 %copy-start.7 = (f32[4,8,128,128]{3,2,1,0:T(8,128)}, f32[4,8,128,128]{3,2,1,0:T(8,128)S(1)}, u32[]{:S(2)}) copy-start(f32[4,8,128,128]{3,2,1,0:T(8,128)S(1)} %copy.66) | copy-start | bytes 6291460
  209.2 5.9 %copy-start.34 = (f32[1,128,128]{1,2,0:T(8,128)S(1)}, f32[1,128,128]{1,2,0:T(8,128)}, u32[]{:S(2)}) copy-start(f32[1,128,128]{1,2,0:T(8,128)} %get-tuple-element.15) | copy-start | bytes 196612
  209.2 5.9 %copy-start.35 = (f32[1,128,128]{1,2,0:T(8,128)S(1)}, f32[1,128,128]{1,2,0:T(8,128)}, u32[]{:S(2)}) copy-start(f32[1,128,128]{1,2,0:T(8,128)} %get-tuple-element.16) | copy-start | bytes 196612
  217.6 4.6 %collective-permute-start.1 = (f32[1,128,128]{2,1,0:T(8,128)}, f32[1,128,128]{2,1,0:T(8,128)}, u32[]{:S(2)}, u32[]{:S(2)}) collective-permute-start(f32[1,128,128]{2,1,0:T(8,128)} %convolution_bitcast_fusion.4), channel_id=1, source_target_pairs={{0,8},{4,12},{8,0},{12,4},{16,24},{20,28},{24,16},{28,20},{32,40},... | collective-permute-start | bytes 196616 | tf_op jit(solution)/shard_map/ppermute | solution.py:12
  228.7 6.1 %collective-permute-start.2 = (f32[1,128,128]{2,1,0:T(8,128)}, f32[1,128,128]{2,1,0:T(8,128)}, u32[]{:S(2)}, u32[]{:S(2)}) collective-permute-start(f32[1,128,128]{2,1,0:T(8,128)} %convolution_bitcast_fusion.3), channel_id=1, source_target_pairs={{0,16},{4,20},{8,24},{12,28},{16,0},{20,4},{24,8},{28,12},{32,48},... | collective-permute-start | bytes 196616 | tf_op jit(solution)/shard_map/ppermute | solution.py:12
  241.2 4.6 %collective-permute-start.3 = (f32[1,128,128]{2,1,0:T(8,128)}, f32[1,128,128]{2,1,0:T(8,128)}, u32[]{:S(2)}, u32[]{:S(2)}) collective-permute-start(f32[1,128,128]{2,1,0:T(8,128)} %convolution_bitcast_fusion.2), channel_id=1, source_target_pairs={{0,32},{4,36},{8,40},{12,44},{16,48},{20,52},{24,56},{28,60},{32,0... | collective-permute-start | bytes 196616 | tf_op jit(solution)/shard_map/ppermute | solution.py:12
  252.3 6.4 %collective-permute-start.4 = (f32[1,128,128]{2,1,0:T(8,128)}, f32[1,128,128]{2,1,0:T(8,128)}, u32[]{:S(2)}, u32[]{:S(2)}) collective-permute-start(f32[1,128,128]{2,1,0:T(8,128)} %convolution_bitcast_fusion.1), channel_id=1, source_target_pairs={{0,64},{4,68},{8,72},{12,76},{16,80},{20,84},{24,88},{28,92},{32,9... | collective-permute-start | bytes 196616 | tf_op jit(solution)/shard_map/ppermute | solution.py:12
  255.6 5.4 %copy-start.16 = (f32[256,128]{1,0:T(8,128)S(1)}, f32[256,128]{1,0:T(8,128)}, u32[]{:S(2)}) copy-start(f32[256,128]{1,0:T(8,128)} %copy-done.15) | copy-start | bytes 393220
  255.6 5.4 %copy-start.32 = (f32[128,128]{1,0:T(8,128)S(1)}, f32[128,128]{1,0:T(8,128)}, u32[]{:S(2)}) copy-start(f32[128,128]{1,0:T(8,128)} %copy-done.31) | copy-start | bytes 196612
  255.6 5.7 %copy-start.14 = (f32[256,128]{1,0:T(8,128)S(1)}, f32[256,128]{1,0:T(8,128)}, u32[]{:S(2)}) copy-start(f32[256,128]{1,0:T(8,128)} %copy-done.13) | copy-start | bytes 393220
  255.6 5.7 %copy-start.30 = (f32[128,128]{1,0:T(8,128)S(1)}, f32[128,128]{1,0:T(8,128)}, u32[]{:S(2)}) copy-start(f32[128,128]{1,0:T(8,128)} %copy-done.29) | copy-start | bytes 196612
  255.6 6.0 %copy-start.12 = (f32[256,128]{1,0:T(8,128)S(1)}, f32[256,128]{1,0:T(8,128)}, u32[]{:S(2)}) copy-start(f32[256,128]{1,0:T(8,128)} %copy-done.11) | copy-start | bytes 393220
  255.6 6.0 %copy-start.28 = (f32[128,128]{1,0:T(8,128)S(1)}, f32[128,128]{1,0:T(8,128)}, u32[]{:S(2)}) copy-start(f32[128,128]{1,0:T(8,128)} %copy-done.27) | copy-start | bytes 196612
  255.6 6.2 %copy-start.26 = (f32[128,128]{1,0:T(8,128)S(1)}, f32[128,128]{1,0:T(8,128)}, u32[]{:S(2)}) copy-start(f32[128,128]{1,0:T(8,128)} %copy-done.25) | copy-start | bytes 196612
  255.6 6.2 %copy-start.33 = (f32[256,128]{0,1:T(8,128)S(1)}, f32[256,128]{0,1:T(8,128)}, u32[]{:S(2)}) copy-start(f32[256,128]{0,1:T(8,128)} %copy.43) | copy-start | bytes 393220
  255.6 6.6 %copy-start.18 = (f32[128,256]{1,0:T(8,128)S(1)}, f32[128,256]{1,0:T(8,128)}, u32[]{:S(2)}) copy-start(f32[128,256]{1,0:T(8,128)} %copy-done.17) | copy-start | bytes 393220
  255.6 6.6 %copy-start.24 = (f32[128,128]{1,0:T(8,128)S(1)}, f32[128,128]{1,0:T(8,128)}, u32[]{:S(2)}) copy-start(f32[128,128]{1,0:T(8,128)} %copy-done.23) | copy-start | bytes 196612
  258.7 8.7 %copy-start.20 = (f32[2,128,128]{2,1,0:T(8,128)S(1)}, f32[2,128,128]{2,1,0:T(8,128)}, u32[]{:S(2)}) copy-start(f32[2,128,128]{2,1,0:T(8,128)} %copy-done.19) | copy-start | bytes 393220
  283.8 8.0 %copy-start.1 = (bf16[8192,128]{1,0:T(8,128)(2,1)S(1)}, bf16[8192,128]{1,0:T(8,128)(2,1)}, u32[]{:S(2)}) copy-start(bf16[8192,128]{1,0:T(8,128)(2,1)} %param.13) | copy-start | bytes 6291460
  (19 other events, 38.0 us)
Sparse Core Ops, SparseCore 0:
  9.0 85.7 all-gather.3
  97.1 78.0 all-gather.5
where the time goes:
time: 300 us; the launch traced here: 299 us
  waiting for transfers between devices  150 us (50%)
  local copies, waits for them, and re-layouts  65.3 us (22%)
  matrix products  51.7 us (17%)
  between operations  14 us (5%)
  other arithmetic  9.34 us (3%)
  starting transfers between devices  8.09 us (3%)
    all_gather x1, waiting for transfers between devices, per_device(): lax.all_gather(leaf_inv, 'rhs', axis=1, tiled=True)  81.1 us
    all_gather x1, waiting for transfers between devices, sent_together(): result = lax.all_gather(both, axis, axis=dim, tiled=True)  57.3 us
    unnamed x80, local copies, waits for them, and re-layouts  46.4 us
    dot_general x8, matrix products, node_down(): jnp.einsum('nik,nkc->nic', back_mat, reduced - parent_part, precision=exa...  11.1 us
    ppermute x5, waiting for transfers between devices, swapped(): lax.ppermute(array, axis, [(i, i ^ 1 << bit) for i in range(lax.axis_size...  11 us
    dot_general x9, matrix products, node_up(): solved = jnp.einsum('nij,njc->nic', inverse, stacked, precision=exact_mode)  10.5 us
    dot_general x8, matrix products, node_up(): upward = jnp.einsum('nkl,nlc->nkc', coarse, reduced, precision=exact_mode)  8.37 us
    ppermute x5, starting transfers between devices, swapped(): lax.ppermute(array, axis, [(i, i ^ 1 << bit) for i in range(lax.axis_size...  8.05 us
  transfers between devices with their start and end apart: 7, of which 6 were waited for; matrix products, arithmetic and copies ran while one was open for 10% of the time, Pallas kernels for 0%

commit v1 on v0

v1 whole, which is shorter than its diff:
```python
import jax
import jax.numpy as jnp
from jax import lax
from jax.experimental import pallas as pl
from jax.experimental.pallas import tpu as pltpu
from jax.sharding import PartitionSpec as P


wide = jnp.float32
narrow = jnp.bfloat16

GROUPS = ((0, 4), (4, 8), (12, 4))
EARLY = (0, 1, 8, 2, 3, 4, 5, 9, 10, 12)
LATE = (6, 7, 11, 13, 14)
FRONT = (((0,), (0,)), ((), ()))


def narrow_dot(a, b):
    return jnp.dot(a.astype(narrow), b.astype(narrow), preferred_element_type=wide)


def parts_of(a):
    high = a.astype(narrow)
    return high, (a - high.astype(wide)).astype(narrow)


def split_dot(a, b, dims=(((1,), (0,)), ((), ()))):
    a_high, a_low = parts_of(a)
    b_high, b_low = parts_of(b)

    def one(p, q):
        return lax.dot_general(p, q, dims, preferred_element_type=wide)

    return one(a_high, b_low) + one(a_low, b_high) + one(a_high, b_high)


def close_dot(a, b):
    return jnp.dot(a, b, precision=lax.Precision.HIGH, preferred_element_type=wide)


def kernel_call(body, out_shape, flops, operands, scalars=0, room=16, **more):
    if scalars:
        more["in_specs"] = [pl.BlockSpec(memory_space=pltpu.SMEM)] * scalars + [
            pl.BlockSpec(a.shape, lambda a=a: (0,) * a.ndim) for a in operands[scalars:]
        ]
    size = sum(a.size * a.dtype.itemsize for a in operands)
    return pl.pallas_call(
        body,
        out_shape=out_shape,
        cost_estimate=pl.CostEstimate(flops=flops, bytes_accessed=size, transcendentals=0),
        compiler_params=pltpu.CompilerParams(vmem_limit_bytes=room * 1024 * 1024),
        **more,
    )(*operands)


def turned(row_ref, part, height):
    return pl.multiple_of(lax.rem(row_ref[0] + part, 4) * height, height)


def near_body(row_ref, own, left, right, rhs, basis, vals, proj):
    count, height, width = own.shape
    for k in range(count):
        rows = jnp.concatenate([own[k], left[k], right[k]], axis=0)
        got = narrow_dot(rows, rhs[k * width : (k + 1) * width, :]).astype(narrow)
        vals[k] = got
        matching = jnp.concatenate(
            [basis[k, pl.ds(turned(row_ref, part, height), height), :] for part in (0, 3, 1)],
            axis=0,
        )
        proj[k] = lax.dot_general(matching, got, FRONT, preferred_element_type=wide)


def near_call(start, row, own, left, right, rhs, basis):
    count, height, width = left.shape
    rank, columns = basis.shape[2], rhs.shape[1]
    some = 2
    base = start // some

    def at(shape, shift):
        return pl.BlockSpec(shape, lambda i, row: (shift + i,) + (0,) * (len(shape) - 1))

    return pl.pallas_call(
        near_body,
        grid_spec=pltpu.PrefetchScalarGridSpec(
            num_scalar_prefetch=1,
            grid=(count // some,),
            in_specs=[
                at((some, height, width), base),
                at((some, height, width), 0),
                at((some, height, width), 0),
                at((some * width, columns), base),
                at((some, width, rank), base),
            ],
            out_specs=[
                at((some, 3 * height, columns), 0),
                at((some, rank, columns), 0),
            ],
        ),
        out_shape=[
            jax.ShapeDtypeStruct((count, 3 * height, columns), narrow),
            jax.ShapeDtypeStruct((count, rank, columns), wide),
        ],
        cost_estimate=pl.CostEstimate(
            flops=count * 2 * 3 * height * width * columns * 4,
            bytes_accessed=count * width * width * 2,
            transcendentals=0,
        ),
        compiler_params=pltpu.CompilerParams(vmem_limit_bytes=16 * 1024 * 1024),
    )(row, own, left, right, rhs, basis)


def far_leaves(row_ref, far_a, far_b, rhs, basis, coarse, part, vals, proj, lead):
    count = part.shape[0]
    height, width = far_a.shape[1], far_a.shape[2]
    half = count // 2
    at = turned(row_ref, 2, height)
    for k in range(count):
        rows = far_a[k] if k < half else far_b[k - half]
        got = narrow_dot(rows, rhs[k * width : (k + 1) * width, :]).astype(narrow)
        vals[k] = got
        total = part[k] + lax.dot_general(
            basis[k, pl.ds(at, height), :], got, FRONT, preferred_element_type=wide
        )
        proj[k] = total
        lead[k] = split_dot(coarse[k], total)


def far_body(*refs):
    far_leaves(*refs)


def last_body(
    row_ref, far_a, far_b, rhs, basis, coarse, part, ups, early, vals, proj, lead, late, up
):
    far_leaves(row_ref, far_a, far_b, rhs, basis, coarse, part, vals, proj, lead)
    slot = {12 + k: lead for k in range(4)}
    where = {12 + k: k for k in range(4)}
    for k, node in enumerate(EARLY):
        slot[16 + node], where[16 + node] = early, k
    for k, node in enumerate(LATE):
        pair = [slot[c][where[c]] for c in (2 * node, 2 * node + 1)]
        value = split_dot(ups[k], jnp.concatenate(pair, axis=0))
        if k == len(LATE) - 1:
            up[...] = value
        else:
            late[k] = value
        slot[16 + node], where[16 + node] = late, k


def far_shapes(count, height, rank, columns):
    return [
        jax.ShapeDtypeStruct((count, height, columns), narrow),
        jax.ShapeDtypeStruct((count, rank, columns), wide),
        jax.ShapeDtypeStruct((count, rank, columns), wide),
    ]


def merge_body(lead0, lead1, inv, basis, back, coarse, early, base):
    value = {}
    for k in range(4):
        value[k] = lead0[k]
    for k in range(8):
        value[4 + k] = lead1[k]
    for k, node in enumerate(EARLY):
        stacked = jnp.concatenate([value[2 * node], value[2 * node + 1]], axis=0)
        solved = split_dot(inv[node], stacked)
        reduced = split_dot(basis[node], solved, FRONT)
        value[16 + node] = split_dot(coarse[node], reduced)
        early[k] = value[16 + node]
        base[k] = solved - split_dot(back[node], reduced)


def prepare_body(inv, basis, back, coarse, ups, paths):
    for k, node in enumerate(LATE):
        ups[k] = split_dot(coarse[node], split_dot(basis[node], inv[node], FRONT))
    value = {30: None}
    rank = paths.shape[1]
    for node in reversed(range(15)):
        above = value[16 + node]
        below = back[node] if above is None else split_dot(back[node], above)
        for k in range(2):
            value[2 * node + k] = below[k * rank : (k + 1) * rank]
            if node < 8:
                paths[2 * node + k] = value[2 * node + k]


def known_body(lead2, late, early, base, inv, basis, back, proj0, proj1, proj2, rest):
    rank = proj0.shape[1]
    value = {12 + k: (lead2, k) for k in range(4)}
    for k, node in enumerate(EARLY):
        value[16 + node] = (early, k)
    for k, node in enumerate(LATE[:-1]):
        value[16 + node] = (late, k)
    known = {node: (lambda k=k: base[k]) for k, node in enumerate(EARLY)}
    for node in LATE:
        pair = [value[c][0][value[c][1]] for c in (2 * node, 2 * node + 1)]
        solved = split_dot(inv[node], jnp.concatenate(pair, axis=0))
        reduced = split_dot(basis[node], solved, FRONT)
        result = solved - split_dot(back[node], reduced)
        known[node] = lambda result=result: result
    projs = [(proj0, k) for k in range(4)] + [(proj1, k) for k in range(8)]
    projs += [(proj2, k) for k in range(4)]
    part = {30: None}
    for node in reversed(range(15)):
        halves = known[node]()
        if part[16 + node] is not None:
            halves = halves + split_dot(back[node], part[16 + node])
        for k in range(2):
            below = halves[k * rank : (k + 1) * rank]
            part[2 * node + k] = below
            if node < 8:
                ref, at = projs[2 * node + k]
                rest[2 * node + k] = ref[at] - below


def top_body(left_ref, packs, up_own, up_sib, down_own, down_sib):
    depth = down_own.shape[0]
    rank = packs.shape[0]
    path = None
    for level in range(depth):
        root = level == depth - 1
        first = 0 if root else 2 * rank + (depth - 2 - level) * 5 * rank
        is_left = left_ref[level] == 1

        def both(matrix):
            one, two = matrix[:, :rank], matrix[:, rank:]
            return jnp.where(is_left, one, two), jnp.where(is_left, two, one)

        if root:
            down = packs[:, first : first + 2 * rank]
        else:
            up_own[level], up_sib[level] = both(packs[:, first : first + 2 * rank])
            down = packs[:, first + 2 * rank : first + 4 * rank]
        if path is not None:
            down = split_dot(path, down)
        down_own[level], down_sib[level] = both(down)
        if not root:
            step = packs[:, first + 4 * rank : first + 5 * rank]
            path = step if path is None else split_dot(path, step)


def out_body(row_ref, top_ref, paths, rest, back, near0, near1, far, out):
    some, width = back.shape[0], back.shape[1]
    height = far.shape[1]
    top = top_ref[...]
    step = pl.program_id(0)
    at = [turned(row_ref, part, height) for part in (0, 3, 1, 2)]
    for k in range(some):
        difference = (rest[k] - split_dot(paths[k], top)).astype(narrow)
        matching = jnp.concatenate([back[k, pl.ds(a, height), :] for a in at], axis=0)
        change = narrow_dot(matching, difference)
        near = jnp.where(step == 0, near0[k], near1[k])
        for j, a in enumerate(at):
            block = far[k] if j == 3 else near[j * height : (j + 1) * height]
            out[pl.ds(pl.multiple_of(k * width + a, height), height), :] = (
                block.astype(wide) - change[j * height : (j + 1) * height]
            )


def out_call(row, top, paths, rest, back, near0, near1, far):
    leaves, width, rank = back.shape
    height, columns = far.shape[1], far.shape[2]
    some = near0.shape[0]

    def at(shape, index):
        return pl.BlockSpec(shape, lambda i, row: (index(i),) + (0,) * (len(shape) - 1))

    return pl.pallas_call(
        out_body,
        grid_spec=pltpu.PrefetchScalarGridSpec(
            num_scalar_prefetch=1,
            grid=(leaves // some,),
            in_specs=[
                pl.BlockSpec(top.shape, lambda i, row: (0, 0)),
                at((some, rank, rank), lambda i: i),
                at((some, rank, columns), lambda i: i),
                at((some, width, rank), lambda i: i),
                at((some, 3 * height, columns), lambda i: 0),
                at((some, 3 * height, columns), lambda i: jnp.maximum(i - 1, 0)),
                at((some, height, columns), lambda i: i),
            ],
            out_specs=at((some * width, columns), lambda i: i),
        ),
        out_shape=jax.ShapeDtypeStruct((leaves * width, columns), wide),
        compiler_params=pltpu.CompilerParams(vmem_limit_bytes=16 * 1024 * 1024),
        name="leaf_result",
    )(row, top, paths, rest, back, near0, near1, far)


def exact(eq, a, b):
    return jnp.einsum(eq, a, b, precision=lax.Precision.HIGHEST)


def top_factors(inv, basis, back, coarse, position, depth):
    total = lax.axis_size("leaf")
    rank = basis.shape[1]
    reduce_mat = exact("ik,ij->kj", basis, inv)
    up_mat = exact("kl,lj->kj", coarse, reduce_mat)
    down_mat = inv - exact("ik,kj->ij", back, reduce_mat)
    halves = [
        jnp.concatenate([up_mat, down_mat[s : s + rank], back[s : s + rank]], axis=1)
        for s in (0, rank)
    ]
    upper = None
    for bit in reversed(range(depth)):
        stride = 1 << bit
        high = (position >> bit) % 2 == 1
        if upper is None:
            got = lax.ppermute(inv[:rank], "leaf", [(stride, 0)])
            upper = jnp.where(high, inv[rank:], got)
            continue
        size, mine = upper.shape[1], halves[0].shape[1]
        most = max(size, mine)
        message = jnp.where(
            high,
            jnp.pad(halves[0], ((0, 0), (0, most - mine))),
            jnp.pad(upper, ((0, 0), (0, most - size))),
        )
        pairs = [(i, i ^ stride) for i in range(0, total, stride)]
        got = lax.ppermute(message, "leaf", pairs)
        upper = jnp.concatenate(
            [
                jnp.where(high, got[:, :size], upper),
                jnp.where(high, halves[1], got[:, :mine]),
            ],
            axis=1,
        )
    return upper


def solve(
    rhs_cols,
    leaf_inv,
    leaf_basis,
    leaf_back,
    leaf_coarse,
    mid_inv,
    mid_basis,
    mid_back,
    mid_coarse,
    top_inv,
    top_basis,
    top_back,
    top_coarse,
):
    leaf_count, height, width = leaf_inv.shape
    rank, columns = leaf_basis.shape[2], rhs_cols.shape[1]
    position = lax.axis_index("leaf")
    leaf_total = lax.axis_size("leaf")
    depth = leaf_total.bit_length() - 1
    ring = lax.axis_size("rhs")
    ahead = [(i, (i + 1) % ring) for i in range(ring)]
    behind = [(i, (i - 1) % ring) for i in range(ring)]
    cut = GROUPS[0][1]
    row = lax.axis_index("rhs").astype(jnp.int32).reshape(1)

    left, right = [], []
    for own in (leaf_inv[:cut], leaf_inv[cut:]):
        left.append(lax.ppermute(own, "rhs", ahead))
        right.append(lax.ppermute(own, "rhs", behind))
    far = []
    for k, (start, count) in enumerate(GROUPS):
        part = 0 if k == 0 else 1
        first = 0 if k == 0 else start - cut
        half = count // 2
        far.append(
            (
                lax.ppermute(left[part][first : first + half], "rhs", ahead),
                lax.ppermute(right[part][first + half : first + count], "rhs", behind),
            )
        )

    packs = top_factors(
        top_inv[0], top_basis[0], top_back[0], top_coarse[0], position, depth
    )
    sides = jnp.stack([1 - (position >> k) % 2 for k in range(depth)]).astype(jnp.int32)
    square = (rank, rank)
    up_own, up_sib, down_own, down_sib = kernel_call(
        top_body,
        [jax.ShapeDtypeStruct((n, *square), wide) for n in (depth - 1, depth - 1, depth, depth)],
        10**8,
        (sides, packs),
        scalars=1,
    )
    ups, paths = kernel_call(
        prepare_body,
        [
            jax.ShapeDtypeStruct((len(LATE), rank, 2 * rank), wide),
            jax.ShapeDtypeStruct((leaf_count, *square), wide),
        ],
        8 * 10**8,
        (mid_inv, mid_basis, mid_back, mid_coarse),
        room=24,
    )

    near0, part0 = near_call(0, row, leaf_inv, left[0], right[0], rhs_cols, leaf_basis)
    near1, part1 = near_call(cut, row, leaf_inv, left[1], right[1], rhs_cols, leaf_basis)

    def of_group(k):
        start, count = GROUPS[k]
        part = part0 if k == 0 else part1[start - cut : start - cut + count]
        return (
            row,
            *far[k],
            rhs_cols[start * width : (start + count) * width],
            leaf_basis[start : start + count],
            leaf_coarse[start : start + count],
            part,
        )

    results = [
        kernel_call(
            far_body,
            far_shapes(GROUPS[k][1], height, rank, columns),
            GROUPS[k][1] * 4 * 10**7,
            of_group(k),
            scalars=1,
        )
        for k in range(2)
    ]
    early, base = kernel_call(
        merge_body,
        [
            jax.ShapeDtypeStruct((len(EARLY), rank, columns), wide),
            jax.ShapeDtypeStruct((len(EARLY), 2 * rank, columns), wide),
        ],
        10**9,
        (results[0][2], results[1][2], mid_inv, mid_basis, mid_back, mid_coarse),
        room=24,
    )
    final = lax.optimization_barrier(
        (of_group(2), ups, early, up_own, up_sib, down_own, down_sib, paths)
    )
    group, ups, early, up_own, up_sib, down_own, down_sib, paths = final
    far2, proj2, lead2, late, current = kernel_call(
        last_body,
        far_shapes(GROUPS[2][1], height, rank, columns)
        + [
            jax.ShapeDtypeStruct((len(LATE) - 1, rank, columns), wide),
            jax.ShapeDtypeStruct((rank, columns), wide),
        ],
        3 * 10**8,
        (*group, ups, early),
        scalars=1,
    )
    rest = kernel_call(
        known_body,
        jax.ShapeDtypeStruct((leaf_count, rank, columns), wide),
        8 * 10**8,
        (
            lead2,
            late,
            early,
            base,
            mid_inv,
            mid_basis,
            mid_back,
            results[0][1],
            results[1][1],
            proj2,
        ),
        room=24,
    )
    far_vals = jnp.concatenate([results[0][0], results[1][0], far2], axis=0)

    top = None
    for level in range(depth):
        mask = 1 << level
        if level in (2, 4):
            mask |= mask >> 1
        pairs = [(i, i ^ mask) for i in range(leaf_total)]
        partner = lax.ppermute(current, "leaf", pairs)
        known = close_dot(down_own[level], current)
        top = known if top is None else top + known
        top = top + close_dot(down_sib[level], partner)
        if level < depth - 1:
            before = close_dot(up_own[level], current)
            current = before + close_dot(up_sib[level], partner)
    return out_call(row, top, paths, rest, leaf_back, near0, near1, far_vals)


def solution(mesh):
    return jax.shard_map(
        solve,
        mesh=mesh,
        in_specs=(P("leaf", "rhs"), P("leaf", "rhs", None))
        + (P("leaf", None, None),) * 11,
        out_specs=P("leaf", "rhs"),
        check_vma=False,
    )
```

time: 300 us -> 134 us (0.45)
  waiting for transfers between devices: 150 us -> 36.7 us
  matrix products: 51.7 us -> 7 us
  local copies, waits for them, and re-layouts: 65.3 us -> 22.7 us
  Pallas kernels: 0 us -> 30.4 us
  starting transfers between devices: 8.09 us -> 32.3 us
  between operations: 14 us -> 0.83 us
  other arithmetic: 9.34 us -> 2.72 us
    all_gather x2 -> x0, waiting for transfers between devices: 138 us -> none  [the longest x1 81.1 us: per_device(): lax.all_gather(leaf_inv, 'rhs', axis=1, tiled=True)]
    dot_general x37 -> x21, matrix products: 51.7 us -> 7 us  [the longest x3 3.84 us: exact(): return jnp.einsum(eq, a, b, precision=lax.Precision.HIGHEST)]
    unnamed x80 -> x52, local copies, waits for them, and re-layouts: 46.4 us -> 9.7 us
    pallas_call x0 -> x10, Pallas kernels: none -> 30.4 us  [the longest x7 17.3 us: kernel_call(): pl.pallas_call(body, out_shape=out_shape, cost_estimate=pl.CostEstimate(f...]
    ppermute x5 -> x20, waiting for transfers between devices: 11 us -> 36.7 us  [the longest x4 17 us: top_factors(): got = lax.ppermute(message, 'leaf', pairs)]
    ppermute x5 -> x20, starting transfers between devices: 8.05 us -> 32.3 us  [the longest x3 9.6 us: solve(): lax.ppermute(right[part][first + half:first + count], 'rhs', behind)]
    slice x0 -> x19, local copies, waits for them, and re-layouts: none -> 12.9 us  [the longest x3 3.16 us: solve(): left[part][first:first + half]]
    sub x4 -> x0, local copies, waits for them, and re-layouts: 7.22 us -> none  [node_down(): solved - jnp.einsum('nik,nkc->nic', back_mat, reduced - parent_part, prec...]
  transfers between devices with their start and end apart: 7 -> 20, of which waited for: 6 -> 8; matrix products, arithmetic and copies ran while one was open for 10% -> 14% of each run, Pallas kernels for 0% -> 19%
where the time goes in v1:
time: 134 us; the launch traced here: 133 us
  waiting for transfers between devices  36.7 us (27%)
  starting transfers between devices  32.3 us (24%)
  Pallas kernels  30.4 us (23%)
  local copies, waits for them, and re-layouts  22.7 us (17%)
  matrix products  7 us (5%)
  other arithmetic  2.72 us (2%)
    pallas_call x7, Pallas kernels, kernel_call(): pl.pallas_call(body, out_shape=out_shape, cost_estimate=pl.CostEstimate(f...  17.3 us
    ppermute x4, waiting for transfers between devices, top_factors(): got = lax.ppermute(message, 'leaf', pairs)  17 us
    ppermute x5, waiting for transfers between devices, solve(): partner = lax.ppermute(current, 'leaf', pairs)  12.8 us
    unnamed x52, local copies, waits for them, and re-layouts  9.7 us
    ppermute x3, starting transfers between devices, solve(): lax.ppermute(right[part][first + half:first + count], 'rhs', behind)  9.6 us
    pallas_call x2, Pallas kernels, near_call(): pl.pallas_call(near_body, grid_spec=pltpu.PrefetchScalarGridSpec(num_scal...  9.38 us
    ppermute x5, starting transfers between devices, solve(): partner = lax.ppermute(current, 'leaf', pairs)  6.38 us
    ppermute x4, starting transfers between devices, top_factors(): got = lax.ppermute(message, 'leaf', pairs)  5.97 us
  transfers between devices with their start and end apart: 20, of which 8 were waited for; matrix products, arithmetic and copies ran while one was open for 14% of the time, Pallas kernels for 19%

profile of v1, /device:TPU:0, one launch (start us, length us, event | category | flops | bytes accessed | tf_op | source)
XLA Modules:
  0.0 132.7 jit_solution(10519456707948085398)
XLA Ops:
  6.3 3.1 %collective-permute-done.10 = f32[128,256]{1,0:T(8,128)S(1)} collective-permute-done((f32[128,256]{1,0:T(8,128)S(1)}, f32[128,256]{1,0:T(8,128)S(1)}, u32[]{:S(2)}, u32[]{:S(2)}) %collective-permute-start.10) | collective-permute-done | bytes 131104 | tf_op jit(solution)/shard_map/ppermute | solution.py:309
  9.4 1.9 %collective-permute-start.11 = (f32[128,640]{1,0:T(8,128)S(1)}, f32[128,640]{1,0:T(8,128)S(1)}, u32[]{:S(2)}, u32[]{:S(2)}) collective-permute-start(f32[128,640]{1,0:T(8,128)S(1)} %get-tuple-element.85), channel_id=1, source_target_pairs={{0,32},{32,0},{64,96},{96,64},{1,33},{33,1},{65,97},{97,65},{2,34}... | collective-permute-start | bytes 983048 | tf_op jit(solution)/shard_map/ppermute | solution.py:320
  11.4 7.0 %collective-permute-done.11 = f32[128,640]{1,0:T(8,128)S(1)} collective-permute-done((f32[128,640]{1,0:T(8,128)S(1)}, f32[128,640]{1,0:T(8,128)S(1)}, u32[]{:S(2)}, u32[]{:S(2)}) %collective-permute-start.11) | collective-permute-done | bytes 327712 | tf_op jit(solution)/shard_map/ppermute | solution.py:320
  18.5 1.9 %collective-permute-start.12 = (f32[128,896]{1,0:T(8,128)S(1)}, f32[128,896]{1,0:T(8,128)S(1)}, u32[]{:S(2)}, u32[]{:S(2)}) collective-permute-start(f32[128,896]{1,0:T(8,128)S(1)} %pad_select_fusion.2), channel_id=1, source_target_pairs={{0,16},{16,0},{32,48},{48,32},{64,80},{80,64},{96,112},{112,96},{1... | collective-permute-start | bytes 1376264 | tf_op jit(solution)/shard_map/ppermute | solution.py:320
  20.5 9.9 %collective-permute-done.12 = f32[128,896]{1,0:T(8,128)S(1)} collective-permute-done((f32[128,896]{1,0:T(8,128)S(1)}, f32[128,896]{1,0:T(8,128)S(1)}, u32[]{:S(2)}, u32[]{:S(2)}) %collective-permute-start.12) | collective-permute-done | bytes 458784 | tf_op jit(solution)/shard_map/ppermute | solution.py:320
  31.6 2.0 %collective-permute-start.13 = (f32[128,1536]{1,0:T(8,128)}, f32[128,1536]{1,0:T(8,128)}, u32[]{:S(2)}, u32[]{:S(2)}) collective-permute-start(f32[128,1536]{1,0:T(8,128)} %pad_select_fusion.1), channel_id=1, source_target_pairs={{0,8},{8,0},{16,24},{24,16},{32,40},{40,32},{48,56},{56,48},{64,72... | collective-permute-start | bytes 2359304 | tf_op jit(solution)/shard_map/ppermute | solution.py:320
  35.0 2.0 %collective-permute-start = (bf16[12,128,512]{2,1,0:T(8,128)(2,1)}, bf16[12,128,512]{2,1,0:T(8,128)(2,1)}, u32[]{:S(2)}, u32[]{:S(2)}) collective-permute-start(bf16[12,128,512]{2,1,0:T(8,128)(2,1)} %slice.153), channel_id=1, source_target_pairs={{0,1},{1,2},{2,3},{3,0},{4,5},{5,6},{6,7},{7,4},{8,9},{9,10},{10,1... | collective-permute-start | bytes 4718600 | tf_op jit(solution)/shard_map/ppermute | solution.py:359
  37.0 2.1 %collective-permute-start.2 = (bf16[12,128,512]{2,1,0:T(8,128)(2,1)}, bf16[12,128,512]{2,1,0:T(8,128)(2,1)}, u32[]{:S(2)}, u32[]{:S(2)}) collective-permute-start(bf16[12,128,512]{2,1,0:T(8,128)(2,1)} %slice.153), channel_id=1, source_target_pairs={{0,3},{1,0},{2,1},{3,2},{4,7},{5,4},{6,5},{7,6},{8,11},{9,8},{10,9... | collective-permute-start | bytes 4718600 | tf_op jit(solution)/shard_map/ppermute | solution.py:360
  40.0 3.2 %collective-permute-start.6 = (bf16[4,128,512]{2,1,0:T(8,128)(2,1)}, bf16[4,128,512]{2,1,0:T(8,128)(2,1)}, u32[]{:S(2)}, u32[]{:S(2)}) collective-permute-start(bf16[4,128,512]{2,1,0:T(8,128)(2,1)} %slice.160), channel_id=1, source_target_pairs={{0,3},{1,0},{2,1},{3,2},{4,7},{5,4},{6,5},{7,6},{8,11},{9,8},{10,9... | collective-permute-start | bytes 1572872 | tf_op jit(solution)/shard_map/ppermute | solution.py:360
  47.7 2.1 %copy-done.1 = f32[15,256,256]{2,1,0:T(8,128)S(1)} copy-done((f32[15,256,256]{2,1,0:T(8,128)S(1)}, f32[15,256,256]{2,1,0:T(8,128)}, u32[]{:S(2)}) %copy-start.1) | copy-done | bytes 3932184
  59.7 3.8 %collective-permute-done.4.left = bf16[4,128,512]{2,1,0:T(8,128)(2,1)} collective-permute-done((bf16[4,128,512]{2,1,0:T(8,128)(2,1)}, bf16[4,128,512]{2,1,0:T(8,128)(2,1)}, u32[]{:S(2)}, u32[]{:S(2)}) %collective-permute-start.4) | collective-permute-done | bytes 524320 | tf_op jit(solution)/shard_map/ppermute | solution.py:359
  67.0 2.8 %collective-permute-start.7 = (bf16[2,128,512]{2,1,0:T(8,128)(2,1)S(1)}, bf16[2,128,512]{2,1,0:T(8,128)(2,1)S(1)}, u32[]{:S(2)}, u32[]{:S(2)}) collective-permute-start(bf16[2,128,512]{2,1,0:T(8,128)(2,1)S(1)} %slice.207), channel_id=1, source_target_pairs={{0,3},{1,0},{2,1},{3,2},{4,7},{5,4},{6,5},{7,6},{8,11},{9,8},{10,9... | collective-permute-start | bytes 786440 | tf_op jit(solution)/shard_map/ppermute | solution.py:369
  72.1 3.3 %collective-permute-start.9 = (bf16[4,128,512]{2,1,0:T(8,128)(2,1)S(1)}, bf16[4,128,512]{2,1,0:T(8,128)(2,1)S(1)}, u32[]{:S(2)}, u32[]{:S(2)}) collective-permute-start(bf16[4,128,512]{2,1,0:T(8,128)(2,1)S(1)} %slice.209), channel_id=1, source_target_pairs={{0,3},{1,0},{2,1},{3,2},{4,7},{5,4},{6,5},{7,6},{8,11},{9,8},{10,9... | collective-permute-start | bytes 1572872 | tf_op jit(solution)/shard_map/ppermute | solution.py:369
  75.4 2.8 %shard_map.129 = (bf16[4,384,128]{2,1,0:T(8,128)(2,1)S(1)}, f32[4,128,128]{2,1,0:T(8,128)S(1)}) custom-call(s32[1]{0:T(128)} %bitcast.row_ref.refs_0_, bf16[16,128,512]{2,1,0:T(8,128)(2,1)S(1)} %copy-done.3, bf16[4,128,512]{2,1,0:T(8,128)(2,1)} %collective-permute-done.4.left, bf16[4,128,512]{2,1,0:T(8,128)(2,1)} %collective-permute-done.6.right, ...), custom_call_target="tpu_custom_call" | custom-call | flops 805306368 | bytes 2097152 | tf_op jit(solution)/shard_map/pallas_call | solution.py:82
  79.3 6.6 %shard_map.127 = (bf16[12,384,128]{2,1,0:T(8,128)(2,1)S(1)}, f32[12,128,128]{2,1,0:T(8,128)S(1)}) custom-call(s32[1]{0:T(128)} %bitcast.row_ref.refs_0_, bf16[16,128,512]{2,1,0:T(8,128)(2,1)S(1)} %copy-done.3, bf16[12,128,512]{2,1,0:T(8,128)(2,1)} %collective-permute-done.left, bf16[12,128,512]{2,1,0:T(8,128)(2,1)} %collective-permute-done.2.right, ...), custom_call_target="tpu_custom_call" | custom-call | flops 2415919104 | bytes 6291456 | tf_op jit(solution)/shard_map/pallas_call | solution.py:82
  88.2 3.5 %collective-permute-start.3 = (bf16[2,128,512]{2,1,0:T(8,128)(2,1)S(1)}, bf16[2,128,512]{2,1,0:T(8,128)(2,1)S(1)}, u32[]{:S(2)}, u32[]{:S(2)}) collective-permute-start(bf16[2,128,512]{2,1,0:T(8,128)(2,1)S(1)} %slice.205), channel_id=1, source_target_pairs={{0,3},{1,0},{2,1},{3,2},{4,7},{5,4},{6,5},{7,6},{8,11},{9,8},{10,9... | collective-permute-start | bytes 786440 | tf_op jit(solution)/shard_map/ppermute | solution.py:369
  93.6 5.7 %shard_map.132 = (f32[10,128,128]{2,1,0:T(8,128)S(1)}, f32[10,256,128]{2,1,0:T(8,128)S(1)}) custom-call(f32[4,128,128]{2,1,0:T(8,128)S(1)} %get-tuple-element.45.lead0, f32[8,128,128]{2,1,0:T(8,128)S(1)} %get-tuple-element.46.lead1, f32[15,256,256]{2,1,0:T(8,128)S(1)} %copy-done.2, f32[15,256,128]{2,1,0:T(8,128)S(1)} %copy-done.7, ...), custom_call_target="tpu_custom_call" | custom-call | flops 1000000000 | bytes 9633792 | tf_op jit(solution)/shard_map/pallas_call | solution.py:47
  103.3 3.7 %shard_map.135.rest = f32[16,128,128]{2,1,0:T(8,128)S(1)} custom-call(f32[4,128,128]{2,1,0:T(8,128)S(1)} %get-tuple-element.68.lead2, f32[4,128,128]{2,1,0:T(8,128)S(1)} %get-tuple-element.69.late, f32[10,128,128]{2,1,0:T(8,128)S(1)} %get-tuple-element.62.early, f32[10,256,128]{2,1,0:T(8,128)S(1)} %get-tuple-element.70.base, f32[15,256,256]{2,1,0:T(8,128)S(1)} %copy-done.2, ...), custom_call_target="tpu_custom_call" | custom-call | flops 800000000 | bytes 11403264 | tf_op jit(solution)/shard_map/pallas_call | solution.py:47
  108.8 2.9 %collective-permute-done.16 = f32[128,128]{1,0:T(8,128)S(1)} collective-permute-done((f32[128,128]{1,0:T(8,128)S(1)}, f32[128,128]{1,0:T(8,128)S(1)}, u32[]{:S(2)}, u32[]{:S(2)}) %collective-permute-start.16) | collective-permute-done | bytes 65568 | tf_op jit(solution)/shard_map/ppermute | solution.py:472
  113.2 4.5 %collective-permute-done.17 = f32[128,128]{1,0:T(8,128)S(1)} collective-permute-done((f32[128,128]{1,0:T(8,128)S(1)}, f32[128,128]{1,0:T(8,128)S(1)}, u32[]{:S(2)}, u32[]{:S(2)}) %collective-permute-start.17) | collective-permute-done | bytes 65568 | tf_op jit(solution)/shard_map/ppermute | solution.py:472
  119.0 3.4 %collective-permute-done.18 = f32[128,128]{1,0:T(8,128)S(1)} collective-permute-done((f32[128,128]{1,0:T(8,128)S(1)}, f32[128,128]{1,0:T(8,128)S(1)}, u32[]{:S(2)}, u32[]{:S(2)}) %collective-permute-start.18) | collective-permute-done | bytes 65568 | tf_op jit(solution)/shard_map/ppermute | solution.py:472
  122.8 3.9 %collective-permute-start.19 = (f32[128,128]{1,0:T(8,128)S(1)}, f32[128,128]{1,0:T(8,128)S(1)}, u32[]{:S(2)}, u32[]{:S(2)}) collective-permute-start(f32[128,128]{1,0:T(8,128)S(1)} %convolution_add_fusion.1), channel_id=1, source_target_pairs={{0,96},{4,100},{8,104},{12,108},{16,112},{20,116},{24,120},{28,124... | collective-permute-start | bytes 196616 | tf_op jit(solution)/shard_map/ppermute | solution.py:472
  126.8 2.1 %collective-permute-done.19 = f32[128,128]{1,0:T(8,128)S(1)} collective-permute-done((f32[128,128]{1,0:T(8,128)S(1)}, f32[128,128]{1,0:T(8,128)S(1)}, u32[]{:S(2)}, u32[]{:S(2)}) %collective-permute-start.19) | collective-permute-done | bytes 65568 | tf_op jit(solution)/shard_map/ppermute | solution.py:472
  129.1 3.6 %leaf_result.1 = f32[8192,128]{1,0:T(8,128)} custom-call(s32[1]{0:T(128)} %bitcast.row_ref.refs_0_, f32[128,128]{1,0:T(8,128)S(1)} %convolution_add_fusion.top_ref, f32[16,128,128]{2,1,0:T(8,128)S(1)} %get-tuple-element.67.paths, f32[16,128,128]{2,1,0:T(8,128)S(1)} %shard_map.135.rest, bf16[16,512,128]{2,1,0:T(8,128)(2,1)S(1)} %copy-done.13, ...), custom_call_target="tpu_custom_call" | custom-call | tf_op jit(solution)/shard_map/leaf_result/pallas_call | solution.py:268
  (134 shorter events, 43.9 us)
Async XLA Ops:
  1.0 8.4 %collective-permute-start.10 = (f32[128,256]{1,0:T(8,128)S(1)}, f32[128,256]{1,0:T(8,128)S(1)}, u32[]{:S(2)}, u32[]{:S(2)}) collective-permute-start(f32[128,256]{1,0:T(8,128)S(1)} %slice_bitcast_fusion), channel_id=1, source_target_pairs={{64,0},{65,1},{66,2},{67,3}} | collective-permute-start | bytes 393224 | tf_op jit(solution)/shard_map/ppermute | solution.py:309
  6.2 24.2 %copy-start.21 = (f32[128,128]{1,0:T(8,128)}, f32[128,128]{1,0:T(8,128)S(1)}, u32[]{:S(2)}) copy-start(f32[128,128]{1,0:T(8,128)S(1)} %get-tuple-element.89) | copy-start | bytes 196612
  9.4 21.1 %copy-start.14 = (f32[128,640]{1,0:T(8,128)}, f32[128,640]{1,0:T(8,128)S(1)}, u32[]{:S(2)}) copy-start(f32[128,640]{1,0:T(8,128)S(1)} %get-tuple-element.86) | copy-start | bytes 983044
  9.4 9.0 %collective-permute-start.11 = (f32[128,640]{1,0:T(8,128)S(1)}, f32[128,640]{1,0:T(8,128)S(1)}, u32[]{:S(2)}, u32[]{:S(2)}) collective-permute-start(f32[128,640]{1,0:T(8,128)S(1)} %get-tuple-element.85), channel_id=1, source_target_pairs={{0,32},{32,0},{64,96},{96,64},{1,33},{33,1},{65,97},{97,65},{2,34}... | collective-permute-start | bytes 983048 | tf_op jit(solution)/shard_map/ppermute | solution.py:320
  18.5 11.9 %collective-permute-start.12 = (f32[128,896]{1,0:T(8,128)S(1)}, f32[128,896]{1,0:T(8,128)S(1)}, u32[]{:S(2)}, u32[]{:S(2)}) collective-permute-start(f32[128,896]{1,0:T(8,128)S(1)} %pad_select_fusion.2), channel_id=1, source_target_pairs={{0,16},{16,0},{32,48},{48,32},{64,80},{80,64},{96,112},{112,96},{1... | collective-permute-start | bytes 1376264 | tf_op jit(solution)/shard_map/ppermute | solution.py:320
  31.6 24.5 %collective-permute-start.13 = (f32[128,1536]{1,0:T(8,128)}, f32[128,1536]{1,0:T(8,128)}, u32[]{:S(2)}, u32[]{:S(2)}) collective-permute-start(f32[128,1536]{1,0:T(8,128)} %pad_select_fusion.1), channel_id=1, source_target_pairs={{0,8},{8,0},{16,24},{24,16},{32,40},{40,32},{48,56},{56,48},{64,72... | collective-permute-start | bytes 2359304 | tf_op jit(solution)/shard_map/ppermute | solution.py:320
  35.0 34.8 %collective-permute-start = (bf16[12,128,512]{2,1,0:T(8,128)(2,1)}, bf16[12,128,512]{2,1,0:T(8,128)(2,1)}, u32[]{:S(2)}, u32[]{:S(2)}) collective-permute-start(bf16[12,128,512]{2,1,0:T(8,128)(2,1)} %slice.153), channel_id=1, source_target_pairs={{0,1},{1,2},{2,3},{3,0},{4,5},{5,6},{6,7},{7,4},{8,9},{9,10},{10,1... | collective-permute-start | bytes 4718600 | tf_op jit(solution)/shard_map/ppermute | solution.py:359
  37.0 34.0 %collective-permute-start.2 = (bf16[12,128,512]{2,1,0:T(8,128)(2,1)}, bf16[12,128,512]{2,1,0:T(8,128)(2,1)}, u32[]{:S(2)}, u32[]{:S(2)}) collective-permute-start(bf16[12,128,512]{2,1,0:T(8,128)(2,1)} %slice.153), channel_id=1, source_target_pairs={{0,3},{1,0},{2,1},{3,2},{4,7},{5,4},{6,5},{7,6},{8,11},{9,8},{10,9... | collective-permute-start | bytes 4718600 | tf_op jit(solution)/shard_map/ppermute | solution.py:360
  40.0 23.5 %collective-permute-start.4 = (bf16[4,128,512]{2,1,0:T(8,128)(2,1)}, bf16[4,128,512]{2,1,0:T(8,128)(2,1)}, u32[]{:S(2)}, u32[]{:S(2)}) collective-permute-start(bf16[4,128,512]{2,1,0:T(8,128)(2,1)} %slice.160), channel_id=1, source_target_pairs={{0,1},{1,2},{2,3},{3,0},{4,5},{5,6},{6,7},{7,4},{8,9},{9,10},{10,1... | collective-permute-start | bytes 1572872 | tf_op jit(solution)/shard_map/ppermute | solution.py:359
  40.0 26.0 %collective-permute-start.6 = (bf16[4,128,512]{2,1,0:T(8,128)(2,1)}, bf16[4,128,512]{2,1,0:T(8,128)(2,1)}, u32[]{:S(2)}, u32[]{:S(2)}) collective-permute-start(bf16[4,128,512]{2,1,0:T(8,128)(2,1)} %slice.160), channel_id=1, source_target_pairs={{0,3},{1,0},{2,1},{3,2},{4,7},{5,4},{6,5},{7,6},{8,11},{9,8},{10,9... | collective-permute-start | bytes 1572872 | tf_op jit(solution)/shard_map/ppermute | solution.py:360
  58.1 41.1 %collective-permute-start.14 = (f32[128,2176]{1,0:T(8,128)S(1)}, f32[128,2176]{1,0:T(8,128)S(1)}, u32[]{:S(2)}, u32[]{:S(2)}) collective-permute-start(f32[128,2176]{1,0:T(8,128)S(1)} %pad_select_fusion), channel_id=1, source_target_pairs={{0,4},{4,0},{8,12},{12,8},{16,20},{20,16},{24,28},{28,24},{32,36},... | collective-permute-start | bytes 3342344 | tf_op jit(solution)/shard_map/ppermute | solution.py:320
  64.5 10.9 %copy-start.24 = (f32[16,128,128]{2,1,0:T(8,128)S(1)}, f32[16,128,128]{2,1,0:T(8,128)}, u32[]{:S(2)}) copy-start(f32[16,128,128]{2,1,0:T(8,128)} %param.17) | copy-start | bytes 3145732
  64.5 13.7 %collective-permute-start.5 = (bf16[2,128,512]{2,1,0:T(8,128)(2,1)S(1)}, bf16[2,128,512]{2,1,0:T(8,128)(2,1)S(1)}, u32[]{:S(2)}, u32[]{:S(2)}) collective-permute-start(bf16[2,128,512]{2,1,0:T(8,128)(2,1)S(1)} %slice.206), channel_id=1, source_target_pairs={{0,1},{1,2},{2,3},{3,0},{4,5},{5,6},{6,7},{7,4},{8,9},{9,10},{10,1... | collective-permute-start | bytes 786440 | tf_op jit(solution)/shard_map/ppermute | solution.py:368
  67.0 11.2 %collective-permute-start.7 = (bf16[2,128,512]{2,1,0:T(8,128)(2,1)S(1)}, bf16[2,128,512]{2,1,0:T(8,128)(2,1)S(1)}, u32[]{:S(2)}, u32[]{:S(2)}) collective-permute-start(bf16[2,128,512]{2,1,0:T(8,128)(2,1)S(1)} %slice.207), channel_id=1, source_target_pairs={{0,3},{1,0},{2,1},{3,2},{4,7},{5,4},{6,5},{7,6},{8,11},{9,8},{10,9... | collective-permute-start | bytes 786440 | tf_op jit(solution)/shard_map/ppermute | solution.py:369
  70.9 20.8 %collective-permute-start.8 = (bf16[4,128,512]{2,1,0:T(8,128)(2,1)S(1)}, bf16[4,128,512]{2,1,0:T(8,128)(2,1)S(1)}, u32[]{:S(2)}, u32[]{:S(2)}) collective-permute-start(bf16[4,128,512]{2,1,0:T(8,128)(2,1)S(1)} %slice.208), channel_id=1, source_target_pairs={{0,1},{1,2},{2,3},{3,0},{4,5},{5,6},{6,7},{7,4},{8,9},{9,10},{10,1... | collective-permute-start | bytes 1572872 | tf_op jit(solution)/shard_map/ppermute | solution.py:368
  72.1 19.6 %collective-permute-start.9 = (bf16[4,128,512]{2,1,0:T(8,128)(2,1)S(1)}, bf16[4,128,512]{2,1,0:T(8,128)(2,1)S(1)}, u32[]{:S(2)}, u32[]{:S(2)}) collective-permute-start(bf16[4,128,512]{2,1,0:T(8,128)(2,1)S(1)} %slice.209), channel_id=1, source_target_pairs={{0,3},{1,0},{2,1},{3,2},{4,7},{5,4},{6,5},{7,6},{8,11},{9,8},{10,9... | collective-permute-start | bytes 1572872 | tf_op jit(solution)/shard_map/ppermute | solution.py:369
  87.2 13.7 %collective-permute-start.1 = (bf16[2,128,512]{2,1,0:T(8,128)(2,1)S(1)}, bf16[2,128,512]{2,1,0:T(8,128)(2,1)S(1)}, u32[]{:S(2)}, u32[]{:S(2)}) collective-permute-start(bf16[2,128,512]{2,1,0:T(8,128)(2,1)S(1)} %slice.204), channel_id=1, source_target_pairs={{0,1},{1,2},{2,3},{3,0},{4,5},{5,6},{6,7},{7,4},{8,9},{9,10},{10,1... | collective-permute-start | bytes 786440 | tf_op jit(solution)/shard_map/ppermute | solution.py:368
  88.2 12.6 %collective-permute-start.3 = (bf16[2,128,512]{2,1,0:T(8,128)(2,1)S(1)}, bf16[2,128,512]{2,1,0:T(8,128)(2,1)S(1)}, u32[]{:S(2)}, u32[]{:S(2)}) collective-permute-start(bf16[2,128,512]{2,1,0:T(8,128)(2,1)S(1)} %slice.205), channel_id=1, source_target_pairs={{0,3},{1,0},{2,1},{3,2},{4,7},{5,4},{6,5},{7,6},{8,11},{9,8},{10,9... | collective-permute-start | bytes 786440 | tf_op jit(solution)/shard_map/ppermute | solution.py:369
  102.7 4.3 %collective-permute-start.15 = (f32[128,128]{1,0:T(8,128)S(1)}, f32[128,128]{1,0:T(8,128)S(1)}, u32[]{:S(2)}, u32[]{:S(2)}) collective-permute-start(f32[128,128]{1,0:T(8,128)S(1)} %get-tuple-element.63), channel_id=1, source_target_pairs={{0,4},{4,0},{8,12},{12,8},{16,20},{20,16},{24,28},{28,24},{32,36},... | collective-permute-start | bytes 196616 | tf_op jit(solution)/shard_map/ppermute | solution.py:472
  107.2 4.6 %collective-permute-start.16 = (f32[128,128]{1,0:T(8,128)S(1)}, f32[128,128]{1,0:T(8,128)S(1)}, u32[]{:S(2)}, u32[]{:S(2)}) collective-permute-start(f32[128,128]{1,0:T(8,128)S(1)} %convolution_add_fusion.8), channel_id=1, source_target_pairs={{0,8},{4,12},{8,0},{12,4},{16,24},{20,28},{24,16},{28,20},{32,40},... | collective-permute-start | bytes 196616 | tf_op jit(solution)/shard_map/ppermute | solution.py:472
  111.9 17.1 %copy-start.13 = (bf16[16,512,128]{2,1,0:T(8,128)(2,1)S(1)}, bf16[16,512,128]{2,1,0:T(8,128)(2,1)}, u32[]{:S(2)}) copy-start(bf16[16,512,128]{2,1,0:T(8,128)(2,1)} %back.7) | copy-start | bytes 6291460
  112.1 5.6 %collective-permute-start.17 = (f32[128,128]{1,0:T(8,128)S(1)}, f32[128,128]{1,0:T(8,128)S(1)}, u32[]{:S(2)}, u32[]{:S(2)}) collective-permute-start(f32[128,128]{1,0:T(8,128)S(1)} %convolution_add_fusion.5), channel_id=1, source_target_pairs={{0,24},{4,28},{8,16},{12,20},{16,8},{20,12},{24,0},{28,4},{32,56},... | collective-permute-start | bytes 196616 | tf_op jit(solution)/shard_map/ppermute | solution.py:472
  118.0 4.3 %collective-permute-start.18 = (f32[128,128]{1,0:T(8,128)S(1)}, f32[128,128]{1,0:T(8,128)S(1)}, u32[]{:S(2)}, u32[]{:S(2)}) collective-permute-start(f32[128,128]{1,0:T(8,128)S(1)} %convolution_add_fusion.3), channel_id=1, source_target_pairs={{0,32},{4,36},{8,40},{12,44},{16,48},{20,52},{24,56},{28,60},{32,0... | collective-permute-start | bytes 196616 | tf_op jit(solution)/shard_map/ppermute | solution.py:472
  122.8 6.1 %collective-permute-start.19 = (f32[128,128]{1,0:T(8,128)S(1)}, f32[128,128]{1,0:T(8,128)S(1)}, u32[]{:S(2)}, u32[]{:S(2)}) collective-permute-start(f32[128,128]{1,0:T(8,128)S(1)} %convolution_add_fusion.1), channel_id=1, source_target_pairs={{0,96},{4,100},{8,104},{12,108},{16,112},{20,116},{24,120},{28,124... | collective-permute-start | bytes 196616 | tf_op jit(solution)/shard_map/ppermute | solution.py:472
  (22 other events, 67.5 us)

commit v2 on v1

v2 whole, which is shorter than its diff:
```python
import functools

import jax
import jax.numpy as jnp
from jax import lax
from jax.experimental import pallas as pl
from jax.experimental.pallas import tpu as pltpu
from jax.sharding import PartitionSpec as P


wide = jnp.float32
narrow = jnp.bfloat16

GROUPS = ((0, 8), (8, 4), (12, 4))
PIECES = ((0, 4), (4, 4), (8, 8))
MERGED = ((0, 1, 2, 3, 8, 9, 12), (4, 5, 10))
LATE = (6, 7, 11, 13, 14)
FRONT = (((0,), (0,)), ((), ()))


def narrow_dot(a, b):
    return jnp.dot(a.astype(narrow), b.astype(narrow), preferred_element_type=wide)


def parts_of(a):
    high = a.astype(narrow)
    return high, (a - high.astype(wide)).astype(narrow)


def split_dot(a, b, dims=(((1,), (0,)), ((), ()))):
    a_high, a_low = parts_of(a)
    b_high, b_low = parts_of(b)

    def one(p, q):
        return lax.dot_general(p, q, dims, preferred_element_type=wide)

    return one(a_high, b_low) + one(a_low, b_high) + one(a_high, b_high)


def close_dot(a, b):
    return jnp.dot(a, b, precision=lax.Precision.HIGH, preferred_element_type=wide)


def kernel_call(body, out_shape, flops, operands, scalars=0, room=10, **more):
    if scalars:
        more["in_specs"] = [pl.BlockSpec(memory_space=pltpu.SMEM)] * scalars + [
            pl.BlockSpec(a.shape, lambda a=a: (0,) * a.ndim) for a in operands[scalars:]
        ]
    size = sum(a.size * a.dtype.itemsize for a in operands)
    return pl.pallas_call(
        body,
        out_shape=out_shape,
        cost_estimate=pl.CostEstimate(flops=flops, bytes_accessed=size, transcendentals=0),
        compiler_params=pltpu.CompilerParams(vmem_limit_bytes=room * 1024 * 1024),
        **more,
    )(*operands)


def turned(row_ref, part, height):
    return pl.multiple_of(lax.rem(row_ref[0] + part, 4) * height, height)


def near_body(row_ref, own, left, right, rhs, basis, vals, proj):
    count, height, width = own.shape
    for k in range(count):
        rows = jnp.concatenate([own[k], left[k], right[k]], axis=0)
        got = narrow_dot(rows, rhs[k * width : (k + 1) * width, :]).astype(narrow)
        vals[k] = got
        matching = jnp.concatenate(
            [basis[k, pl.ds(turned(row_ref, part, height), height), :] for part in (0, 3, 1)],
            axis=0,
        )
        proj[k] = lax.dot_general(matching, got, FRONT, preferred_element_type=wide)


def near_call(piece, row, own, left, right, rhs, basis):
    start, count = PIECES[piece]
    height, width = left.shape[1:]
    rank, columns = basis.shape[2], rhs.shape[1]
    some = 4
    base = start // some

    def at(shape, shift):
        return pl.BlockSpec(shape, lambda i, row: (shift + i,) + (0,) * (len(shape) - 1))

    return pl.pallas_call(
        near_body,
        grid_spec=pltpu.PrefetchScalarGridSpec(
            num_scalar_prefetch=1,
            grid=(count // some,),
            in_specs=[
                at((some, height, width), base),
                at((some, height, width), 0),
                at((some, height, width), 0),
                at((some * width, columns), base),
                at((some, width, rank), base),
            ],
            out_specs=[
                at((some, 3 * height, columns), 0),
                at((some, rank, columns), 0),
            ],
        ),
        out_shape=[
            jax.ShapeDtypeStruct((count, 3 * height, columns), narrow),
            jax.ShapeDtypeStruct((count, rank, columns), wide),
        ],
        cost_estimate=pl.CostEstimate(
            flops=count * 2 * 3 * height * width * columns * 4,
            bytes_accessed=count * width * width * 2,
            transcendentals=0,
        ),
        compiler_params=pltpu.CompilerParams(vmem_limit_bytes=8 * 1024 * 1024),
    )(row, own, left, right, rhs, basis)


def far_leaves(group, row_ref, far_a, far_b, rhs, basis, coarse, parts, vals, proj, lead):
    start, count = GROUPS[group]
    height, width = far_a.shape[1], far_a.shape[2]
    half = count // 2
    at = turned(row_ref, 2, height)
    for k in range(count):
        leaf = start + k
        rows = far_a[k] if k < half else far_b[k - half]
        got = narrow_dot(rows, rhs[leaf * width : (leaf + 1) * width, :]).astype(narrow)
        vals[k] = got
        before = parts[k // half][k % half] if group == 0 else parts[0][leaf - PIECES[2][0]]
        total = before + lax.dot_general(
            basis[leaf, pl.ds(at, height), :], got, FRONT, preferred_element_type=wide
        )
        proj[k] = total
        lead[k] = split_dot(coarse[leaf], total)


def far_body(group, refs):
    inputs, outputs = refs[:6], refs[-3:]
    far_leaves(group, *inputs, refs[6:-3], *outputs)


def last_body(
    row_ref, far_a, far_b, rhs, basis, coarse, part, ups, early0, early1,
    vals, proj, lead, late, up,
):
    far_leaves(2, row_ref, far_a, far_b, rhs, basis, coarse, (part,), vals, proj, lead)
    value = {12 + k: (lead, k) for k in range(4)}
    for early, nodes in zip((early0, early1), MERGED):
        for k, node in enumerate(nodes):
            value[16 + node] = (early, k)
    for k, node in enumerate(LATE):
        pair = [value[c][0][value[c][1]] for c in (2 * node, 2 * node + 1)]
        got = split_dot(ups[k], jnp.concatenate(pair, axis=0))
        if k == len(LATE) - 1:
            up[...] = got
        else:
            late[k] = got
        value[16 + node] = (late, k)


def far_shapes(count, height, rank, columns):
    return [
        jax.ShapeDtypeStruct((count, height, columns), narrow),
        jax.ShapeDtypeStruct((count, rank, columns), wide),
        jax.ShapeDtypeStruct((count, rank, columns), wide),
    ]


def merge_body(group, lead, inv, basis, back, coarse, early, base):
    value = {GROUPS[group][0] + k: (lead, k) for k in range(lead.shape[0])}
    for k, node in enumerate(MERGED[group]):
        pair = [value[c][0][value[c][1]] for c in (2 * node, 2 * node + 1)]
        solved = split_dot(inv[node], jnp.concatenate(pair, axis=0))
        reduced = split_dot(basis[node], solved, FRONT)
        early[k] = split_dot(coarse[node], reduced)
        base[k] = solved - split_dot(back[node], reduced)
        value[16 + node] = (early, k)


def prepare_body(inv, basis, back, coarse, ups, paths):
    for k, node in enumerate(LATE):
        ups[k] = split_dot(coarse[node], split_dot(basis[node], inv[node], FRONT))
    value = {30: None}
    rank = paths.shape[1]
    for node in reversed(range(15)):
        above = value[16 + node]
        below = back[node] if above is None else split_dot(back[node], above)
        for k in range(2):
            value[2 * node + k] = below[k * rank : (k + 1) * rank]
            if node < 8:
                paths[2 * node + k] = value[2 * node + k]


def late_body(lead2, late, early0, early1, inv, basis, back, base):
    value = {12 + k: (lead2, k) for k in range(4)}
    for early, nodes in zip((early0, early1), MERGED):
        for k, node in enumerate(nodes):
            value[16 + node] = (early, k)
    for k, node in enumerate(LATE[:-1]):
        value[16 + node] = (late, k)
    for k, node in enumerate(LATE):
        pair = [value[c][0][value[c][1]] for c in (2 * node, 2 * node + 1)]
        solved = split_dot(inv[node], jnp.concatenate(pair, axis=0))
        reduced = split_dot(basis[node], solved, FRONT)
        base[k] = solved - split_dot(back[node], reduced)


def known_body(base0, base1, base2, back, proj0, proj1, proj2, rest):
    rank = proj0.shape[1]
    known = {}
    for base, nodes in zip((base0, base1, base2), (*MERGED, LATE)):
        for k, node in enumerate(nodes):
            known[node] = (base, k)
    projs = [(proj, k) for proj in (proj0, proj1, proj2) for k in range(proj.shape[0])]
    part = {30: None}
    for node in reversed(range(15)):
        ref, at = known[node]
        halves = ref[at]
        if part[16 + node] is not None:
            halves = halves + split_dot(back[node], part[16 + node])
        for k in range(2):
            below = halves[k * rank : (k + 1) * rank]
            part[2 * node + k] = below
            if node < 8:
                ref, at = projs[2 * node + k]
                rest[2 * node + k] = ref[at] - below


def spread_body(size, flags, got, upper, low_half, high_half, wider, message):
    high, next_high = flags[0] == 1, flags[1] == 1
    mine = low_half.shape[1]
    if size:
        wider[:, :size] = jnp.where(high, got[:, :size], upper[...])
        wider[:, size:] = jnp.where(high, high_half[...], got[:, :mine])
    else:
        wider[...] = jnp.where(high, upper[...], got[...])
    held = wider.shape[1]
    both = min(mine, held)
    message[:, :both] = jnp.where(next_high, low_half[:, :both], wider[:, :both])
    if mine > held:
        message[:, held:] = low_half[:, held:]
    if held > mine:
        message[:, mine:] = wider[:, mine:]


def top_body(left_ref, got, upper, high_half, up_own, up_sib, down_own, down_sib, packs):
    depth = down_own.shape[0]
    rank = packs.shape[0]
    size = upper.shape[1]
    high = left_ref[0] == 0
    packs[:, :size] = jnp.where(high, got[:, :size], upper[...])
    packs[:, size:] = jnp.where(high, high_half[...], got[:, : high_half.shape[1]])
    path = None
    for level in range(depth):
        root = level == depth - 1
        first = 0 if root else 2 * rank + (depth - 2 - level) * 5 * rank
        is_left = left_ref[level] == 1

        def both(matrix):
            one, two = matrix[:, :rank], matrix[:, rank:]
            return jnp.where(is_left, one, two), jnp.where(is_left, two, one)

        if root:
            down = packs[:, first : first + 2 * rank]
        else:
            up_own[level], up_sib[level] = both(packs[:, first : first + 2 * rank])
            down = packs[:, first + 2 * rank : first + 4 * rank]
        if path is not None:
            down = split_dot(path, down)
        down_own[level], down_sib[level] = both(down)
        if not root:
            step = packs[:, first + 4 * rank : first + 5 * rank]
            path = step if path is None else split_dot(path, step)


def out_body(
    row_ref, top_ref, paths, rest, back, near0, near1, near2, far0, far1, far2, out
):
    some, width = back.shape[0], back.shape[1]
    height = far0.shape[1]
    top = top_ref[...]
    leaf = pl.program_id(0) * some
    at = [turned(row_ref, part, height) for part in (0, 3, 1, 2)]

    def pick(refs, spans, k):
        chosen = refs[-1][k]
        for ref, (start, _) in zip(refs[-2::-1], spans[:0:-1]):
            chosen = jnp.where(leaf < start, ref[k], chosen)
        return chosen

    for k in range(some):
        difference = (rest[k] - split_dot(paths[k], top)).astype(narrow)
        matching = jnp.concatenate([back[k, pl.ds(a, height), :] for a in at], axis=0)
        change = narrow_dot(matching, difference)
        near = pick((near0, near1, near2), PIECES, k)
        far = pick((far0, far1, far2), GROUPS, k)
        for j, a in enumerate(at):
            block = far if j == 3 else near[j * height : (j + 1) * height]
            out[pl.ds(pl.multiple_of(k * width + a, height), height), :] = (
                block.astype(wide) - change[j * height : (j + 1) * height]
            )


def out_call(row, top, paths, rest, back, nears, fars):
    leaves, width, rank = back.shape
    height, columns = fars[0].shape[1:]
    some = 2

    def at(shape):
        return pl.BlockSpec(shape, lambda i, row: (i,) + (0,) * (len(shape) - 1))

    def within(shape, span):
        first, most = span[0] // some, span[1] // some - 1
        return pl.BlockSpec(
            shape, lambda i, row: (jnp.clip(i - first, 0, most),) + (0,) * (len(shape) - 1)
        )

    return pl.pallas_call(
        out_body,
        grid_spec=pltpu.PrefetchScalarGridSpec(
            num_scalar_prefetch=1,
            grid=(leaves // some,),
            in_specs=[
                pl.BlockSpec(top.shape, lambda i, row: (0, 0)),
                at((some, rank, rank)),
                at((some, rank, columns)),
                at((some, width, rank)),
                *[within((some, 3 * height, columns), span) for span in PIECES],
                *[within((some, height, columns), span) for span in GROUPS],
            ],
            out_specs=at((some * width, columns)),
        ),
        out_shape=jax.ShapeDtypeStruct((leaves * width, columns), wide),
        compiler_params=pltpu.CompilerParams(vmem_limit_bytes=8 * 1024 * 1024),
        name="leaf_result",
    )(row, top, paths, rest, back, *nears, *fars)


def exact(eq, a, b):
    return jnp.einsum(eq, a, b, precision=lax.Precision.HIGHEST)


def top_factors(inv, basis, back, coarse, position, depth):
    total = lax.axis_size("leaf")
    rank = basis.shape[1]
    reduce_mat = exact("ik,ij->kj", basis, inv)
    up_mat = exact("kl,lj->kj", coarse, reduce_mat)
    down_mat = inv - exact("ik,kj->ij", back, reduce_mat)
    halves = [
        jnp.concatenate([up_mat, down_mat[s : s + rank], back[s : s + rank]], axis=1)
        for s in (0, rank)
    ]
    high = [((position >> bit) % 2).astype(jnp.int32) for bit in range(depth)]
    mine = halves[0].shape[1]
    upper, message, size = inv[rank:], inv[:rank], 0
    for bit in reversed(range(depth)):
        stride = 1 << bit
        if size == 0:
            pairs = [(stride, 0)]
        else:
            pairs = [(i, i ^ stride) for i in range(0, total, stride)]
        got = lax.ppermute(message, "leaf", pairs)
        if bit == 0:
            return got, upper, halves[1]
        held = size + mine if size else 2 * rank
        upper, message = kernel_call(
            functools.partial(spread_body, size),
            [
                jax.ShapeDtypeStruct((rank, held), wide),
                jax.ShapeDtypeStruct((rank, max(held, mine)), wide),
            ],
            10**6,
            (jnp.stack([high[bit], high[bit - 1]]), got, upper, *halves),
            scalars=1,
        )
        size = held


def solve(
    rhs_cols,
    leaf_inv,
    leaf_basis,
    leaf_back,
    leaf_coarse,
    mid_inv,
    mid_basis,
    mid_back,
    mid_coarse,
    top_inv,
    top_basis,
    top_back,
    top_coarse,
):
    leaf_count, height, _ = leaf_inv.shape
    rank, columns = leaf_basis.shape[2], rhs_cols.shape[1]
    position = lax.axis_index("leaf")
    leaf_total = lax.axis_size("leaf")
    depth = leaf_total.bit_length() - 1
    ring = lax.axis_size("rhs")
    ahead = [(i, (i + 1) % ring) for i in range(ring)]
    behind = [(i, (i - 1) % ring) for i in range(ring)]
    row = lax.axis_index("rhs").astype(jnp.int32).reshape(1)

    own = [leaf_inv[start : start + count] for start, count in PIECES]
    left, right = {}, {}
    for k, forth_first in ((0, True), (1, False), (1, True), (0, False), (2, True), (2, False)):
        if forth_first:
            left[k] = lax.ppermute(own[k], "rhs", ahead)
        else:
            right[k] = lax.ppermute(own[k], "rhs", behind)
    pairs = ((left[0], right[1]),) + tuple(
        (left[2][s : s + 2], right[2][s + 2 : s + 4]) for s in (0, 4)
    )
    far = [
        (lax.ppermute(one, "rhs", ahead), lax.ppermute(two, "rhs", behind))
        for one, two in pairs
    ]

    got, upper, own_half = top_factors(
        top_inv[0], top_basis[0], top_back[0], top_coarse[0], position, depth
    )
    sides = jnp.stack([1 - (position >> k) % 2 for k in range(depth)]).astype(jnp.int32)
    square = (rank, rank)
    up_own, up_sib, down_own, down_sib = kernel_call(
        top_body,
        [jax.ShapeDtypeStruct((n, *square), wide) for n in (depth - 1, depth - 1, depth, depth)],
        10**8,
        (sides, got, upper, own_half),
        scalars=1,
        scratch_shapes=[pltpu.VMEM((rank, upper.shape[1] + own_half.shape[1]), wide)],
    )
    ups, paths = kernel_call(
        prepare_body,
        [
            jax.ShapeDtypeStruct((len(LATE), rank, 2 * rank), wide),
            jax.ShapeDtypeStruct((leaf_count, *square), wide),
        ],
        8 * 10**8,
        (mid_inv, mid_basis, mid_back, mid_coarse),
        room=12,
    )

    nears, parts = [], []
    for k in range(len(PIECES)):
        near, part = near_call(k, row, leaf_inv, left[k], right[k], rhs_cols, leaf_basis)
        nears.append(near)
        parts.append(part)
    shared = (rhs_cols, leaf_basis, leaf_coarse)
    results, merged = [], []
    for k in range(2):
        count = GROUPS[k][1]
        results.append(
            kernel_call(
                lambda *refs, k=k: far_body(k, refs),
                far_shapes(count, height, rank, columns),
                count * 4 * 10**7,
                (row, *far[k], *shared, *(parts[:2] if k == 0 else parts[2:])),
                scalars=1,
            )
        )
        merged.append(
            kernel_call(
                functools.partial(merge_body, k),
                [
                    jax.ShapeDtypeStruct((len(MERGED[k]), rank, columns), wide),
                    jax.ShapeDtypeStruct((len(MERGED[k]), 2 * rank, columns), wide),
                ],
                len(MERGED[k]) * 10**8,
                (results[k][2], mid_inv, mid_basis, mid_back, mid_coarse),
                room=12,
            )
        )
    earlies = [m[0] for m in merged]
    final = lax.optimization_barrier(
        (far[2], parts[2], ups, earlies, up_own, up_sib, down_own, down_sib, paths)
    )
    last_far, part, ups, earlies, up_own, up_sib, down_own, down_sib, paths = final
    *last, late, current = kernel_call(
        last_body,
        far_shapes(GROUPS[2][1], height, rank, columns)
        + [
            jax.ShapeDtypeStruct((len(LATE) - 1, rank, columns), wide),
            jax.ShapeDtypeStruct((rank, columns), wide),
        ],
        3 * 10**8,
        (row, *last_far, *shared, part, ups, *earlies),
        scalars=1,
    )
    results.append(last)
    bases = [m[1] for m in merged]
    bases.append(
        kernel_call(
            late_body,
            jax.ShapeDtypeStruct((len(LATE), 2 * rank, columns), wide),
            4 * 10**8,
            (last[2], late, *earlies, mid_inv, mid_basis, mid_back),
            room=12,
        )
    )
    rest = kernel_call(
        known_body,
        jax.ShapeDtypeStruct((leaf_count, rank, columns), wide),
        4 * 10**8,
        (*bases, mid_back, *[r[1] for r in results]),
        room=12,
    )

    top = None
    for level in range(depth):
        mask = 1 << level
        if level in (2, 4):
            mask |= mask >> 1
        pairs = [(i, i ^ mask) for i in range(leaf_total)]
        partner = lax.ppermute(current, "leaf", pairs)
        known = close_dot(down_own[level], current)
        top = known if top is None else top + known
        top = top + close_dot(down_sib[level], partner)
        if level < depth - 1:
            before = close_dot(up_own[level], current)
            current = before + close_dot(up_sib[level], partner)
    return out_call(row, top, paths, rest, leaf_back, nears, [r[0] for r in results])


def solution(mesh):
    return jax.shard_map(
        solve,
        mesh=mesh,
        in_specs=(P("leaf", "rhs"), P("leaf", "rhs", None))
        + (P("leaf", None, None),) * 11,
        out_specs=P("leaf", "rhs"),
        check_vma=False,
    )
```

time: 134 us -> 151 us (1.13)
  waiting for transfers between devices: 36.7 us -> 59.5 us
  Pallas kernels: 30.4 us -> 39.2 us
  starting transfers between devices: 32.3 us -> 24.8 us
  local copies, waits for them, and re-layouts: 22.7 us -> 19.6 us
  other arithmetic: 2.72 us -> 0.35 us
    ppermute x11 -> x12, waiting for transfers between devices: 6.93 us -> 20.9 us  [the longest x3 8.7 us: solve(): lax.ppermute(two, 'rhs', behind)]
    slice x17 -> x5, local copies, waits for them, and re-layouts: 12.9 us -> 5.41 us  [the longest x2 2.25 us: solve(): own = [leaf_inv[start:start + count] for start, count in PIECES]]
    pallas_call x7 -> x13, Pallas kernels: 17.3 us -> 23.9 us  [kernel_call(): pl.pallas_call(body, out_shape=out_shape, cost_estimate=pl.CostEstimate(f...]
    ppermute x4 -> x5, waiting for transfers between devices: 17 us -> 22.5 us  [top_factors(): got = lax.ppermute(message, 'leaf', pairs)]
    ppermute x11 -> x12, starting transfers between devices: 20 us -> 15 us  [the longest x3 7.46 us: solve(): right[k] = lax.ppermute(own[k], 'rhs', behind)]
    ppermute x5, starting transfers between devices: 6.38 us -> 2.85 us  [solve(): partner = lax.ppermute(current, 'leaf', pairs)]
    unnamed x52 -> x50, local copies, waits for them, and re-layouts: 9.7 us -> 13.2 us
    ppermute x5, waiting for transfers between devices: 12.8 us -> 16.1 us  [solve(): partner = lax.ppermute(current, 'leaf', pairs)]
  transfers between devices with their start and end apart: 20 -> 22, of which waited for: 8 -> 11; matrix products, arithmetic and copies ran while one was open for 14% -> 7% of each run, Pallas kernels for 19% -> 18%
where the time goes in v2:
time: 151 us; the launch traced here: 150 us
  waiting for transfers between devices  59.5 us (39%)
  Pallas kernels  39.2 us (26%)
  starting transfers between devices  24.8 us (16%)
  local copies, waits for them, and re-layouts  19.6 us (13%)
  matrix products  6.17 us (4%)
    pallas_call x13, Pallas kernels, kernel_call(): pl.pallas_call(body, out_shape=out_shape, cost_estimate=pl.CostEstimate(f...  23.9 us
    ppermute x5, waiting for transfers between devices, top_factors(): got = lax.ppermute(message, 'leaf', pairs)  22.5 us
    ppermute x5, waiting for transfers between devices, solve(): partner = lax.ppermute(current, 'leaf', pairs)  16.1 us
    unnamed x50, local copies, waits for them, and re-layouts  13.2 us
    pallas_call x3, Pallas kernels, near_call(): pl.pallas_call(near_body, grid_spec=pltpu.PrefetchScalarGridSpec(num_scal...  9.18 us
    ppermute x3, waiting for transfers between devices, solve(): lax.ppermute(two, 'rhs', behind)  8.7 us
    ppermute x3, starting transfers between devices, solve(): right[k] = lax.ppermute(own[k], 'rhs', behind)  7.46 us
    ppermute x5, starting transfers between devices, top_factors(): got = lax.ppermute(message, 'leaf', pairs)  7.02 us
  transfers between devices with their start and end apart: 22, of which 11 were waited for; matrix products, arithmetic and copies ran while one was open for 7% of the time, Pallas kernels for 18%

profile of v2, /device:TPU:0, one launch (start us, length us, event | category | flops | bytes accessed | tf_op | source)
XLA Modules:
  0.0 150.2 jit_solution(8828865261490279379)
XLA Ops:
  6.5 2.9 %collective-permute-done.12.got = f32[128,256]{1,0:T(8,128)S(1)} collective-permute-done((f32[128,256]{1,0:T(8,128)S(1)}, f32[128,256]{1,0:T(8,128)S(1)}, u32[]{:S(2)}, u32[]{:S(2)}) %collective-permute-start.12) | collective-permute-done | bytes 131104 | tf_op jit(solution)/shard_map/ppermute | solution.py:359
  12.7 7.2 %collective-permute-done.13.got = f32[128,640]{1,0:T(8,128)S(1)} collective-permute-done((f32[128,640]{1,0:T(8,128)}, f32[128,640]{1,0:T(8,128)S(1)}, u32[]{:S(2)}, u32[]{:S(2)}) %collective-permute-start.13) | collective-permute-done | bytes 327712 | tf_op jit(solution)/shard_map/ppermute | solution.py:359
  25.0 10.2 %collective-permute-done.14.got = f32[128,896]{1,0:T(8,128)} collective-permute-done((f32[128,896]{1,0:T(8,128)}, f32[128,896]{1,0:T(8,128)}, u32[]{:S(2)}, u32[]{:S(2)}) %collective-permute-start.14) | collective-permute-done | bytes 458784 | tf_op jit(solution)/shard_map/ppermute | solution.py:359
  40.3 4.1 %collective-permute-start.2 = (bf16[8,128,512]{2,1,0:T(8,128)(2,1)}, bf16[8,128,512]{2,1,0:T(8,128)(2,1)}, u32[]{:S(2)}, u32[]{:S(2)}) collective-permute-start(bf16[8,128,512]{2,1,0:T(8,128)(2,1)} %slice.105), channel_id=1, source_target_pairs={{0,3},{1,0},{2,1},{3,2},{4,7},{5,4},{6,5},{7,6},{8,11},{9,8},{10,9... | collective-permute-start | bytes 3145736 | tf_op jit(solution)/shard_map/ppermute | solution.py:407
  45.6 3.2 %collective-permute-start.6 = (bf16[4,128,512]{2,1,0:T(8,128)(2,1)}, bf16[4,128,512]{2,1,0:T(8,128)(2,1)}, u32[]{:S(2)}, u32[]{:S(2)}) collective-permute-start(bf16[4,128,512]{2,1,0:T(8,128)(2,1)} %get-tuple-element.97), channel_id=1, source_target_pairs={{0,3},{1,0},{2,1},{3,2},{4,7},{5,4},{6,5},{7,6},{8,11},{9,8},{10,9... | collective-permute-start | bytes 1572872 | tf_op jit(solution)/shard_map/ppermute | solution.py:407
  48.8 2.3 %collective-permute-done.15.got = f32[128,1536]{1,0:T(8,128)S(1)} collective-permute-done((f32[128,1536]{1,0:T(8,128)S(1)}, f32[128,1536]{1,0:T(8,128)S(1)}, u32[]{:S(2)}, u32[]{:S(2)}) %collective-permute-start.15) | collective-permute-done | bytes 786464 | tf_op jit(solution)/shard_map/ppermute | solution.py:359
  52.0 2.0 %collective-permute-start.4 = (bf16[4,128,512]{2,1,0:T(8,128)(2,1)}, bf16[4,128,512]{2,1,0:T(8,128)(2,1)}, u32[]{:S(2)}, u32[]{:S(2)}) collective-permute-start(bf16[4,128,512]{2,1,0:T(8,128)(2,1)} %get-tuple-element.98), channel_id=1, source_target_pairs={{0,1},{1,2},{2,3},{3,0},{4,5},{5,6},{6,7},{7,4},{8,9},{9,10},{10,1... | collective-permute-start | bytes 1572872 | tf_op jit(solution)/shard_map/ppermute | solution.py:405
  60.0 6.3 %collective-permute-done.9.left = bf16[4,128,512]{2,1,0:T(8,128)(2,1)} collective-permute-done((bf16[4,128,512]{2,1,0:T(8,128)(2,1)}, bf16[4,128,512]{2,1,0:T(8,128)(2,1)}, u32[]{:S(2)}, u32[]{:S(2)}) %collective-permute-start.9) | collective-permute-done | bytes 524320 | tf_op jit(solution)/shard_map/ppermute | solution.py:405
  66.4 2.1 %copy-done.3 = f32[15,256,256]{2,1,0:T(8,128)S(1)} copy-done((f32[15,256,256]{2,1,0:T(8,128)S(1)}, f32[15,256,256]{2,1,0:T(8,128)}, u32[]{:S(2)}) %copy-start.3) | copy-done | bytes 3932184
  73.0 2.6 %shard_map.130 = (bf16[4,384,128]{2,1,0:T(8,128)(2,1)S(1)}, f32[4,128,128]{2,1,0:T(8,128)S(1)}) custom-call(s32[1]{0:T(128)} %bitcast.row_ref.refs_0_, bf16[16,128,512]{2,1,0:T(8,128)(2,1)S(1)} %copy-done.8, bf16[4,128,512]{2,1,0:T(8,128)(2,1)} %collective-permute-done.9.left, bf16[4,128,512]{2,1,0:T(8,128)(2,1)} %collective-permute-done.6.right, ...), custom_call_target="tpu_custom_call" | custom-call | flops 805306368 | bytes 2097152 | tf_op jit(solution)/shard_map/pallas_call | solution.py:86
  75.7 2.0 %collective-permute-start.5 = (bf16[4,128,512]{2,1,0:T(8,128)(2,1)}, bf16[4,128,512]{2,1,0:T(8,128)(2,1)S(1)}, u32[]{:S(2)}, u32[]{:S(2)}) collective-permute-start(bf16[4,128,512]{2,1,0:T(8,128)(2,1)} %collective-permute-done.4.left), channel_id=1, source_target_pairs={{0,1},{1,2},{2,3},{3,0},{4,5},{5,6},{6,7},{7,4},{8,9},{9,10},{10,1... | collective-permute-start | bytes 1572872 | tf_op jit(solution)/shard_map/ppermute | solution.py:412
  81.2 5.9 %collective-permute-done.8.right = bf16[4,128,512]{2,1,0:T(8,128)(2,1)S(1)} collective-permute-done((bf16[4,128,512]{2,1,0:T(8,128)(2,1)}, bf16[4,128,512]{2,1,0:T(8,128)(2,1)S(1)}, u32[]{:S(2)}, u32[]{:S(2)}) %collective-permute-start.8) | collective-permute-done | bytes 524320 | tf_op jit(solution)/shard_map/ppermute | solution.py:407
  87.1 2.5 %shard_map.129 = (bf16[4,384,128]{2,1,0:T(8,128)(2,1)S(1)}, f32[4,128,128]{2,1,0:T(8,128)S(1)}) custom-call(s32[1]{0:T(128)} %bitcast.row_ref.refs_0_, bf16[16,128,512]{2,1,0:T(8,128)(2,1)S(1)} %copy-done.8, bf16[4,128,512]{2,1,0:T(8,128)(2,1)} %collective-permute-done.4.left, bf16[4,128,512]{2,1,0:T(8,128)(2,1)S(1)} %collective-permute-done.8.right, ...), custom_call_target="tpu_custom_call" | custom-call | flops 805306368 | bytes 2097152 | tf_op jit(solution)/shard_map/pallas_call | solution.py:86
  89.6 8.7 %collective-permute-done.7.refs_2_ = bf16[4,128,512]{2,1,0:T(8,128)(2,1)S(1)} collective-permute-done((bf16[4,128,512]{2,1,0:T(8,128)(2,1)}, bf16[4,128,512]{2,1,0:T(8,128)(2,1)S(1)}, u32[]{:S(2)}, u32[]{:S(2)}) %collective-permute-start.7) | collective-permute-done | bytes 524320 | tf_op jit(solution)/shard_map/ppermute | solution.py:412
  103.1 4.0 %shard_map.132 = (f32[7,128,128]{2,1,0:T(8,128)S(1)}, f32[7,256,128]{2,1,0:T(8,128)S(1)}) custom-call(f32[8,128,128]{2,1,0:T(8,128)S(1)} %get-tuple-element.55.lead, f32[15,256,256]{2,1,0:T(8,128)S(1)} %copy-done.4, f32[15,256,128]{2,1,0:T(8,128)S(1)} %copy-done.10, f32[15,256,128]{2,1,0:T(8,128)S(1)} %copy-done.5, f32[15,128,128]{2,1,0:T(8,128)S(1)} %copy-done.12), custom_call_target="tpu_custom_call" | custom-call | flops 700000000 | bytes 9371648 | tf_op jit(solution)/shard_map/pallas_call | solution.py:50
  107.1 4.1 %shard_map.127 = (bf16[8,384,128]{2,1,0:T(8,128)(2,1)S(1)}, f32[8,128,128]{2,1,0:T(8,128)S(1)}) custom-call(s32[1]{0:T(128)} %bitcast.row_ref.refs_0_, bf16[16,128,512]{2,1,0:T(8,128)(2,1)S(1)} %copy-done.8, bf16[8,128,512]{2,1,0:T(8,128)(2,1)} %collective-permute-done.left, bf16[8,128,512]{2,1,0:T(8,128)(2,1)} %collective-permute-done.2.right, ...), custom_call_target="tpu_custom_call" | custom-call | flops 1610612736 | bytes 4194304 | tf_op jit(solution)/shard_map/pallas_call | solution.py:86
  114.2 2.0 %shard_map.139 = (f32[4,128,128]{2,1,0:T(8,128)S(1)}, f32[4,128,128]{2,1,0:T(8,128)S(1)}, f32[5,128,128]{2,1,0:T(8,128)S(1)}, f32[5,128,128]{2,1,0:T(8,128)S(1)}) custom-call(s32[5]{0:T(128)S(1)} %stack.53.left_ref, f32[128,2176]{1,0:T(8,128)} %collective-permute-done.16.got, f32[128,2176]{1,0:T(8,128)S(1)} %copy-done.17, ...), custom_call_target="tpu_custom_call" | custom-call | flops 100000000 | bytes 2555924 | tf_op jit(solution)/shard_map/pallas_call | solution.py:50
  118.6 2.7 %shard_map.141.base2 = f32[5,256,128]{2,1,0:T(8,128)S(1)} custom-call(f32[4,128,128]{2,1,0:T(8,128)S(1)} %get-tuple-element.86.lead2, f32[4,128,128]{2,1,0:T(8,128)S(1)} %get-tuple-element.87.late, f32[7,128,128]{2,1,0:T(8,128)S(1)} %get-tuple-element.77.early0, f32[3,128,128]{2,1,0:T(8,128)S(1)} %get-tuple-element.78.early1, f32[15,256,256]{2,1,0:T(8,128)S(1)} %copy-done.4, ...), custom_call_target="tpu_custom_call" | custom-call | flops 400000000 | bytes 9043968 | tf_op jit(solution)/shard_map/pallas_call | solution.py:50
  122.5 2.1 %collective-permute-start.18 = (f32[128,128]{1,0:T(8,128)S(1)}, f32[128,128]{1,0:T(8,128)S(1)}, u32[]{:S(2)}, u32[]{:S(2)}) collective-permute-start(f32[128,128]{1,0:T(8,128)S(1)} %convolution_add_fusion.8), channel_id=1, source_target_pairs={{0,8},{4,12},{8,0},{12,4},{16,24},{20,28},{24,16},{28,20},{32,40},... | collective-permute-start | bytes 196616 | tf_op jit(solution)/shard_map/ppermute | solution.py:511
  125.2 2.2 %collective-permute-done.18 = f32[128,128]{1,0:T(8,128)S(1)} collective-permute-done((f32[128,128]{1,0:T(8,128)S(1)}, f32[128,128]{1,0:T(8,128)S(1)}, u32[]{:S(2)}, u32[]{:S(2)}) %collective-permute-start.18) | collective-permute-done | bytes 65568 | tf_op jit(solution)/shard_map/ppermute | solution.py:511
  128.5 4.8 %collective-permute-done.19 = f32[128,128]{1,0:T(8,128)S(1)} collective-permute-done((f32[128,128]{1,0:T(8,128)S(1)}, f32[128,128]{1,0:T(8,128)S(1)}, u32[]{:S(2)}, u32[]{:S(2)}) %collective-permute-start.19) | collective-permute-done | bytes 65568 | tf_op jit(solution)/shard_map/ppermute | solution.py:511
  134.1 3.9 %collective-permute-done.20 = f32[128,128]{1,0:T(8,128)S(1)} collective-permute-done((f32[128,128]{1,0:T(8,128)S(1)}, f32[128,128]{1,0:T(8,128)S(1)}, u32[]{:S(2)}, u32[]{:S(2)}) %collective-permute-start.20) | collective-permute-done | bytes 65568 | tf_op jit(solution)/shard_map/ppermute | solution.py:511
  138.8 5.2 %collective-permute-done.21 = f32[128,128]{1,0:T(8,128)S(1)} collective-permute-done((f32[128,128]{1,0:T(8,128)S(1)}, f32[128,128]{1,0:T(8,128)S(1)}, u32[]{:S(2)}, u32[]{:S(2)}) %collective-permute-start.21) | collective-permute-done | bytes 65568 | tf_op jit(solution)/shard_map/ppermute | solution.py:511
  144.1 6.1 %leaf_result.1 = f32[8192,128]{1,0:T(8,128)} custom-call(s32[1]{0:T(128)} %bitcast.row_ref.refs_0_, f32[128,128]{1,0:T(8,128)S(1)} %convolution_add_fusion.top_ref, f32[16,128,128]{2,1,0:T(8,128)S(1)} %get-tuple-element.83.paths, f32[16,128,128]{2,1,0:T(8,128)S(1)} %shard_map.142.rest, bf16[16,512,128]{2,1,0:T(8,128)(2,1)S(1)} %copy-done.15, ...), custom_call_target="tpu_custom_call" | custom-call | tf_op jit(solution)/shard_map/leaf_result/pallas_call | solution.py:315
  (121 shorter events, 50.5 us)
Async XLA Ops:
  1.0 8.4 %collective-permute-start.12 = (f32[128,256]{1,0:T(8,128)S(1)}, f32[128,256]{1,0:T(8,128)S(1)}, u32[]{:S(2)}, u32[]{:S(2)}) collective-permute-start(f32[128,256]{1,0:T(8,128)S(1)} %get-tuple-element.106), channel_id=1, source_target_pairs={{64,0},{65,1},{66,2},{67,3}} | collective-permute-start | bytes 393224 | tf_op jit(solution)/shard_map/ppermute | solution.py:359
  6.4 32.7 %copy-start.13 = (f32[128,640]{1,0:T(8,128)}, f32[128,640]{1,0:T(8,128)S(1)}, u32[]{:S(2)}) copy-start(f32[128,640]{1,0:T(8,128)S(1)} %get-tuple-element.108.low_half) | copy-start | bytes 983044
  6.5 32.7 %copy-start.6 = (bf16[16,128,512]{2,1,0:T(8,128)(2,1)S(1)}, bf16[16,128,512]{2,1,0:T(8,128)(2,1)}, u32[]{:S(2)}) copy-start(bf16[16,128,512]{2,1,0:T(8,128)(2,1)} %own.5) | copy-start | bytes 6291460
  10.7 9.2 %collective-permute-start.13 = (f32[128,640]{1,0:T(8,128)}, f32[128,640]{1,0:T(8,128)S(1)}, u32[]{:S(2)}, u32[]{:S(2)}) collective-permute-start(f32[128,640]{1,0:T(8,128)} %get-tuple-element.59), channel_id=1, source_target_pairs={{0,32},{32,0},{64,96},{96,64},{1,33},{33,1},{65,97},{97,65},{2,34}... | collective-permute-start | bytes 983048 | tf_op jit(solution)/shard_map/ppermute | solution.py:359
  22.9 12.2 %collective-permute-start.14 = (f32[128,896]{1,0:T(8,128)}, f32[128,896]{1,0:T(8,128)}, u32[]{:S(2)}, u32[]{:S(2)}) collective-permute-start(f32[128,896]{1,0:T(8,128)} %get-tuple-element.61), channel_id=1, source_target_pairs={{0,16},{16,0},{32,48},{48,32},{64,80},{80,64},{96,112},{112,96},{1... | collective-permute-start | bytes 1376264 | tf_op jit(solution)/shard_map/ppermute | solution.py:359
  37.2 13.9 %collective-permute-start.15 = (f32[128,1536]{1,0:T(8,128)S(1)}, f32[128,1536]{1,0:T(8,128)S(1)}, u32[]{:S(2)}, u32[]{:S(2)}) collective-permute-start(f32[128,1536]{1,0:T(8,128)S(1)} %get-tuple-element.63), channel_id=1, source_target_pairs={{0,8},{8,0},{16,24},{24,16},{32,40},{40,32},{48,56},{56,48},{64,72... | collective-permute-start | bytes 2359304 | tf_op jit(solution)/shard_map/ppermute | solution.py:359
  40.3 35.4 %collective-permute-start.2 = (bf16[8,128,512]{2,1,0:T(8,128)(2,1)}, bf16[8,128,512]{2,1,0:T(8,128)(2,1)}, u32[]{:S(2)}, u32[]{:S(2)}) collective-permute-start(bf16[8,128,512]{2,1,0:T(8,128)(2,1)} %slice.105), channel_id=1, source_target_pairs={{0,3},{1,0},{2,1},{3,2},{4,7},{5,4},{6,5},{7,6},{8,11},{9,8},{10,9... | collective-permute-start | bytes 3145736 | tf_op jit(solution)/shard_map/ppermute | solution.py:407
  44.4 34.3 %collective-permute-start = (bf16[8,128,512]{2,1,0:T(8,128)(2,1)}, bf16[8,128,512]{2,1,0:T(8,128)(2,1)}, u32[]{:S(2)}, u32[]{:S(2)}) collective-permute-start(bf16[8,128,512]{2,1,0:T(8,128)(2,1)} %slice.105), channel_id=1, source_target_pairs={{0,1},{1,2},{2,3},{3,0},{4,5},{5,6},{6,7},{7,4},{8,9},{9,10},{10,1... | collective-permute-start | bytes 3145736 | tf_op jit(solution)/shard_map/ppermute | solution.py:405
  45.6 20.8 %collective-permute-start.9 = (bf16[4,128,512]{2,1,0:T(8,128)(2,1)}, bf16[4,128,512]{2,1,0:T(8,128)(2,1)}, u32[]{:S(2)}, u32[]{:S(2)}) collective-permute-start(bf16[4,128,512]{2,1,0:T(8,128)(2,1)} %get-tuple-element.97), channel_id=1, source_target_pairs={{0,1},{1,2},{2,3},{3,0},{4,5},{5,6},{6,7},{7,4},{8,9},{9,10},{10,1... | collective-permute-start | bytes 1572872 | tf_op jit(solution)/shard_map/ppermute | solution.py:405
  45.6 26.4 %collective-permute-start.6 = (bf16[4,128,512]{2,1,0:T(8,128)(2,1)}, bf16[4,128,512]{2,1,0:T(8,128)(2,1)}, u32[]{:S(2)}, u32[]{:S(2)}) collective-permute-start(bf16[4,128,512]{2,1,0:T(8,128)(2,1)} %get-tuple-element.97), channel_id=1, source_target_pairs={{0,3},{1,0},{2,1},{3,2},{4,7},{5,4},{6,5},{7,6},{8,11},{9,8},{10,9... | collective-permute-start | bytes 1572872 | tf_op jit(solution)/shard_map/ppermute | solution.py:407
  52.0 23.6 %collective-permute-start.4 = (bf16[4,128,512]{2,1,0:T(8,128)(2,1)}, bf16[4,128,512]{2,1,0:T(8,128)(2,1)}, u32[]{:S(2)}, u32[]{:S(2)}) collective-permute-start(bf16[4,128,512]{2,1,0:T(8,128)(2,1)} %get-tuple-element.98), channel_id=1, source_target_pairs={{0,1},{1,2},{2,3},{3,0},{4,5},{5,6},{6,7},{7,4},{8,9},{9,10},{10,1... | collective-permute-start | bytes 1572872 | tf_op jit(solution)/shard_map/ppermute | solution.py:405
  66.3 47.8 %collective-permute-start.16 = (f32[128,2176]{1,0:T(8,128)}, f32[128,2176]{1,0:T(8,128)}, u32[]{:S(2)}, u32[]{:S(2)}) collective-permute-start(f32[128,2176]{1,0:T(8,128)} %get-tuple-element.65), channel_id=1, source_target_pairs={{0,4},{4,0},{8,12},{12,8},{16,20},{20,16},{24,28},{28,24},{32,36},... | collective-permute-start | bytes 3342344 | tf_op jit(solution)/shard_map/ppermute | solution.py:359
  72.0 15.1 %collective-permute-start.8 = (bf16[4,128,512]{2,1,0:T(8,128)(2,1)}, bf16[4,128,512]{2,1,0:T(8,128)(2,1)S(1)}, u32[]{:S(2)}, u32[]{:S(2)}) collective-permute-start(bf16[4,128,512]{2,1,0:T(8,128)(2,1)} %get-tuple-element.98), channel_id=1, source_target_pairs={{0,3},{1,0},{2,1},{3,2},{4,7},{5,4},{6,5},{7,6},{8,11},{9,8},{10,9... | collective-permute-start | bytes 1572872 | tf_op jit(solution)/shard_map/ppermute | solution.py:407
  75.6 22.7 %collective-permute-start.7 = (bf16[4,128,512]{2,1,0:T(8,128)(2,1)}, bf16[4,128,512]{2,1,0:T(8,128)(2,1)S(1)}, u32[]{:S(2)}, u32[]{:S(2)}) collective-permute-start(bf16[4,128,512]{2,1,0:T(8,128)(2,1)} %collective-permute-done.6.right), channel_id=1, source_target_pairs={{0,3},{1,0},{2,1},{3,2},{4,7},{5,4},{6,5},{7,6},{8,11},{9,8},{10,9... | collective-permute-start | bytes 1572872 | tf_op jit(solution)/shard_map/ppermute | solution.py:412
  75.7 23.9 %collective-permute-start.5 = (bf16[4,128,512]{2,1,0:T(8,128)(2,1)}, bf16[4,128,512]{2,1,0:T(8,128)(2,1)S(1)}, u32[]{:S(2)}, u32[]{:S(2)}) collective-permute-start(bf16[4,128,512]{2,1,0:T(8,128)(2,1)} %collective-permute-done.4.left), channel_id=1, source_target_pairs={{0,1},{1,2},{2,3},{3,0},{4,5},{5,6},{6,7},{7,4},{8,9},{9,10},{10,1... | collective-permute-start | bytes 1572872 | tf_op jit(solution)/shard_map/ppermute | solution.py:412
  78.7 32.4 %collective-permute-start.11 = (bf16[2,128,512]{2,1,0:T(8,128)(2,1)S(1)}, bf16[2,128,512]{2,1,0:T(8,128)(2,1)S(1)}, u32[]{:S(2)}, u32[]{:S(2)}) collective-permute-start(bf16[2,128,512]{2,1,0:T(8,128)(2,1)S(1)} %get-tuple-element.99), channel_id=1, source_target_pairs={{0,3},{1,0},{2,1},{3,2},{4,7},{5,4},{6,5},{7,6},{8,11},{9,8},{10,9... | collective-permute-start | bytes 786440 | tf_op jit(solution)/shard_map/ppermute | solution.py:412
  87.1 24.1 %collective-permute-start.10 = (bf16[2,128,512]{2,1,0:T(8,128)(2,1)S(1)}, bf16[2,128,512]{2,1,0:T(8,128)(2,1)S(1)}, u32[]{:S(2)}, u32[]{:S(2)}) collective-permute-start(bf16[2,128,512]{2,1,0:T(8,128)(2,1)S(1)} %get-tuple-element.101), channel_id=1, source_target_pairs={{0,1},{1,2},{2,3},{3,0},{4,5},{5,6},{6,7},{7,4},{8,9},{9,10},{10,1... | collective-permute-start | bytes 786440 | tf_op jit(solution)/shard_map/ppermute | solution.py:412
  98.3 17.9 %collective-permute-start.3 = (bf16[2,128,512]{2,1,0:T(8,128)(2,1)S(1)}, bf16[2,128,512]{2,1,0:T(8,128)(2,1)S(1)}, u32[]{:S(2)}, u32[]{:S(2)}) collective-permute-start(bf16[2,128,512]{2,1,0:T(8,128)(2,1)S(1)} %get-tuple-element.100), channel_id=1, source_target_pairs={{0,3},{1,0},{2,1},{3,2},{4,7},{5,4},{6,5},{7,6},{8,11},{9,8},{10,9... | collective-permute-start | bytes 786440 | tf_op jit(solution)/shard_map/ppermute | solution.py:412
  99.5 16.7 %collective-permute-start.1 = (bf16[2,128,512]{2,1,0:T(8,128)(2,1)S(1)}, bf16[2,128,512]{2,1,0:T(8,128)(2,1)S(1)}, u32[]{:S(2)}, u32[]{:S(2)}) collective-permute-start(bf16[2,128,512]{2,1,0:T(8,128)(2,1)S(1)} %get-tuple-element.102), channel_id=1, source_target_pairs={{0,1},{1,2},{2,3},{3,0},{4,5},{5,6},{6,7},{7,4},{8,9},{9,10},{10,1... | collective-permute-start | bytes 786440 | tf_op jit(solution)/shard_map/ppermute | solution.py:412
  118.2 4.2 %collective-permute-start.17 = (f32[128,128]{1,0:T(8,128)S(1)}, f32[128,128]{1,0:T(8,128)S(1)}, u32[]{:S(2)}, u32[]{:S(2)}) collective-permute-start(f32[128,128]{1,0:T(8,128)S(1)} %get-tuple-element.79), channel_id=1, source_target_pairs={{0,4},{4,0},{8,12},{12,8},{16,20},{20,16},{24,28},{28,24},{32,36},... | collective-permute-start | bytes 196616 | tf_op jit(solution)/shard_map/ppermute | solution.py:511
  122.5 4.8 %collective-permute-start.18 = (f32[128,128]{1,0:T(8,128)S(1)}, f32[128,128]{1,0:T(8,128)S(1)}, u32[]{:S(2)}, u32[]{:S(2)}) collective-permute-start(f32[128,128]{1,0:T(8,128)S(1)} %convolution_add_fusion.8), channel_id=1, source_target_pairs={{0,8},{4,12},{8,0},{12,4},{16,24},{20,28},{24,16},{28,20},{32,40},... | collective-permute-start | bytes 196616 | tf_op jit(solution)/shard_map/ppermute | solution.py:511
  127.8 5.6 %collective-permute-start.19 = (f32[128,128]{1,0:T(8,128)S(1)}, f32[128,128]{1,0:T(8,128)S(1)}, u32[]{:S(2)}, u32[]{:S(2)}) collective-permute-start(f32[128,128]{1,0:T(8,128)S(1)} %convolution_add_fusion.5), channel_id=1, source_target_pairs={{0,24},{4,28},{8,16},{12,20},{16,8},{20,12},{24,0},{28,4},{32,56},... | collective-permute-start | bytes 196616 | tf_op jit(solution)/shard_map/ppermute | solution.py:511
  133.7 4.3 %collective-permute-start.20 = (f32[128,128]{1,0:T(8,128)S(1)}, f32[128,128]{1,0:T(8,128)S(1)}, u32[]{:S(2)}, u32[]{:S(2)}) collective-permute-start(f32[128,128]{1,0:T(8,128)S(1)} %convolution_add_fusion.3), channel_id=1, source_target_pairs={{0,32},{4,36},{8,40},{12,44},{16,48},{20,52},{24,56},{28,60},{32,0... | collective-permute-start | bytes 196616 | tf_op jit(solution)/shard_map/ppermute | solution.py:511
  138.4 5.6 %collective-permute-start.21 = (f32[128,128]{1,0:T(8,128)S(1)}, f32[128,128]{1,0:T(8,128)S(1)}, u32[]{:S(2)}, u32[]{:S(2)}) collective-permute-start(f32[128,128]{1,0:T(8,128)S(1)} %convolution_add_fusion.1), channel_id=1, source_target_pairs={{0,96},{4,100},{8,104},{12,108},{16,112},{20,116},{24,120},{28,124... | collective-permute-start | bytes 196616 | tf_op jit(solution)/shard_map/ppermute | solution.py:511
  (23 other events, 140.5 us)

commit v3 on v2

--- a/solution.py
+++ b/solution.py
@@ -11,10 +11,10 @@
 wide = jnp.float32
 narrow = jnp.bfloat16
 
-GROUPS = ((0, 8), (8, 4), (12, 4))
-PIECES = ((0, 4), (4, 4), (8, 8))
-MERGED = ((0, 1, 2, 3, 8, 9, 12), (4, 5, 10))
-LATE = (6, 7, 11, 13, 14)
+GROUPS = ((0, 8), (8, 8))
+PIECES = ((0, 4), (4, 4), (8, 4), (12, 4))
+MERGED = (0, 1, 2, 3, 8, 9, 12)
+LATE = (4, 5, 6, 7, 10, 11, 13, 14)
 FRONT = (((0,), (0,)), ((), ()))
 
 
@@ -28,13 +28,12 @@
 
 
 def split_dot(a, b, dims=(((1,), (0,)), ((), ()))):
-    a_high, a_low = parts_of(a)
-    b_high, b_low = parts_of(b)
-
-    def one(p, q):
-        return lax.dot_general(p, q, dims, preferred_element_type=wide)
-
-    return one(a_high, b_low) + one(a_low, b_high) + one(a_high, b_high)
+    rows_at = 1 - dims[0][0][0]
+    left = jnp.concatenate(parts_of(a), axis=rows_at)
+    right = jnp.concatenate(parts_of(b), axis=1)
+    full = lax.dot_general(left, right, dims, preferred_element_type=wide)
+    m, n = a.shape[rows_at], b.shape[1]
+    return (full[m:, n:] + full[m:, :n] + full[:m, n:]) + full[:m, :n]
 
 
 def close_dot(a, b):
@@ -64,13 +63,12 @@
     count, height, width = own.shape
     for k in range(count):
         rows = jnp.concatenate([own[k], left[k], right[k]], axis=0)
-        got = narrow_dot(rows, rhs[k * width : (k + 1) * width, :]).astype(narrow)
-        vals[k] = got
-        matching = jnp.concatenate(
-            [basis[k, pl.ds(turned(row_ref, part, height), height), :] for part in (0, 3, 1)],
-            axis=0,
-        )
-        proj[k] = lax.dot_general(matching, got, FRONT, preferred_element_type=wide)
+        got = narrow_dot(rows, rhs[k * width : (k + 1) * width, :])
+        vals[k] = got.astype(narrow)
+    at = [turned(row_ref, part, height) for part in (0, 3, 1)]
+    for k in range(count):
+        matching = jnp.concatenate([basis[k, pl.ds(a, height), :] for a in at], axis=0)
+        proj[k] = lax.dot_general(matching, vals[k], FRONT, preferred_element_type=wide)
 
 
 def near_call(piece, row, own, left, right, rhs, basis):
@@ -113,7 +111,9 @@
     )(row, own, left, right, rhs, basis)
 
 
-def far_leaves(group, row_ref, far_a, far_b, rhs, basis, coarse, parts, vals, proj, lead):
+def far_leaves(
+    group, row_ref, far_a, far_b, rhs, basis, coarse, part_a, part_b, vals, proj, lead
+):
     start, count = GROUPS[group]
     height, width = far_a.shape[1], far_a.shape[2]
     half = count // 2
@@ -121,30 +121,27 @@
     for k in range(count):
         leaf = start + k
         rows = far_a[k] if k < half else far_b[k - half]
-        got = narrow_dot(rows, rhs[leaf * width : (leaf + 1) * width, :]).astype(narrow)
-        vals[k] = got
-        before = parts[k // half][k % half] if group == 0 else parts[0][leaf - PIECES[2][0]]
-        total = before + lax.dot_general(
-            basis[leaf, pl.ds(at, height), :], got, FRONT, preferred_element_type=wide
+        got = narrow_dot(rows, rhs[leaf * width : (leaf + 1) * width, :])
+        vals[k] = got.astype(narrow)
+    for k in range(count):
+        before = part_a[k] if k < half else part_b[k - half]
+        proj[k] = before + lax.dot_general(
+            basis[start + k, pl.ds(at, height), :], vals[k], FRONT, preferred_element_type=wide
         )
-        proj[k] = total
-        lead[k] = split_dot(coarse[leaf], total)
-
-
-def far_body(group, refs):
-    inputs, outputs = refs[:6], refs[-3:]
-    far_leaves(group, *inputs, refs[6:-3], *outputs)
+    for k in range(count):
+        lead[k] = split_dot(coarse[start + k], proj[k])
 
 
 def last_body(
-    row_ref, far_a, far_b, rhs, basis, coarse, part, ups, early0, early1,
+    row_ref, far_a, far_b, rhs, basis, coarse, part_a, part_b, ups, early,
     vals, proj, lead, late, up,
 ):
-    far_leaves(2, row_ref, far_a, far_b, rhs, basis, coarse, (part,), vals, proj, lead)
-    value = {12 + k: (lead, k) for k in range(4)}
-    for early, nodes in zip((early0, early1), MERGED):
-        for k, node in enumerate(nodes):
-            value[16 + node] = (early, k)
+    far_leaves(
+        1, row_ref, far_a, far_b, rhs, basis, coarse, part_a, part_b, vals, proj, lead
+    )
+    value = {8 + k: (lead, k) for k in range(8)}
+    for k, node in enumerate(MERGED):
+        value[16 + node] = (early, k)
     for k, node in enumerate(LATE):
         pair = [value[c][0][value[c][1]] for c in (2 * node, 2 * node + 1)]
         got = split_dot(ups[k], jnp.concatenate(pair, axis=0))
@@ -163,15 +160,26 @@
     ]
 
 
-def merge_body(group, lead, inv, basis, back, coarse, early, base):
-    value = {GROUPS[group][0] + k: (lead, k) for k in range(lead.shape[0])}
-    for k, node in enumerate(MERGED[group]):
-        pair = [value[c][0][value[c][1]] for c in (2 * node, 2 * node + 1)]
-        solved = split_dot(inv[node], jnp.concatenate(pair, axis=0))
-        reduced = split_dot(basis[node], solved, FRONT)
-        early[k] = split_dot(coarse[node], reduced)
-        base[k] = solved - split_dot(back[node], reduced)
-        value[16 + node] = (early, k)
+def by_level(nodes):
+    for first, last in ((0, 8), (8, 12), (12, 14), (14, 15)):
+        level = [(k, node) for k, node in enumerate(nodes) if first <= node < last]
+        if level:
+            yield level
+
+
+def merge_body(lead, inv, basis, back, coarse, early, base):
+    value = {k: (lead, k) for k in range(lead.shape[0])}
+    for level in by_level(MERGED):
+        solved, reduced = {}, {}
+        for k, node in level:
+            pair = [value[c][0][value[c][1]] for c in (2 * node, 2 * node + 1)]
+            solved[k] = split_dot(inv[node], jnp.concatenate(pair, axis=0))
+        for k, node in level:
+            reduced[k] = split_dot(basis[node], solved[k], FRONT)
+        for k, node in level:
+            early[k] = split_dot(coarse[node], reduced[k])
+            base[k] = solved[k] - split_dot(back[node], reduced[k])
+            value[16 + node] = (early, k)
 
 
 def prepare_body(inv, basis, back, coarse, ups, paths):
@@ -188,27 +196,29 @@
                 paths[2 * node + k] = value[2 * node + k]
 
 
-def late_body(lead2, late, early0, early1, inv, basis, back, base):
-    value = {12 + k: (lead2, k) for k in range(4)}
-    for early, nodes in zip((early0, early1), MERGED):
-        for k, node in enumerate(nodes):
-            value[16 + node] = (early, k)
+def late_body(lead, late, early, inv, basis, back, base):
+    value = {8 + k: (lead, k) for k in range(8)}
+    for k, node in enumerate(MERGED):
+        value[16 + node] = (early, k)
     for k, node in enumerate(LATE[:-1]):
         value[16 + node] = (late, k)
+    reduced = {}
     for k, node in enumerate(LATE):
         pair = [value[c][0][value[c][1]] for c in (2 * node, 2 * node + 1)]
-        solved = split_dot(inv[node], jnp.concatenate(pair, axis=0))
-        reduced = split_dot(basis[node], solved, FRONT)
-        base[k] = solved - split_dot(back[node], reduced)
-
-
-def known_body(base0, base1, base2, back, proj0, proj1, proj2, rest):
+        base[k] = split_dot(inv[node], jnp.concatenate(pair, axis=0))
+    for k, node in enumerate(LATE):
+        reduced[k] = split_dot(basis[node], base[k], FRONT)
+    for k, node in enumerate(LATE):
+        base[k] -= split_dot(back[node], reduced[k])
+
+
+def known_body(base0, base1, back, proj0, proj1, rest):
     rank = proj0.shape[1]
     known = {}
-    for base, nodes in zip((base0, base1, base2), (*MERGED, LATE)):
+    for base, nodes in ((base0, MERGED), (base1, LATE)):
         for k, node in enumerate(nodes):
             known[node] = (base, k)
-    projs = [(proj, k) for proj in (proj0, proj1, proj2) for k in range(proj.shape[0])]
+    projs = [(proj, k) for proj in (proj0, proj1) for k in range(proj.shape[0])]
     part = {30: None}
     for node in reversed(range(15)):
         ref, at = known[node]
@@ -271,7 +281,7 @@
 
 
 def out_body(
-    row_ref, top_ref, paths, rest, back, near0, near1, near2, far0, far1, far2, out
+    row_ref, top_ref, paths, rest, back, near0, near1, near2, near3, far0, far1, out
 ):
     some, width = back.shape[0], back.shape[1]
     height = far0.shape[1]
@@ -289,8 +299,8 @@
         difference = (rest[k] - split_dot(paths[k], top)).astype(narrow)
         matching = jnp.concatenate([back[k, pl.ds(a, height), :] for a in at], axis=0)
         change = narrow_dot(matching, difference)
-        near = pick((near0, near1, near2), PIECES, k)
-        far = pick((far0, far1, far2), GROUPS, k)
+        near = pick((near0, near1, near2, near3), PIECES, k)
+        far = pick((far0, far1), GROUPS, k)
         for j, a in enumerate(at):
             block = far if j == 3 else near[j * height : (j + 1) * height]
             out[pl.ds(pl.multiple_of(k * width + a, height), height), :] = (
@@ -301,7 +311,7 @@
 def out_call(row, top, paths, rest, back, nears, fars):
     leaves, width, rank = back.shape
     height, columns = fars[0].shape[1:]
-    some = 2
+    some = 4
 
     def at(shape):
         return pl.BlockSpec(shape, lambda i, row: (i,) + (0,) * (len(shape) - 1))
@@ -398,16 +408,14 @@
     behind = [(i, (i - 1) % ring) for i in range(ring)]
     row = lax.axis_index("rhs").astype(jnp.int32).reshape(1)
 
-    own = [leaf_inv[start : start + count] for start, count in PIECES]
-    left, right = {}, {}
-    for k, forth_first in ((0, True), (1, False), (1, True), (0, False), (2, True), (2, False)):
-        if forth_first:
-            left[k] = lax.ppermute(own[k], "rhs", ahead)
-        else:
-            right[k] = lax.ppermute(own[k], "rhs", behind)
-    pairs = ((left[0], right[1]),) + tuple(
-        (left[2][s : s + 2], right[2][s + 2 : s + 4]) for s in (0, 4)
-    )
+    own, whole = [], leaf_inv
+    for start, count in PIECES:
+        own.append(whole[start : start + count])
+        if start == 0:
+            whole, own[0] = lax.optimization_barrier((whole, own[0]))
+    left = [lax.ppermute(a, "rhs", ahead) for a in own]
+    right = [lax.ppermute(a, "rhs", behind) for a in own]
+    pairs = ((left[0], right[1]), (left[2], right[3]))
     far = [
         (lax.ppermute(one, "rhs", ahead), lax.ppermute(two, "rhs", behind))
         for one, two in pairs
@@ -443,62 +451,50 @@
         nears.append(near)
         parts.append(part)
     shared = (rhs_cols, leaf_basis, leaf_coarse)
-    results, merged = [], []
-    for k in range(2):
-        count = GROUPS[k][1]
-        results.append(
-            kernel_call(
-                lambda *refs, k=k: far_body(k, refs),
-                far_shapes(count, height, rank, columns),
-                count * 4 * 10**7,
-                (row, *far[k], *shared, *(parts[:2] if k == 0 else parts[2:])),
-                scalars=1,
-            )
-        )
-        merged.append(
-            kernel_call(
-                functools.partial(merge_body, k),
-                [
-                    jax.ShapeDtypeStruct((len(MERGED[k]), rank, columns), wide),
-                    jax.ShapeDtypeStruct((len(MERGED[k]), 2 * rank, columns), wide),
-                ],
-                len(MERGED[k]) * 10**8,
-                (results[k][2], mid_inv, mid_basis, mid_back, mid_coarse),
-                room=12,
-            )
-        )
-    earlies = [m[0] for m in merged]
+    first = kernel_call(
+        functools.partial(far_leaves, 0),
+        far_shapes(GROUPS[0][1], height, rank, columns),
+        3 * 10**8,
+        (row, *far[0], *shared, *parts[:2]),
+        scalars=1,
+    )
+    early, early_base = kernel_call(
+        merge_body,
+        [
+            jax.ShapeDtypeStruct((len(MERGED), rank, columns), wide),
+            jax.ShapeDtypeStruct((len(MERGED), 2 * rank, columns), wide),
+        ],
+        len(MERGED) * 10**8,
+        (first[2], mid_inv, mid_basis, mid_back, mid_coarse),
+        room=12,
+    )
     final = lax.optimization_barrier(
-        (far[2], parts[2], ups, earlies, up_own, up_sib, down_own, down_sib, paths)
-    )
-    last_far, part, ups, earlies, up_own, up_sib, down_own, down_sib, paths = final
+        (far[1], parts[2:], ups, early, up_own, up_sib, down_own, down_sib, paths)
+    )
+    last_far, last_parts, ups, early, up_own, up_sib, down_own, down_sib, paths = final
     *last, late, current = kernel_call(
         last_body,
-        far_shapes(GROUPS[2][1], height, rank, columns)
+        far_shapes(GROUPS[1][1], height, rank, columns)
         + [
             jax.ShapeDtypeStruct((len(LATE) - 1, rank, columns), wide),
             jax.ShapeDtypeStruct((rank, columns), wide),
         ],
-        3 * 10**8,
-        (row, *last_far, *shared, part, ups, *earlies),
+        4 * 10**8,
+        (row, *last_far, *shared, *last_parts, ups, early),
         scalars=1,
     )
-    results.append(last)
-    bases = [m[1] for m in merged]
-    bases.append(
-        kernel_call(
-            late_body,
-            jax.ShapeDtypeStruct((len(LATE), 2 * rank, columns), wide),
-            4 * 10**8,
-            (last[2], late, *earlies, mid_inv, mid_basis, mid_back),
-            room=12,
-        )
+    late_base = kernel_call(
+        late_body,
+        jax.ShapeDtypeStruct((len(LATE), 2 * rank, columns), wide),
+        6 * 10**8,
+        (last[2], late, early, mid_inv, mid_basis, mid_back),
+        room=12,
     )
     rest = kernel_call(
         known_body,
         jax.ShapeDtypeStruct((leaf_count, rank, columns), wide),
         4 * 10**8,
-        (*bases, mid_back, *[r[1] for r in results]),
+        (early_base, late_base, mid_back, first[1], last[1]),
         room=12,
     )
 
@@ -515,7 +511,7 @@
         if level < depth - 1:
             before = close_dot(up_own[level], current)
             current = before + close_dot(up_sib[level], partner)
-    return out_call(row, top, paths, rest, leaf_back, nears, [r[0] for r in results])
+    return out_call(row, top, paths, rest, leaf_back, nears, (first[0], last[0]))
 
 
 def solution(mesh):

time: 151 us -> 137 us (0.907)
  waiting for transfers between devices: 59.5 us -> 48 us
  Pallas kernels: 39.2 us -> 33.8 us
  starting transfers between devices: 24.8 us -> 29.3 us
  local copies, waits for them, and re-layouts: 19.6 us -> 17.8 us
    ppermute x3 -> x2, waiting for transfers between devices: 8.7 us -> 0.01 us  [solve(): lax.ppermute(two, 'rhs', behind)]
    ppermute x6 -> x8, starting transfers between devices: 9.49 us -> 13.8 us  [the longest x4 12.6 us: solve(): right = [lax.ppermute(a, 'rhs', behind) for a in own]]
    ppermute x3 -> x2, starting transfers between devices: 2.66 us -> 5.77 us  [solve(): lax.ppermute(two, 'rhs', behind)]
    ppermute x3 -> x2, starting transfers between devices: 2.82 us -> 0.01 us  [solve(): lax.ppermute(one, 'rhs', ahead)]
    slice x4 -> x2, local copies, waits for them, and re-layouts: 4.38 us -> 2.03 us  [solve(): own.append(whole[start:start + count])]
    pallas_call x1, Pallas kernels: 6.09 us -> 3.79 us  [out_call(): pl.pallas_call(out_body, grid_spec=pltpu.PrefetchScalarGridSpec(num_scala...]
    ppermute x5, waiting for transfers between devices: 22.5 us -> 20.3 us  [top_factors(): got = lax.ppermute(message, 'leaf', pairs)]
    pallas_call x13 -> x11, Pallas kernels: 23.9 us -> 22.3 us  [kernel_call(): pl.pallas_call(body, out_shape=out_shape, cost_estimate=pl.CostEstimate(f...]
  transfers between devices with their start and end apart: 22 -> 22, of which waited for: 11 -> 11; matrix products, arithmetic and copies ran while one was open for 7% -> 6% of each run, Pallas kernels for 18% -> 17%
where the time goes in v3:
time: 137 us; the launch traced here: 136 us
  waiting for transfers between devices  48 us (35%)
  Pallas kernels  33.8 us (25%)
  starting transfers between devices  29.3 us (21%)
  local copies, waits for them, and re-layouts  17.8 us (13%)
  matrix products  6.17 us (5%)
    pallas_call x11, Pallas kernels, kernel_call(): pl.pallas_call(body, out_shape=out_shape, cost_estimate=pl.CostEstimate(f...  22.3 us
    ppermute x5, waiting for transfers between devices, top_factors(): got = lax.ppermute(message, 'leaf', pairs)  20.3 us
    ppermute x5, waiting for transfers between devices, solve(): partner = lax.ppermute(current, 'leaf', pairs)  16.2 us
    unnamed x54, local copies, waits for them, and re-layouts  13.7 us
    ppermute x4, starting transfers between devices, solve(): right = [lax.ppermute(a, 'rhs', behind) for a in own]  12.6 us
    pallas_call x4, Pallas kernels, near_call(): pl.pallas_call(near_body, grid_spec=pltpu.PrefetchScalarGridSpec(num_scal...  7.72 us
    ppermute x4, waiting for transfers between devices, solve(): right = [lax.ppermute(a, 'rhs', behind) for a in own]  7.28 us
    ppermute x5, starting transfers between devices, top_factors(): got = lax.ppermute(message, 'leaf', pairs)  7.02 us
  transfers between devices with their start and end apart: 22, of which 11 were waited for; matrix products, arithmetic and copies ran while one was open for 6% of the time, Pallas kernels for 17%

profile of v3, /device:TPU:0, one launch (start us, length us, event | category | flops | bytes accessed | tf_op | source)
XLA Modules:
  0.0 136.0 jit_solution(4353478657438386786)
XLA Ops:
  6.5 2.9 %collective-permute-done.12.got = f32[128,256]{1,0:T(8,128)S(1)} collective-permute-done((f32[128,256]{1,0:T(8,128)S(1)}, f32[128,256]{1,0:T(8,128)S(1)}, u32[]{:S(2)}, u32[]{:S(2)}) %collective-permute-start.12) | collective-permute-done | bytes 131104 | tf_op jit(solution)/shard_map/ppermute | solution.py:369
  12.7 7.2 %collective-permute-done.13.got = f32[128,640]{1,0:T(8,128)S(1)} collective-permute-done((f32[128,640]{1,0:T(8,128)}, f32[128,640]{1,0:T(8,128)S(1)}, u32[]{:S(2)}, u32[]{:S(2)}) %collective-permute-start.13) | collective-permute-done | bytes 327712 | tf_op jit(solution)/shard_map/ppermute | solution.py:369
  25.0 10.2 %collective-permute-done.14.got = f32[128,896]{1,0:T(8,128)} collective-permute-done((f32[128,896]{1,0:T(8,128)}, f32[128,896]{1,0:T(8,128)}, u32[]{:S(2)}, u32[]{:S(2)}) %collective-permute-start.14) | collective-permute-done | bytes 458784 | tf_op jit(solution)/shard_map/ppermute | solution.py:369
  40.8 4.1 %collective-permute-start.10 = (bf16[4,128,512]{2,1,0:T(8,128)(2,1)}, bf16[4,128,512]{2,1,0:T(8,128)(2,1)S(1)}, u32[]{:S(2)}, u32[]{:S(2)}) collective-permute-start(bf16[4,128,512]{2,1,0:T(8,128)(2,1)} %slice.96), channel_id=1, source_target_pairs={{0,3},{1,0},{2,1},{3,2},{4,7},{5,4},{6,5},{7,6},{8,11},{9,8},{10,9... | collective-permute-start | bytes 1572872 | tf_op jit(solution)/shard_map/ppermute | solution.py:417
  46.2 3.2 %collective-permute-start.8 = (bf16[4,128,512]{2,1,0:T(8,128)(2,1)}, bf16[4,128,512]{2,1,0:T(8,128)(2,1)}, u32[]{:S(2)}, u32[]{:S(2)}) collective-permute-start(bf16[4,128,512]{2,1,0:T(8,128)(2,1)} %get-tuple-element.95), channel_id=1, source_target_pairs={{0,3},{1,0},{2,1},{3,2},{4,7},{5,4},{6,5},{7,6},{8,11},{9,8},{10,9... | collective-permute-start | bytes 1572872 | tf_op jit(solution)/shard_map/ppermute | solution.py:417
  49.4 2.6 %collective-permute-done.10.right = bf16[4,128,512]{2,1,0:T(8,128)(2,1)S(1)} collective-permute-done((bf16[4,128,512]{2,1,0:T(8,128)(2,1)}, bf16[4,128,512]{2,1,0:T(8,128)(2,1)S(1)}, u32[]{:S(2)}, u32[]{:S(2)}) %collective-permute-start.10) | collective-permute-done | bytes 524320 | tf_op jit(solution)/shard_map/ppermute | solution.py:417
  52.3 4.1 %collective-permute-start.2 = (bf16[4,128,512]{2,1,0:T(8,128)(2,1)}, bf16[4,128,512]{2,1,0:T(8,128)(2,1)}, u32[]{:S(2)}, u32[]{:S(2)}) collective-permute-start(bf16[4,128,512]{2,1,0:T(8,128)(2,1)} %get-tuple-element.96), channel_id=1, source_target_pairs={{0,3},{1,0},{2,1},{3,2},{4,7},{5,4},{6,5},{7,6},{8,11},{9,8},{10,9... | collective-permute-start | bytes 1572872 | tf_op jit(solution)/shard_map/ppermute | solution.py:417
  57.6 2.4 %shard_map.137 = (f32[128,2176]{1,0:T(8,128)S(1)}, f32[128,2176]{1,0:T(8,128)}) custom-call(s32[2]{0:T(128)S(1)} %pad_add_fusion.flags, f32[128,1536]{1,0:T(8,128)} %collective-permute-done.15.got, f32[128,1536]{1,0:T(8,128)S(1)} %copy-done.16, f32[128,640]{1,0:T(8,128)S(1)} %get-tuple-element.103.low_half, f32[128,640]{1,0:T(8,128)S(1)} %get-tuple-element.102.high_half), custom_call_target="tpu_custom_call" | custom-call | flops 1000000 | bytes 2228232 | tf_op jit(solution)/shard_map/pallas_call | solution.py:49
  63.3 4.0 %collective-permute-done.5.left = bf16[4,128,512]{2,1,0:T(8,128)(2,1)S(1)} collective-permute-done((bf16[4,128,512]{2,1,0:T(8,128)(2,1)}, bf16[4,128,512]{2,1,0:T(8,128)(2,1)S(1)}, u32[]{:S(2)}, u32[]{:S(2)}) %collective-permute-start.5) | collective-permute-done | bytes 524320 | tf_op jit(solution)/shard_map/ppermute | solution.py:416
  68.2 3.2 %collective-permute-start.9 = (bf16[4,128,512]{2,1,0:T(8,128)(2,1)}, bf16[4,128,512]{2,1,0:T(8,128)(2,1)}, u32[]{:S(2)}, u32[]{:S(2)}) collective-permute-start(bf16[4,128,512]{2,1,0:T(8,128)(2,1)} %collective-permute-done.8.right), channel_id=1, source_target_pairs={{0,3},{1,0},{2,1},{3,2},{4,7},{5,4},{6,5},{7,6},{8,11},{9,8},{10,9... | collective-permute-start | bytes 1572872 | tf_op jit(solution)/shard_map/ppermute | solution.py:420
  71.4 4.7 %collective-permute-done.4.right = bf16[4,128,512]{2,1,0:T(8,128)(2,1)S(1)} collective-permute-done((bf16[4,128,512]{2,1,0:T(8,128)(2,1)S(1)}, bf16[4,128,512]{2,1,0:T(8,128)(2,1)S(1)}, u32[]{:S(2)}, u32[]{:S(2)}) %collective-permute-start.4) | collective-permute-done | bytes 524320 | tf_op jit(solution)/shard_map/ppermute | solution.py:417
  76.9 2.5 %collective-permute-start.3 = (bf16[4,128,512]{2,1,0:T(8,128)(2,1)}, bf16[4,128,512]{2,1,0:T(8,128)(2,1)S(1)}, u32[]{:S(2)}, u32[]{:S(2)}) collective-permute-start(bf16[4,128,512]{2,1,0:T(8,128)(2,1)} %collective-permute-done.2.right), channel_id=1, source_target_pairs={{0,3},{1,0},{2,1},{3,2},{4,7},{5,4},{6,5},{7,6},{8,11},{9,8},{10,9... | collective-permute-start | bytes 1572872 | tf_op jit(solution)/shard_map/ppermute | solution.py:420
  79.6 2.1 %copy-done.4 = f32[15,256,256]{2,1,0:T(8,128)S(1)} copy-done((f32[15,256,256]{2,1,0:T(8,128)S(1)}, f32[15,256,256]{2,1,0:T(8,128)}, u32[]{:S(2)}) %copy-start.4) | copy-done | bytes 3932184
  86.0 2.7 %shard_map.129 = (f32[8,128,256]{2,1,0:T(8,128)S(1)}, f32[16,128,128]{2,1,0:T(8,128)S(1)}) custom-call(f32[15,256,256]{2,1,0:T(8,128)S(1)} %copy-done.4, f32[15,256,128]{2,1,0:T(8,128)S(1)} %copy-done.8, f32[15,256,128]{2,1,0:T(8,128)S(1)} %copy-done.6, f32[15,128,128]{2,1,0:T(8,128)S(1)} %copy-done.11), custom_call_target="tpu_custom_call" | custom-call | flops 800000000 | bytes 8847360 | tf_op jit(solution)/shard_map/pallas_call | solution.py:49
  90.6 2.0 %shard_map.131 = (bf16[4,384,128]{2,1,0:T(8,128)(2,1)S(1)}, f32[4,128,128]{2,1,0:T(8,128)S(1)}) custom-call(s32[1]{0:T(128)} %bitcast.row_ref, bf16[16,128,512]{2,1,0:T(8,128)(2,1)S(1)} %copy-done.3, bf16[4,128,512]{2,1,0:T(8,128)(2,1)} %collective-permute-done.11.left, bf16[4,128,512]{2,1,0:T(8,128)(2,1)} %collective-permute-done.8.right, ...), custom_call_target="tpu_custom_call" | custom-call | flops 805306368 | bytes 2097152 | tf_op jit(solution)/shard_map/pallas_call | solution.py:84
  96.6 2.2 %shard_map.132 = (bf16[8,128,128]{2,1,0:T(8,128)(2,1)S(1)}, f32[8,128,128]{2,1,0:T(8,128)S(1)}, f32[8,128,128]{2,1,0:T(8,128)S(1)}) custom-call(s32[1]{0:T(128)} %bitcast.row_ref, bf16[4,128,512]{2,1,0:T(8,128)(2,1)} %collective-permute-done.7.far_a, bf16[4,128,512]{2,1,0:T(8,128)(2,1)} %collective-permute-done.9.far_b, bf16[8192,128]{1,0:T(8,128)(2,1)S(1)} %copy-done.1, ...), custom_call_target="tpu_custom_call" | custom-call | flops 300000000 | bytes 6815748 | tf_op jit(solution)/shard_map/pallas_call | solution.py:49
  99.7 2.4 %shard_map.133 = (f32[7,128,128]{2,1,0:T(8,128)S(1)}, f32[7,256,128]{2,1,0:T(8,128)S(1)}) custom-call(f32[8,128,128]{2,1,0:T(8,128)S(1)} %get-tuple-element.57.lead, f32[15,256,256]{2,1,0:T(8,128)S(1)} %copy-done.5, f32[15,256,128]{2,1,0:T(8,128)S(1)} %copy-done.9, f32[15,256,128]{2,1,0:T(8,128)S(1)} %copy-done.7, f32[15,128,128]{2,1,0:T(8,128)S(1)} %copy-done.11), custom_call_target="tpu_custom_call" | custom-call | flops 700000000 | bytes 9371648 | tf_op jit(solution)/shard_map/pallas_call | solution.py:49
  102.1 2.2 %shard_map.138 = (f32[4,128,128]{2,1,0:T(8,128)S(1)}, f32[4,128,128]{2,1,0:T(8,128)S(1)}, f32[5,128,128]{2,1,0:T(8,128)S(1)}, f32[5,128,128]{2,1,0:T(8,128)S(1)}) custom-call(s32[5]{0:T(128)S(1)} %stack.53.left_ref, f32[128,2176]{1,0:T(8,128)} %collective-permute-done.16.got, f32[128,2176]{1,0:T(8,128)S(1)} %copy-done.14, ...), custom_call_target="tpu_custom_call" | custom-call | flops 100000000 | bytes 2555924 | tf_op jit(solution)/shard_map/pallas_call | solution.py:49
  104.3 2.7 %shard_map.139 = (bf16[8,128,128]{2,1,0:T(8,128)(2,1)S(1)}, f32[8,128,128]{2,1,0:T(8,128)S(1)}, f32[8,128,128]{2,1,0:T(8,128)S(1)}, f32[7,128,128]{2,1,0:T(8,128)S(1)}, f32[128,128]{1,0:T(8,128)S(1)}) custom-call(s32[1]{0:T(128)} %bitcast.row_ref, bf16[4,128,512]{2,1,0:T(8,128)(2,1)} %collective-permute-done.1.far_a, ...), custom_call_target="tpu_custom_call" | custom-call | flops 400000000 | bytes 8323076 | tf_op jit(solution)/shard_map/pallas_call | solution.py:49
  113.2 2.2 %collective-permute-done.18 = f32[128,128]{1,0:T(8,128)S(1)} collective-permute-done((f32[128,128]{1,0:T(8,128)S(1)}, f32[128,128]{1,0:T(8,128)S(1)}, u32[]{:S(2)}, u32[]{:S(2)}) %collective-permute-start.18) | collective-permute-done | bytes 65568 | tf_op jit(solution)/shard_map/ppermute | solution.py:507
  116.5 4.8 %collective-permute-done.19 = f32[128,128]{1,0:T(8,128)S(1)} collective-permute-done((f32[128,128]{1,0:T(8,128)S(1)}, f32[128,128]{1,0:T(8,128)S(1)}, u32[]{:S(2)}, u32[]{:S(2)}) %collective-permute-start.19) | collective-permute-done | bytes 65568 | tf_op jit(solution)/shard_map/ppermute | solution.py:507
  122.2 3.9 %collective-permute-done.20 = f32[128,128]{1,0:T(8,128)S(1)} collective-permute-done((f32[128,128]{1,0:T(8,128)S(1)}, f32[128,128]{1,0:T(8,128)S(1)}, u32[]{:S(2)}, u32[]{:S(2)}) %collective-permute-start.20) | collective-permute-done | bytes 65568 | tf_op jit(solution)/shard_map/ppermute | solution.py:507
  126.7 5.3 %collective-permute-done.21 = f32[128,128]{1,0:T(8,128)S(1)} collective-permute-done((f32[128,128]{1,0:T(8,128)S(1)}, f32[128,128]{1,0:T(8,128)S(1)}, u32[]{:S(2)}, u32[]{:S(2)}) %collective-permute-start.21) | collective-permute-done | bytes 65568 | tf_op jit(solution)/shard_map/ppermute | solution.py:507
  132.2 3.8 %leaf_result.1 = f32[8192,128]{1,0:T(8,128)} custom-call(s32[1]{0:T(128)} %bitcast.row_ref, f32[128,128]{1,0:T(8,128)S(1)} %convolution_add_fusion.top_ref, f32[16,128,128]{2,1,0:T(8,128)S(1)} %get-tuple-element.83.paths, f32[16,128,128]{2,1,0:T(8,128)S(1)} %shard_map.141.rest, bf16[16,512,128]{2,1,0:T(8,128)(2,1)S(1)} %copy-done.12, ...), custom_call_target="tpu_custom_call" | custom-call | tf_op jit(solution)/shard_map/leaf_result/pallas_call | solution.py:325
  (122 shorter events, 47.8 us)
Async XLA Ops:
  1.0 8.4 %collective-permute-start.12 = (f32[128,256]{1,0:T(8,128)S(1)}, f32[128,256]{1,0:T(8,128)S(1)}, u32[]{:S(2)}, u32[]{:S(2)}) collective-permute-start(f32[128,256]{1,0:T(8,128)S(1)} %get-tuple-element.101), channel_id=1, source_target_pairs={{64,0},{65,1},{66,2},{67,3}} | collective-permute-start | bytes 393224 | tf_op jit(solution)/shard_map/ppermute | solution.py:369
  6.4 33.5 %copy-start.3 = (bf16[16,128,512]{2,1,0:T(8,128)(2,1)S(1)}, bf16[16,128,512]{2,1,0:T(8,128)(2,1)}, u32[]{:S(2)}) copy-start(bf16[16,128,512]{2,1,0:T(8,128)(2,1)} %own.7) | copy-start | bytes 6291460
  10.7 9.2 %collective-permute-start.13 = (f32[128,640]{1,0:T(8,128)}, f32[128,640]{1,0:T(8,128)S(1)}, u32[]{:S(2)}, u32[]{:S(2)}) collective-permute-start(f32[128,640]{1,0:T(8,128)} %get-tuple-element.59), channel_id=1, source_target_pairs={{0,32},{32,0},{64,96},{96,64},{1,33},{33,1},{65,97},{97,65},{2,34}... | collective-permute-start | bytes 983048 | tf_op jit(solution)/shard_map/ppermute | solution.py:369
  23.0 12.2 %collective-permute-start.14 = (f32[128,896]{1,0:T(8,128)}, f32[128,896]{1,0:T(8,128)}, u32[]{:S(2)}, u32[]{:S(2)}) collective-permute-start(f32[128,896]{1,0:T(8,128)} %get-tuple-element.61), channel_id=1, source_target_pairs={{0,16},{16,0},{32,48},{48,32},{64,80},{80,64},{96,112},{112,96},{1... | collective-permute-start | bytes 1376264 | tf_op jit(solution)/shard_map/ppermute | solution.py:369
  38.1 14.2 %collective-permute-start.15 = (f32[128,1536]{1,0:T(8,128)}, f32[128,1536]{1,0:T(8,128)}, u32[]{:S(2)}, u32[]{:S(2)}) collective-permute-start(f32[128,1536]{1,0:T(8,128)} %get-tuple-element.63), channel_id=1, source_target_pairs={{0,8},{8,0},{16,24},{24,16},{32,40},{40,32},{48,56},{56,48},{64,72... | collective-permute-start | bytes 2359304 | tf_op jit(solution)/shard_map/ppermute | solution.py:369
  40.8 11.2 %collective-permute-start.10 = (bf16[4,128,512]{2,1,0:T(8,128)(2,1)}, bf16[4,128,512]{2,1,0:T(8,128)(2,1)S(1)}, u32[]{:S(2)}, u32[]{:S(2)}) collective-permute-start(bf16[4,128,512]{2,1,0:T(8,128)(2,1)} %slice.96), channel_id=1, source_target_pairs={{0,3},{1,0},{2,1},{3,2},{4,7},{5,4},{6,5},{7,6},{8,11},{9,8},{10,9... | collective-permute-start | bytes 1572872 | tf_op jit(solution)/shard_map/ppermute | solution.py:417
  45.0 16.1 %collective-permute-start.6 = (bf16[4,128,512]{2,1,0:T(8,128)(2,1)}, bf16[4,128,512]{2,1,0:T(8,128)(2,1)}, u32[]{:S(2)}, u32[]{:S(2)}) collective-permute-start(bf16[4,128,512]{2,1,0:T(8,128)(2,1)} %slice.96), channel_id=1, source_target_pairs={{0,1},{1,2},{2,3},{3,0},{4,5},{5,6},{6,7},{7,4},{8,9},{9,10},{10,1... | collective-permute-start | bytes 1572872 | tf_op jit(solution)/shard_map/ppermute | solution.py:416
  46.2 15.1 %collective-permute-start.11 = (bf16[4,128,512]{2,1,0:T(8,128)(2,1)}, bf16[4,128,512]{2,1,0:T(8,128)(2,1)}, u32[]{:S(2)}, u32[]{:S(2)}) collective-permute-start(bf16[4,128,512]{2,1,0:T(8,128)(2,1)} %get-tuple-element.95), channel_id=1, source_target_pairs={{0,1},{1,2},{2,3},{3,0},{4,5},{5,6},{6,7},{7,4},{8,9},{9,10},{10,1... | collective-permute-start | bytes 1572872 | tf_op jit(solution)/shard_map/ppermute | solution.py:416
  46.2 16.2 %collective-permute-start.8 = (bf16[4,128,512]{2,1,0:T(8,128)(2,1)}, bf16[4,128,512]{2,1,0:T(8,128)(2,1)}, u32[]{:S(2)}, u32[]{:S(2)}) collective-permute-start(bf16[4,128,512]{2,1,0:T(8,128)(2,1)} %get-tuple-element.95), channel_id=1, source_target_pairs={{0,3},{1,0},{2,1},{3,2},{4,7},{5,4},{6,5},{7,6},{8,11},{9,8},{10,9... | collective-permute-start | bytes 1572872 | tf_op jit(solution)/shard_map/ppermute | solution.py:417
  52.0 15.3 %collective-permute-start.5 = (bf16[4,128,512]{2,1,0:T(8,128)(2,1)}, bf16[4,128,512]{2,1,0:T(8,128)(2,1)S(1)}, u32[]{:S(2)}, u32[]{:S(2)}) collective-permute-start(bf16[4,128,512]{2,1,0:T(8,128)(2,1)} %get-tuple-element.96), channel_id=1, source_target_pairs={{0,1},{1,2},{2,3},{3,0},{4,5},{5,6},{6,7},{7,4},{8,9},{9,10},{10,1... | collective-permute-start | bytes 1572872 | tf_op jit(solution)/shard_map/ppermute | solution.py:416
  52.3 15.9 %collective-permute-start.2 = (bf16[4,128,512]{2,1,0:T(8,128)(2,1)}, bf16[4,128,512]{2,1,0:T(8,128)(2,1)}, u32[]{:S(2)}, u32[]{:S(2)}) collective-permute-start(bf16[4,128,512]{2,1,0:T(8,128)(2,1)} %get-tuple-element.96), channel_id=1, source_target_pairs={{0,3},{1,0},{2,1},{3,2},{4,7},{5,4},{6,5},{7,6},{8,11},{9,8},{10,9... | collective-permute-start | bytes 1572872 | tf_op jit(solution)/shard_map/ppermute | solution.py:417
  61.1 41.0 %collective-permute-start.16 = (f32[128,2176]{1,0:T(8,128)}, f32[128,2176]{1,0:T(8,128)}, u32[]{:S(2)}, u32[]{:S(2)}) collective-permute-start(f32[128,2176]{1,0:T(8,128)} %get-tuple-element.65), channel_id=1, source_target_pairs={{0,4},{4,0},{8,12},{12,8},{16,20},{20,16},{24,28},{28,24},{32,36},... | collective-permute-start | bytes 3342344 | tf_op jit(solution)/shard_map/ppermute | solution.py:369
  61.3 14.8 %collective-permute-start.4 = (bf16[4,128,512]{2,1,0:T(8,128)(2,1)S(1)}, bf16[4,128,512]{2,1,0:T(8,128)(2,1)S(1)}, u32[]{:S(2)}, u32[]{:S(2)}) collective-permute-start(bf16[4,128,512]{2,1,0:T(8,128)(2,1)S(1)} %copy-done.25), channel_id=1, source_target_pairs={{0,3},{1,0},{2,1},{3,2},{4,7},{5,4},{6,5},{7,6},{8,11},{9,8},{10,9... | collective-permute-start | bytes 1572872 | tf_op jit(solution)/shard_map/ppermute | solution.py:417
  62.4 17.1 %collective-permute-start = (bf16[4,128,512]{2,1,0:T(8,128)(2,1)S(1)}, bf16[4,128,512]{2,1,0:T(8,128)(2,1)}, u32[]{:S(2)}, u32[]{:S(2)}) collective-permute-start(bf16[4,128,512]{2,1,0:T(8,128)(2,1)S(1)} %copy-done.25), channel_id=1, source_target_pairs={{0,1},{1,2},{2,3},{3,0},{4,5},{5,6},{6,7},{7,4},{8,9},{9,10},{10,1... | collective-permute-start | bytes 1572872 | tf_op jit(solution)/shard_map/ppermute | solution.py:416
  68.2 28.4 %collective-permute-start.7 = (bf16[4,128,512]{2,1,0:T(8,128)(2,1)}, bf16[4,128,512]{2,1,0:T(8,128)(2,1)}, u32[]{:S(2)}, u32[]{:S(2)}) collective-permute-start(bf16[4,128,512]{2,1,0:T(8,128)(2,1)} %collective-permute-done.6.left), channel_id=1, source_target_pairs={{0,1},{1,2},{2,3},{3,0},{4,5},{5,6},{6,7},{7,4},{8,9},{9,10},{10,1... | collective-permute-start | bytes 1572872 | tf_op jit(solution)/shard_map/ppermute | solution.py:420
  68.2 28.4 %collective-permute-start.9 = (bf16[4,128,512]{2,1,0:T(8,128)(2,1)}, bf16[4,128,512]{2,1,0:T(8,128)(2,1)}, u32[]{:S(2)}, u32[]{:S(2)}) collective-permute-start(bf16[4,128,512]{2,1,0:T(8,128)(2,1)} %collective-permute-done.8.right), channel_id=1, source_target_pairs={{0,3},{1,0},{2,1},{3,2},{4,7},{5,4},{6,5},{7,6},{8,11},{9,8},{10,9... | collective-permute-start | bytes 1572872 | tf_op jit(solution)/shard_map/ppermute | solution.py:420
  76.9 27.3 %collective-permute-start.3 = (bf16[4,128,512]{2,1,0:T(8,128)(2,1)}, bf16[4,128,512]{2,1,0:T(8,128)(2,1)S(1)}, u32[]{:S(2)}, u32[]{:S(2)}) collective-permute-start(bf16[4,128,512]{2,1,0:T(8,128)(2,1)} %collective-permute-done.2.right), channel_id=1, source_target_pairs={{0,3},{1,0},{2,1},{3,2},{4,7},{5,4},{6,5},{7,6},{8,11},{9,8},{10,9... | collective-permute-start | bytes 1572872 | tf_op jit(solution)/shard_map/ppermute | solution.py:420
  79.5 24.8 %collective-permute-start.1 = (bf16[4,128,512]{2,1,0:T(8,128)(2,1)}, bf16[4,128,512]{2,1,0:T(8,128)(2,1)}, u32[]{:S(2)}, u32[]{:S(2)}) collective-permute-start(bf16[4,128,512]{2,1,0:T(8,128)(2,1)} %collective-permute-done.left), channel_id=1, source_target_pairs={{0,1},{1,2},{2,3},{3,0},{4,5},{5,6},{6,7},{7,4},{8,9},{9,10},{10,1... | collective-permute-start | bytes 1572872 | tf_op jit(solution)/shard_map/ppermute | solution.py:420
  107.0 3.6 %collective-permute-start.17 = (f32[128,128]{1,0:T(8,128)S(1)}, f32[128,128]{1,0:T(8,128)S(1)}, u32[]{:S(2)}, u32[]{:S(2)}) collective-permute-start(f32[128,128]{1,0:T(8,128)S(1)} %get-tuple-element.79), channel_id=1, source_target_pairs={{0,4},{4,0},{8,12},{12,8},{16,20},{20,16},{24,28},{28,24},{32,36},... | collective-permute-start | bytes 196616 | tf_op jit(solution)/shard_map/ppermute | solution.py:507
  110.6 21.5 %copy-start.12 = (bf16[16,512,128]{2,1,0:T(8,128)(2,1)S(1)}, bf16[16,512,128]{2,1,0:T(8,128)(2,1)}, u32[]{:S(2)}) copy-start(bf16[16,512,128]{2,1,0:T(8,128)(2,1)} %back.9) | copy-start | bytes 6291460
  110.8 4.6 %collective-permute-start.18 = (f32[128,128]{1,0:T(8,128)S(1)}, f32[128,128]{1,0:T(8,128)S(1)}, u32[]{:S(2)}, u32[]{:S(2)}) collective-permute-start(f32[128,128]{1,0:T(8,128)S(1)} %convolution_add_fusion.8), channel_id=1, source_target_pairs={{0,8},{4,12},{8,0},{12,4},{16,24},{20,28},{24,16},{28,20},{32,40},... | collective-permute-start | bytes 196616 | tf_op jit(solution)/shard_map/ppermute | solution.py:507
  115.8 5.6 %collective-permute-start.19 = (f32[128,128]{1,0:T(8,128)S(1)}, f32[128,128]{1,0:T(8,128)S(1)}, u32[]{:S(2)}, u32[]{:S(2)}) collective-permute-start(f32[128,128]{1,0:T(8,128)S(1)} %convolution_add_fusion.5), channel_id=1, source_target_pairs={{0,24},{4,28},{8,16},{12,20},{16,8},{20,12},{24,0},{28,4},{32,56},... | collective-permute-start | bytes 196616 | tf_op jit(solution)/shard_map/ppermute | solution.py:507
  121.7 4.3 %collective-permute-start.20 = (f32[128,128]{1,0:T(8,128)S(1)}, f32[128,128]{1,0:T(8,128)S(1)}, u32[]{:S(2)}, u32[]{:S(2)}) collective-permute-start(f32[128,128]{1,0:T(8,128)S(1)} %convolution_add_fusion.3), channel_id=1, source_target_pairs={{0,32},{4,36},{8,40},{12,44},{16,48},{20,52},{24,56},{28,60},{32,0... | collective-permute-start | bytes 196616 | tf_op jit(solution)/shard_map/ppermute | solution.py:507
  126.4 5.6 %collective-permute-start.21 = (f32[128,128]{1,0:T(8,128)S(1)}, f32[128,128]{1,0:T(8,128)S(1)}, u32[]{:S(2)}, u32[]{:S(2)}) collective-permute-start(f32[128,128]{1,0:T(8,128)S(1)} %convolution_add_fusion.1), channel_id=1, source_target_pairs={{0,96},{4,100},{8,104},{12,108},{16,112},{20,116},{24,120},{28,124... | collective-permute-start | bytes 196616 | tf_op jit(solution)/shard_map/ppermute | solution.py:507
  (25 other events, 70.7 us)

commit v4 on v3

--- a/solution.py
+++ b/solution.py
@@ -233,8 +233,8 @@
                 rest[2 * node + k] = ref[at] - below
 
 
-def spread_body(size, flags, got, upper, low_half, high_half, wider, message):
-    high, next_high = flags[0] == 1, flags[1] == 1
+def spread_body(size, bit, spot, got, upper, low_half, high_half, wider, message):
+    high, next_high = (lax.rem(spot[1] >> b, 2) == 1 for b in (bit, bit - 1))
     mine = low_half.shape[1]
     if size:
         wider[:, :size] = jnp.where(high, got[:, :size], upper[...])
@@ -250,18 +250,18 @@
         message[:, mine:] = wider[:, mine:]
 
 
-def top_body(left_ref, got, upper, high_half, up_own, up_sib, down_own, down_sib, packs):
+def top_body(spot, got, upper, high_half, up_own, up_sib, down_own, down_sib, packs):
     depth = down_own.shape[0]
     rank = packs.shape[0]
     size = upper.shape[1]
-    high = left_ref[0] == 0
+    high = lax.rem(spot[1], 2) == 1
     packs[:, :size] = jnp.where(high, got[:, :size], upper[...])
     packs[:, size:] = jnp.where(high, high_half[...], got[:, : high_half.shape[1]])
     path = None
     for level in range(depth):
         root = level == depth - 1
         first = 0 if root else 2 * rank + (depth - 2 - level) * 5 * rank
-        is_left = left_ref[level] == 1
+        is_left = lax.rem(spot[1] >> level, 2) == 0
 
         def both(matrix):
             one, two = matrix[:, :rank], matrix[:, rank:]
@@ -347,7 +347,7 @@
     return jnp.einsum(eq, a, b, precision=lax.Precision.HIGHEST)
 
 
-def top_factors(inv, basis, back, coarse, position, depth):
+def top_factors(inv, basis, back, coarse, spot, depth):
     total = lax.axis_size("leaf")
     rank = basis.shape[1]
     reduce_mat = exact("ik,ij->kj", basis, inv)
@@ -357,7 +357,6 @@
         jnp.concatenate([up_mat, down_mat[s : s + rank], back[s : s + rank]], axis=1)
         for s in (0, rank)
     ]
-    high = [((position >> bit) % 2).astype(jnp.int32) for bit in range(depth)]
     mine = halves[0].shape[1]
     upper, message, size = inv[rank:], inv[:rank], 0
     for bit in reversed(range(depth)):
@@ -371,13 +370,13 @@
             return got, upper, halves[1]
         held = size + mine if size else 2 * rank
         upper, message = kernel_call(
-            functools.partial(spread_body, size),
+            functools.partial(spread_body, size, bit),
             [
                 jax.ShapeDtypeStruct((rank, held), wide),
                 jax.ShapeDtypeStruct((rank, max(held, mine)), wide),
             ],
             10**6,
-            (jnp.stack([high[bit], high[bit - 1]]), got, upper, *halves),
+            (spot, got, upper, *halves),
             scalars=1,
         )
         size = held
@@ -406,13 +405,13 @@
     ring = lax.axis_size("rhs")
     ahead = [(i, (i + 1) % ring) for i in range(ring)]
     behind = [(i, (i - 1) % ring) for i in range(ring)]
-    row = lax.axis_index("rhs").astype(jnp.int32).reshape(1)
+    row = jnp.stack([lax.axis_index("rhs"), position]).astype(jnp.int32)
 
     own, whole = [], leaf_inv
     for start, count in PIECES:
         own.append(whole[start : start + count])
         if start == 0:
-            whole, own[0] = lax.optimization_barrier((whole, own[0]))
+            whole, own[0], row = lax.optimization_barrier((whole, own[0], row))
     left = [lax.ppermute(a, "rhs", ahead) for a in own]
     right = [lax.ppermute(a, "rhs", behind) for a in own]
     pairs = ((left[0], right[1]), (left[2], right[3]))
@@ -422,15 +421,14 @@
     ]
 
     got, upper, own_half = top_factors(
-        top_inv[0], top_basis[0], top_back[0], top_coarse[0], position, depth
-    )
-    sides = jnp.stack([1 - (position >> k) % 2 for k in range(depth)]).astype(jnp.int32)
+        top_inv[0], top_basis[0], top_back[0], top_coarse[0], row, depth
+    )
     square = (rank, rank)
     up_own, up_sib, down_own, down_sib = kernel_call(
         top_body,
         [jax.ShapeDtypeStruct((n, *square), wide) for n in (depth - 1, depth - 1, depth, depth)],
         10**8,
-        (sides, got, upper, own_half),
+        (row, got, upper, own_half),
         scalars=1,
         scratch_shapes=[pltpu.VMEM((rank, upper.shape[1] + own_half.shape[1]), wide)],
     )

time: 137 us -> 126 us (0.920)
  local copies, waits for them, and re-layouts: 17.8 us -> 2.3 us
  waiting for transfers between devices: 48 us -> 60 us
  Pallas kernels: 33.8 us -> 25.6 us
  starting transfers between devices: 29.3 us -> 31.4 us
    unnamed x54 -> x22, local copies, waits for them, and re-layouts: 13.7 us -> 0.05 us
    ppermute x4, waiting for transfers between devices: 4.2 us -> 11.2 us  [solve(): left = [lax.ppermute(a, 'rhs', ahead) for a in own]]
    pallas_call x11, Pallas kernels: 22.3 us -> 15.9 us  [kernel_call(): pl.pallas_call(body, out_shape=out_shape, cost_estimate=pl.CostEstimate(f...]
    ppermute x2, waiting for transfers between devices: 0.01 us -> 3.6 us  [solve(): lax.ppermute(one, 'rhs', ahead)]
    pallas_call x4, Pallas kernels: 7.72 us -> 5.32 us  [near_call(): pl.pallas_call(near_body, grid_spec=pltpu.PrefetchScalarGridSpec(num_scal...]
    slice x2, local copies, waits for them, and re-layouts: 2.03 us -> 0.21 us  [solve(): own.append(whole[start:start + count])]
  transfers between devices with their start and end apart: 22 -> 22, of which waited for: 11 -> 14; matrix products, arithmetic and copies ran while one was open for 6% -> 5% of each run, Pallas kernels for 17% -> 14%
where the time goes in v4:
time: 126 us
  waiting for transfers between devices  60 us (48%)
  starting transfers between devices  31.4 us (25%)
  Pallas kernels  25.6 us (20%)
  matrix products  6.16 us (5%)
  local copies, waits for them, and re-layouts  2.3 us (2%)
    ppermute x5, waiting for transfers between devices, top_factors(): got = lax.ppermute(message, 'leaf', pairs)  20.6 us
    ppermute x5, waiting for transfers between devices, solve(): partner = lax.ppermute(current, 'leaf', pairs)  16.2 us
    pallas_call x11, Pallas kernels, kernel_call(): pl.pallas_call(body, out_shape=out_shape, cost_estimate=pl.CostEstimate(f...  15.9 us
    ppermute x4, starting transfers between devices, solve(): right = [lax.ppermute(a, 'rhs', behind) for a in own]  11.7 us
    ppermute x4, waiting for transfers between devices, solve(): left = [lax.ppermute(a, 'rhs', ahead) for a in own]  11.2 us
    ppermute x4, waiting for transfers between devices, solve(): right = [lax.ppermute(a, 'rhs', behind) for a in own]  8.46 us
    ppermute x5, starting transfers between devices, top_factors(): got = lax.ppermute(message, 'leaf', pairs)  7.4 us
    ppermute x2, starting transfers between devices, solve(): lax.ppermute(two, 'rhs', behind)  6.93 us
  transfers between devices with their start and end apart: 22, of which 14 were waited for; matrix products, arithmetic and copies ran while one was open for 5% of the time, Pallas kernels for 14%

profile of v4, /device:TPU:0, one launch (start us, length us, event | category | flops | bytes accessed | tf_op | source)
XLA Modules:
  0.0 126.2 jit_solution(5631522753245903839)
XLA Ops:
  6.6 2.9 %collective-permute-done.12.got = f32[128,256]{1,0:T(8,128)S(1)} collective-permute-done((f32[128,256]{1,0:T(8,128)S(1)}, f32[128,256]{1,0:T(8,128)S(1)}, u32[]{:S(2)}, u32[]{:S(2)}) %collective-permute-start.12) | collective-permute-done | bytes 131104 | tf_op jit(solution)/shard_map/ppermute | solution.py:368
  12.0 7.0 %collective-permute-done.13.got = f32[128,640]{1,0:T(8,128)S(1)} collective-permute-done((f32[128,640]{1,0:T(8,128)S(1)}, f32[128,640]{1,0:T(8,128)S(1)}, u32[]{:S(2)}, u32[]{:S(2)}) %collective-permute-start.13) | collective-permute-done | bytes 327712 | tf_op jit(solution)/shard_map/ppermute | solution.py:368
  21.6 9.9 %collective-permute-done.14.got = f32[128,896]{1,0:T(8,128)S(1)} collective-permute-done((f32[128,896]{1,0:T(8,128)S(1)}, f32[128,896]{1,0:T(8,128)S(1)}, u32[]{:S(2)}, u32[]{:S(2)}) %collective-permute-start.14) | collective-permute-done | bytes 458784 | tf_op jit(solution)/shard_map/ppermute | solution.py:368
  32.3 2.2 %collective-permute-start.15 = (f32[128,1536]{1,0:T(8,128)S(1)}, f32[128,1536]{1,0:T(8,128)S(1)}, u32[]{:S(2)}, u32[]{:S(2)}) collective-permute-start(f32[128,1536]{1,0:T(8,128)S(1)} %get-tuple-element.65), channel_id=1, source_target_pairs={{0,8},{8,0},{16,24},{24,16},{32,40},{40,32},{48,56},{56,48},{64,72... | collective-permute-start | bytes 2359304 | tf_op jit(solution)/shard_map/ppermute | solution.py:368
  34.5 4.2 %collective-permute-start.10 = (bf16[4,128,512]{2,1,0:T(8,128)(2,1)S(1)}, bf16[4,128,512]{2,1,0:T(8,128)(2,1)S(1)}, u32[]{:S(2)}, u32[]{:S(2)}) collective-permute-start(bf16[4,128,512]{2,1,0:T(8,128)(2,1)S(1)} %slice.96), channel_id=1, source_target_pairs={{0,3},{1,0},{2,1},{3,2},{4,7},{5,4},{6,5},{7,6},{8,11},{9,8},{10,9... | collective-permute-start | bytes 1572872 | tf_op jit(solution)/shard_map/ppermute | solution.py:416
  39.0 3.3 %collective-permute-start.8 = (bf16[4,128,512]{2,1,0:T(8,128)(2,1)S(1)}, bf16[4,128,512]{2,1,0:T(8,128)(2,1)S(1)}, u32[]{:S(2)}, u32[]{:S(2)}) collective-permute-start(bf16[4,128,512]{2,1,0:T(8,128)(2,1)S(1)} %get-tuple-element.97), channel_id=1, source_target_pairs={{0,3},{1,0},{2,1},{3,2},{4,7},{5,4},{6,5},{7,6},{8,11},{9,8},{10,9... | collective-permute-start | bytes 1572872 | tf_op jit(solution)/shard_map/ppermute | solution.py:416
  42.3 3.1 %collective-permute-done.10.right = bf16[4,128,512]{2,1,0:T(8,128)(2,1)S(1)} collective-permute-done((bf16[4,128,512]{2,1,0:T(8,128)(2,1)S(1)}, bf16[4,128,512]{2,1,0:T(8,128)(2,1)S(1)}, u32[]{:S(2)}, u32[]{:S(2)}) %collective-permute-start.10) | collective-permute-done | bytes 524320 | tf_op jit(solution)/shard_map/ppermute | solution.py:416
  46.4 4.2 %collective-permute-start.2 = (bf16[4,128,512]{2,1,0:T(8,128)(2,1)S(1)}, bf16[4,128,512]{2,1,0:T(8,128)(2,1)S(1)}, u32[]{:S(2)}, u32[]{:S(2)}) collective-permute-start(bf16[4,128,512]{2,1,0:T(8,128)(2,1)S(1)} %get-tuple-element.98), channel_id=1, source_target_pairs={{0,3},{1,0},{2,1},{3,2},{4,7},{5,4},{6,5},{7,6},{8,11},{9,8},{10,9... | collective-permute-start | bytes 1572872 | tf_op jit(solution)/shard_map/ppermute | solution.py:416
  51.4 3.3 %collective-permute-done.11.left = bf16[4,128,512]{2,1,0:T(8,128)(2,1)S(1)} collective-permute-done((bf16[4,128,512]{2,1,0:T(8,128)(2,1)S(1)}, bf16[4,128,512]{2,1,0:T(8,128)(2,1)S(1)}, u32[]{:S(2)}, u32[]{:S(2)}) %collective-permute-start.11) | collective-permute-done | bytes 524320 | tf_op jit(solution)/shard_map/ppermute | solution.py:415
  54.7 2.0 %collective-permute-start = (bf16[4,128,512]{2,1,0:T(8,128)(2,1)S(1)}, bf16[4,128,512]{2,1,0:T(8,128)(2,1)S(1)}, u32[]{:S(2)}, u32[]{:S(2)}) collective-permute-start(bf16[4,128,512]{2,1,0:T(8,128)(2,1)S(1)} %get-tuple-element.99), channel_id=1, source_target_pairs={{0,1},{1,2},{2,3},{3,0},{4,5},{5,6},{6,7},{7,4},{8,9},{9,10},{10,1... | collective-permute-start | bytes 1572872 | tf_op jit(solution)/shard_map/ppermute | solution.py:415
  56.7 7.9 %collective-permute-done.5.left = bf16[4,128,512]{2,1,0:T(8,128)(2,1)S(1)} collective-permute-done((bf16[4,128,512]{2,1,0:T(8,128)(2,1)S(1)}, bf16[4,128,512]{2,1,0:T(8,128)(2,1)S(1)}, u32[]{:S(2)}, u32[]{:S(2)}) %collective-permute-start.5) | collective-permute-done | bytes 524320 | tf_op jit(solution)/shard_map/ppermute | solution.py:415
  64.6 3.2 %collective-permute-start.9 = (bf16[4,128,512]{2,1,0:T(8,128)(2,1)S(1)}, bf16[4,128,512]{2,1,0:T(8,128)(2,1)S(1)}, u32[]{:S(2)}, u32[]{:S(2)}) collective-permute-start(bf16[4,128,512]{2,1,0:T(8,128)(2,1)S(1)} %collective-permute-done.8.right), channel_id=1, source_target_pairs={{0,3},{1,0},{2,1},{3,2},{4,7},{5,4},{6,5},{7,6},{8,11},{9,8},{10,9... | collective-permute-start | bytes 1572872 | tf_op jit(solution)/shard_map/ppermute | solution.py:419
  67.9 5.3 %collective-permute-done.4.right = bf16[4,128,512]{2,1,0:T(8,128)(2,1)S(1)} collective-permute-done((bf16[4,128,512]{2,1,0:T(8,128)(2,1)S(1)}, bf16[4,128,512]{2,1,0:T(8,128)(2,1)S(1)}, u32[]{:S(2)}, u32[]{:S(2)}) %collective-permute-start.4) | collective-permute-done | bytes 524320 | tf_op jit(solution)/shard_map/ppermute | solution.py:416
  73.2 3.7 %collective-permute-start.3 = (bf16[4,128,512]{2,1,0:T(8,128)(2,1)S(1)}, bf16[4,128,512]{2,1,0:T(8,128)(2,1)S(1)}, u32[]{:S(2)}, u32[]{:S(2)}) collective-permute-start(bf16[4,128,512]{2,1,0:T(8,128)(2,1)S(1)} %collective-permute-done.2.right), channel_id=1, source_target_pairs={{0,3},{1,0},{2,1},{3,2},{4,7},{5,4},{6,5},{7,6},{8,11},{9,8},{10,9... | collective-permute-start | bytes 1572872 | tf_op jit(solution)/shard_map/ppermute | solution.py:419
  76.9 2.7 %shard_map.129 = (f32[8,128,256]{2,1,0:T(8,128)S(1)}, f32[16,128,128]{2,1,0:T(8,128)S(1)}) custom-call(f32[15,256,256]{2,1,0:T(8,128)S(1)} %copy-done.4, f32[15,256,128]{2,1,0:T(8,128)S(1)} %copy-done.6, f32[15,256,128]{2,1,0:T(8,128)S(1)} %copy-done.5, f32[15,128,128]{2,1,0:T(8,128)S(1)} %copy-done.8), custom_call_target="tpu_custom_call" | custom-call | flops 800000000 | bytes 8847360 | tf_op jit(solution)/shard_map/pallas_call | solution.py:49
  85.0 2.1 %collective-permute-done.7.far_a = bf16[4,128,512]{2,1,0:T(8,128)(2,1)S(1)} collective-permute-done((bf16[4,128,512]{2,1,0:T(8,128)(2,1)S(1)}, bf16[4,128,512]{2,1,0:T(8,128)(2,1)S(1)}, u32[]{:S(2)}, u32[]{:S(2)}) %collective-permute-start.7) | collective-permute-done | bytes 524320 | tf_op jit(solution)/shard_map/ppermute | solution.py:419
  88.5 2.4 %shard_map.133 = (f32[7,128,128]{2,1,0:T(8,128)S(1)}, f32[7,256,128]{2,1,0:T(8,128)S(1)}) custom-call(f32[8,128,128]{2,1,0:T(8,128)S(1)} %get-tuple-element.59.lead, f32[15,256,256]{2,1,0:T(8,128)S(1)} %copy-done.4, f32[15,256,128]{2,1,0:T(8,128)S(1)} %copy-done.6, f32[15,256,128]{2,1,0:T(8,128)S(1)} %copy-done.5, f32[15,128,128]{2,1,0:T(8,128)S(1)} %copy-done.8), custom_call_target="tpu_custom_call" | custom-call | flops 700000000 | bytes 9371648 | tf_op jit(solution)/shard_map/pallas_call | solution.py:49
  94.0 2.2 %shard_map.139 = (bf16[8,128,128]{2,1,0:T(8,128)(2,1)S(1)}, f32[8,128,128]{2,1,0:T(8,128)S(1)}, f32[8,128,128]{2,1,0:T(8,128)S(1)}, f32[7,128,128]{2,1,0:T(8,128)S(1)}, f32[128,128]{1,0:T(8,128)S(1)}) custom-call(s32[2]{0:T(128)S(1)} %pad_add_fusion.row_ref.spot, bf16[4,128,512]{2,1,0:T(8,128)(2,1)S(1)} %collective-permute-done.1.far_a, ...), custom_call_target="tpu_custom_call" | custom-call | flops 400000000 | bytes 8323080 | tf_op jit(solution)/shard_map/pallas_call | solution.py:49
  100.1 2.1 %collective-permute-start.18 = (f32[128,128]{1,0:T(8,128)S(1)}, f32[128,128]{1,0:T(8,128)S(1)}, u32[]{:S(2)}, u32[]{:S(2)}) collective-permute-start(f32[128,128]{1,0:T(8,128)S(1)} %convolution_add_fusion.8), channel_id=1, source_target_pairs={{0,8},{4,12},{8,0},{12,4},{16,24},{20,28},{24,16},{28,20},{32,40},... | collective-permute-start | bytes 196616 | tf_op jit(solution)/shard_map/ppermute | solution.py:505
  102.8 2.2 %collective-permute-done.18 = f32[128,128]{1,0:T(8,128)S(1)} collective-permute-done((f32[128,128]{1,0:T(8,128)S(1)}, f32[128,128]{1,0:T(8,128)S(1)}, u32[]{:S(2)}, u32[]{:S(2)}) %collective-permute-start.18) | collective-permute-done | bytes 65568 | tf_op jit(solution)/shard_map/ppermute | solution.py:505
  106.1 4.8 %collective-permute-done.19 = f32[128,128]{1,0:T(8,128)S(1)} collective-permute-done((f32[128,128]{1,0:T(8,128)S(1)}, f32[128,128]{1,0:T(8,128)S(1)}, u32[]{:S(2)}, u32[]{:S(2)}) %collective-permute-start.19) | collective-permute-done | bytes 65568 | tf_op jit(solution)/shard_map/ppermute | solution.py:505
  111.7 3.9 %collective-permute-done.20 = f32[128,128]{1,0:T(8,128)S(1)} collective-permute-done((f32[128,128]{1,0:T(8,128)S(1)}, f32[128,128]{1,0:T(8,128)S(1)}, u32[]{:S(2)}, u32[]{:S(2)}) %collective-permute-start.20) | collective-permute-done | bytes 65568 | tf_op jit(solution)/shard_map/ppermute | solution.py:505
  116.2 5.3 %collective-permute-done.21 = f32[128,128]{1,0:T(8,128)S(1)} collective-permute-done((f32[128,128]{1,0:T(8,128)S(1)}, f32[128,128]{1,0:T(8,128)S(1)}, u32[]{:S(2)}, u32[]{:S(2)}) %collective-permute-start.21) | collective-permute-done | bytes 65568 | tf_op jit(solution)/shard_map/ppermute | solution.py:505
  121.7 4.4 %leaf_result.1 = f32[8192,128]{1,0:T(8,128)} custom-call(s32[2]{0:T(128)S(1)} %pad_add_fusion.row_ref.spot, f32[128,128]{1,0:T(8,128)S(1)} %convolution_add_fusion.top_ref, f32[16,128,128]{2,1,0:T(8,128)S(1)} %get-tuple-element.85.paths, f32[16,128,128]{2,1,0:T(8,128)S(1)} %shard_map.141.rest, bf16[16,512,128]{2,1,0:T(8,128)(2,1)S(1)} %copy-done.9, ...), custom_call_target="tpu_custom_call" | custom-call | tf_op jit(solution)/shard_map/leaf_result/pallas_call | solution.py:325
  (86 shorter events, 31.1 us)
Async XLA Ops:
  1.1 8.4 %collective-permute-start.12 = (f32[128,256]{1,0:T(8,128)S(1)}, f32[128,256]{1,0:T(8,128)S(1)}, u32[]{:S(2)}, u32[]{:S(2)}) collective-permute-start(f32[128,256]{1,0:T(8,128)S(1)} %get-tuple-element.103), channel_id=1, source_target_pairs={{64,0},{65,1},{66,2},{67,3}} | collective-permute-start | bytes 393224 | tf_op jit(solution)/shard_map/ppermute | solution.py:368
  9.5 67.4 %copy-start.8 = (f32[15,128,128]{2,1,0:T(8,128)S(1)}, f32[15,128,128]{2,1,0:T(8,128)}, u32[]{:S(2)}) copy-start(f32[15,128,128]{2,1,0:T(8,128)} %coarse.6) | copy-start | bytes 2949124
  10.1 9.0 %collective-permute-start.13 = (f32[128,640]{1,0:T(8,128)S(1)}, f32[128,640]{1,0:T(8,128)S(1)}, u32[]{:S(2)}, u32[]{:S(2)}) collective-permute-start(f32[128,640]{1,0:T(8,128)S(1)} %get-tuple-element.61), channel_id=1, source_target_pairs={{0,32},{32,0},{64,96},{96,64},{1,33},{33,1},{65,97},{97,65},{2,34}... | collective-permute-start | bytes 983048 | tf_op jit(solution)/shard_map/ppermute | solution.py:368
  19.1 57.8 %copy-start.6 = (f32[15,256,128]{2,1,0:T(8,128)S(1)}, f32[15,256,128]{2,1,0:T(8,128)}, u32[]{:S(2)}) copy-start(f32[15,256,128]{2,1,0:T(8,128)} %basis.17) | copy-start | bytes 5898244
  19.7 11.9 %collective-permute-start.14 = (f32[128,896]{1,0:T(8,128)S(1)}, f32[128,896]{1,0:T(8,128)S(1)}, u32[]{:S(2)}, u32[]{:S(2)}) collective-permute-start(f32[128,896]{1,0:T(8,128)S(1)} %get-tuple-element.63), channel_id=1, source_target_pairs={{0,16},{16,0},{32,48},{48,32},{64,80},{80,64},{96,112},{112,96},{1... | collective-permute-start | bytes 1376264 | tf_op jit(solution)/shard_map/ppermute | solution.py:368
  32.3 14.1 %collective-permute-start.15 = (f32[128,1536]{1,0:T(8,128)S(1)}, f32[128,1536]{1,0:T(8,128)S(1)}, u32[]{:S(2)}, u32[]{:S(2)}) collective-permute-start(f32[128,1536]{1,0:T(8,128)S(1)} %get-tuple-element.65), channel_id=1, source_target_pairs={{0,8},{8,0},{16,24},{24,16},{32,40},{40,32},{48,56},{56,48},{64,72... | collective-permute-start | bytes 2359304 | tf_op jit(solution)/shard_map/ppermute | solution.py:368
  34.5 10.9 %collective-permute-start.10 = (bf16[4,128,512]{2,1,0:T(8,128)(2,1)S(1)}, bf16[4,128,512]{2,1,0:T(8,128)(2,1)S(1)}, u32[]{:S(2)}, u32[]{:S(2)}) collective-permute-start(bf16[4,128,512]{2,1,0:T(8,128)(2,1)S(1)} %slice.96), channel_id=1, source_target_pairs={{0,3},{1,0},{2,1},{3,2},{4,7},{5,4},{6,5},{7,6},{8,11},{9,8},{10,9... | collective-permute-start | bytes 1572872 | tf_op jit(solution)/shard_map/ppermute | solution.py:416
  38.7 12.6 %collective-permute-start.6 = (bf16[4,128,512]{2,1,0:T(8,128)(2,1)S(1)}, bf16[4,128,512]{2,1,0:T(8,128)(2,1)S(1)}, u32[]{:S(2)}, u32[]{:S(2)}) collective-permute-start(bf16[4,128,512]{2,1,0:T(8,128)(2,1)S(1)} %slice.96), channel_id=1, source_target_pairs={{0,1},{1,2},{2,3},{3,0},{4,5},{5,6},{6,7},{7,4},{8,9},{9,10},{10,1... | collective-permute-start | bytes 1572872 | tf_op jit(solution)/shard_map/ppermute | solution.py:415
  38.9 15.8 %collective-permute-start.11 = (bf16[4,128,512]{2,1,0:T(8,128)(2,1)S(1)}, bf16[4,128,512]{2,1,0:T(8,128)(2,1)S(1)}, u32[]{:S(2)}, u32[]{:S(2)}) collective-permute-start(bf16[4,128,512]{2,1,0:T(8,128)(2,1)S(1)} %get-tuple-element.97), channel_id=1, source_target_pairs={{0,1},{1,2},{2,3},{3,0},{4,5},{5,6},{6,7},{7,4},{8,9},{9,10},{10,1... | collective-permute-start | bytes 1572872 | tf_op jit(solution)/shard_map/ppermute | solution.py:415
  39.0 15.8 %collective-permute-start.8 = (bf16[4,128,512]{2,1,0:T(8,128)(2,1)S(1)}, bf16[4,128,512]{2,1,0:T(8,128)(2,1)S(1)}, u32[]{:S(2)}, u32[]{:S(2)}) collective-permute-start(bf16[4,128,512]{2,1,0:T(8,128)(2,1)S(1)} %get-tuple-element.97), channel_id=1, source_target_pairs={{0,3},{1,0},{2,1},{3,2},{4,7},{5,4},{6,5},{7,6},{8,11},{9,8},{10,9... | collective-permute-start | bytes 1572872 | tf_op jit(solution)/shard_map/ppermute | solution.py:416
  45.4 19.2 %collective-permute-start.5 = (bf16[4,128,512]{2,1,0:T(8,128)(2,1)S(1)}, bf16[4,128,512]{2,1,0:T(8,128)(2,1)S(1)}, u32[]{:S(2)}, u32[]{:S(2)}) collective-permute-start(bf16[4,128,512]{2,1,0:T(8,128)(2,1)S(1)} %get-tuple-element.98), channel_id=1, source_target_pairs={{0,1},{1,2},{2,3},{3,0},{4,5},{5,6},{6,7},{7,4},{8,9},{9,10},{10,1... | collective-permute-start | bytes 1572872 | tf_op jit(solution)/shard_map/ppermute | solution.py:415
  46.4 18.2 %collective-permute-start.2 = (bf16[4,128,512]{2,1,0:T(8,128)(2,1)S(1)}, bf16[4,128,512]{2,1,0:T(8,128)(2,1)S(1)}, u32[]{:S(2)}, u32[]{:S(2)}) collective-permute-start(bf16[4,128,512]{2,1,0:T(8,128)(2,1)S(1)} %get-tuple-element.98), channel_id=1, source_target_pairs={{0,3},{1,0},{2,1},{3,2},{4,7},{5,4},{6,5},{7,6},{8,11},{9,8},{10,9... | collective-permute-start | bytes 1572872 | tf_op jit(solution)/shard_map/ppermute | solution.py:416
  51.3 39.7 %collective-permute-start.16 = (f32[128,2176]{1,0:T(8,128)S(1)}, f32[128,2176]{1,0:T(8,128)S(1)}, u32[]{:S(2)}, u32[]{:S(2)}) collective-permute-start(f32[128,2176]{1,0:T(8,128)S(1)} %get-tuple-element.67), channel_id=1, source_target_pairs={{0,4},{4,0},{8,12},{12,8},{16,20},{20,16},{24,28},{28,24},{32,36},... | collective-permute-start | bytes 3342344 | tf_op jit(solution)/shard_map/ppermute | solution.py:368
  54.7 18.5 %collective-permute-start.4 = (bf16[4,128,512]{2,1,0:T(8,128)(2,1)S(1)}, bf16[4,128,512]{2,1,0:T(8,128)(2,1)S(1)}, u32[]{:S(2)}, u32[]{:S(2)}) collective-permute-start(bf16[4,128,512]{2,1,0:T(8,128)(2,1)S(1)} %get-tuple-element.99), channel_id=1, source_target_pairs={{0,3},{1,0},{2,1},{3,2},{4,7},{5,4},{6,5},{7,6},{8,11},{9,8},{10,9... | collective-permute-start | bytes 1572872 | tf_op jit(solution)/shard_map/ppermute | solution.py:416
  54.7 22.2 %collective-permute-start = (bf16[4,128,512]{2,1,0:T(8,128)(2,1)S(1)}, bf16[4,128,512]{2,1,0:T(8,128)(2,1)S(1)}, u32[]{:S(2)}, u32[]{:S(2)}) collective-permute-start(bf16[4,128,512]{2,1,0:T(8,128)(2,1)S(1)} %get-tuple-element.99), channel_id=1, source_target_pairs={{0,1},{1,2},{2,3},{3,0},{4,5},{5,6},{6,7},{7,4},{8,9},{9,10},{10,1... | collective-permute-start | bytes 1572872 | tf_op jit(solution)/shard_map/ppermute | solution.py:415
  64.6 22.5 %collective-permute-start.7 = (bf16[4,128,512]{2,1,0:T(8,128)(2,1)S(1)}, bf16[4,128,512]{2,1,0:T(8,128)(2,1)S(1)}, u32[]{:S(2)}, u32[]{:S(2)}) collective-permute-start(bf16[4,128,512]{2,1,0:T(8,128)(2,1)S(1)} %collective-permute-done.6.left), channel_id=1, source_target_pairs={{0,1},{1,2},{2,3},{3,0},{4,5},{5,6},{6,7},{7,4},{8,9},{9,10},{10,1... | collective-permute-start | bytes 1572872 | tf_op jit(solution)/shard_map/ppermute | solution.py:419
  64.6 22.5 %collective-permute-start.9 = (bf16[4,128,512]{2,1,0:T(8,128)(2,1)S(1)}, bf16[4,128,512]{2,1,0:T(8,128)(2,1)S(1)}, u32[]{:S(2)}, u32[]{:S(2)}) collective-permute-start(bf16[4,128,512]{2,1,0:T(8,128)(2,1)S(1)} %collective-permute-done.8.right), channel_id=1, source_target_pairs={{0,3},{1,0},{2,1},{3,2},{4,7},{5,4},{6,5},{7,6},{8,11},{9,8},{10,9... | collective-permute-start | bytes 1572872 | tf_op jit(solution)/shard_map/ppermute | solution.py:419
  73.2 19.3 %collective-permute-start.3 = (bf16[4,128,512]{2,1,0:T(8,128)(2,1)S(1)}, bf16[4,128,512]{2,1,0:T(8,128)(2,1)S(1)}, u32[]{:S(2)}, u32[]{:S(2)}) collective-permute-start(bf16[4,128,512]{2,1,0:T(8,128)(2,1)S(1)} %collective-permute-done.2.right), channel_id=1, source_target_pairs={{0,3},{1,0},{2,1},{3,2},{4,7},{5,4},{6,5},{7,6},{8,11},{9,8},{10,9... | collective-permute-start | bytes 1572872 | tf_op jit(solution)/shard_map/ppermute | solution.py:419
  76.9 17.1 %collective-permute-start.1 = (bf16[4,128,512]{2,1,0:T(8,128)(2,1)S(1)}, bf16[4,128,512]{2,1,0:T(8,128)(2,1)S(1)}, u32[]{:S(2)}, u32[]{:S(2)}) collective-permute-start(bf16[4,128,512]{2,1,0:T(8,128)(2,1)S(1)} %collective-permute-done.left), channel_id=1, source_target_pairs={{0,1},{1,2},{2,3},{3,0},{4,5},{5,6},{6,7},{7,4},{8,9},{9,10},{10,1... | collective-permute-start | bytes 1572872 | tf_op jit(solution)/shard_map/ppermute | solution.py:419
  96.2 3.7 %collective-permute-start.17 = (f32[128,128]{1,0:T(8,128)S(1)}, f32[128,128]{1,0:T(8,128)S(1)}, u32[]{:S(2)}, u32[]{:S(2)}) collective-permute-start(f32[128,128]{1,0:T(8,128)S(1)} %get-tuple-element.81), channel_id=1, source_target_pairs={{0,4},{4,0},{8,12},{12,8},{16,20},{20,16},{24,28},{28,24},{32,36},... | collective-permute-start | bytes 196616 | tf_op jit(solution)/shard_map/ppermute | solution.py:505
  100.1 4.8 %collective-permute-start.18 = (f32[128,128]{1,0:T(8,128)S(1)}, f32[128,128]{1,0:T(8,128)S(1)}, u32[]{:S(2)}, u32[]{:S(2)}) collective-permute-start(f32[128,128]{1,0:T(8,128)S(1)} %convolution_add_fusion.8), channel_id=1, source_target_pairs={{0,8},{4,12},{8,0},{12,4},{16,24},{20,28},{24,16},{28,20},{32,40},... | collective-permute-start | bytes 196616 | tf_op jit(solution)/shard_map/ppermute | solution.py:505
  105.3 5.6 %collective-permute-start.19 = (f32[128,128]{1,0:T(8,128)S(1)}, f32[128,128]{1,0:T(8,128)S(1)}, u32[]{:S(2)}, u32[]{:S(2)}) collective-permute-start(f32[128,128]{1,0:T(8,128)S(1)} %convolution_add_fusion.5), channel_id=1, source_target_pairs={{0,24},{4,28},{8,16},{12,20},{16,8},{20,12},{24,0},{28,4},{32,56},... | collective-permute-start | bytes 196616 | tf_op jit(solution)/shard_map/ppermute | solution.py:505
  111.3 4.3 %collective-permute-start.20 = (f32[128,128]{1,0:T(8,128)S(1)}, f32[128,128]{1,0:T(8,128)S(1)}, u32[]{:S(2)}, u32[]{:S(2)}) collective-permute-start(f32[128,128]{1,0:T(8,128)S(1)} %convolution_add_fusion.3), channel_id=1, source_target_pairs={{0,32},{4,36},{8,40},{12,44},{16,48},{20,52},{24,56},{28,60},{32,0... | collective-permute-start | bytes 196616 | tf_op jit(solution)/shard_map/ppermute | solution.py:505
  116.0 5.6 %collective-permute-start.21 = (f32[128,128]{1,0:T(8,128)S(1)}, f32[128,128]{1,0:T(8,128)S(1)}, u32[]{:S(2)}, u32[]{:S(2)}) collective-permute-start(f32[128,128]{1,0:T(8,128)S(1)} %convolution_add_fusion.1), channel_id=1, source_target_pairs={{0,96},{4,100},{8,104},{12,108},{16,112},{20,116},{24,120},{28,124... | collective-permute-start | bytes 196616 | tf_op jit(solution)/shard_map/ppermute | solution.py:505
  (9 other events, 180.2 us)

commit v5 on v4

--- a/solution.py
+++ b/solution.py
@@ -34,10 +34,6 @@
     full = lax.dot_general(left, right, dims, preferred_element_type=wide)
     m, n = a.shape[rows_at], b.shape[1]
     return (full[m:, n:] + full[m:, :n] + full[:m, n:]) + full[:m, :n]
-
-
-def close_dot(a, b):
-    return jnp.dot(a, b, precision=lax.Precision.HIGH, preferred_element_type=wide)
 
 
 def kernel_call(body, out_shape, flops, operands, scalars=0, room=10, **more):
@@ -233,51 +229,85 @@
                 rest[2 * node + k] = ref[at] - below
 
 
-def spread_body(size, bit, spot, got, upper, low_half, high_half, wider, message):
+def spread_body(size, mine, next_mine, bit, spot, got, upper, low_half, high_half, wider, message):
     high, next_high = (lax.rem(spot[1] >> b, 2) == 1 for b in (bit, bit - 1))
-    mine = low_half.shape[1]
     if size:
         wider[:, :size] = jnp.where(high, got[:, :size], upper[...])
-        wider[:, size:] = jnp.where(high, high_half[...], got[:, :mine])
+        wider[:, size:] = jnp.where(high, high_half[:, :mine], got[:, :mine])
     else:
         wider[...] = jnp.where(high, upper[...], got[...])
     held = wider.shape[1]
-    both = min(mine, held)
+    both = min(next_mine, held)
     message[:, :both] = jnp.where(next_high, low_half[:, :both], wider[:, :both])
-    if mine > held:
-        message[:, held:] = low_half[:, held:]
-    if held > mine:
-        message[:, mine:] = wider[:, mine:]
-
-
-def top_body(spot, got, upper, high_half, up_own, up_sib, down_own, down_sib, packs):
-    depth = down_own.shape[0]
+    if next_mine > held:
+        message[:, held:] = low_half[:, held:next_mine]
+    if held > next_mine:
+        message[:, next_mine:] = wider[:, next_mine:]
+
+
+def top_body(spot, got, upper, high_half, up_first, down_first, up_x, down_x, down_y, packs):
     rank = packs.shape[0]
     size = upper.shape[1]
+    mine = pack_width(0, rank)
     high = lax.rem(spot[1], 2) == 1
     packs[:, :size] = jnp.where(high, got[:, :size], upper[...])
-    packs[:, size:] = jnp.where(high, high_half[...], got[:, : high_half.shape[1]])
-    path = None
-    for level in range(depth):
-        root = level == depth - 1
-        first = 0 if root else 2 * rank + (depth - 2 - level) * 5 * rank
+    packs[:, size:] = jnp.where(high, high_half[:, :mine], got[:, :mine])
+
+    def sided(level, matrix):
         is_left = lax.rem(spot[1] >> level, 2) == 0
-
-        def both(matrix):
-            one, two = matrix[:, :rank], matrix[:, rank:]
-            return jnp.where(is_left, one, two), jnp.where(is_left, two, one)
-
-        if root:
-            down = packs[:, first : first + 2 * rank]
-        else:
-            up_own[level], up_sib[level] = both(packs[:, first : first + 2 * rank])
-            down = packs[:, first + 2 * rank : first + 4 * rank]
-        if path is not None:
-            down = split_dot(path, down)
-        down_own[level], down_sib[level] = both(down)
-        if not root:
-            step = packs[:, first + 4 * rank : first + 5 * rank]
-            path = step if path is None else split_dot(path, step)
+        one, two = matrix[:, :rank], matrix[:, rank:]
+        return jnp.concatenate(
+            [jnp.where(is_left, one, two), jnp.where(is_left, two, one)], axis=1
+        )
+
+    ups, downs, sibling, path = {}, {}, {}, None
+    end = packs.shape[1]
+    for level in range(4):
+        first = end - pack_width(level, rank)
+        end = first
+        ups[level] = sided(level, packs[:, first : first + 2 * rank])
+        down = packs[:, first + 2 * rank : first + 4 * rank]
+        downs[level] = sided(level, down if path is None else split_dot(path, down))
+        step = packs[:, first + 4 * rank : first + 5 * rank]
+        path = step if path is None else split_dot(path, step)
+        if level % 2:
+            sibling[level] = sided(level, packs[:, first + 5 * rank : first + 7 * rank])
+    downs[4] = sided(4, split_dot(path, packs[:, : 2 * rank]))
+
+    def joined(above, low):
+        near = split_dot(above[:, :rank], ups[low])
+        return near, split_dot(above[:, rank:], sibling[low])
+
+    up_first[...] = ups[0]
+    down_first[...] = downs[0]
+    up_x[:, : 2 * rank], up_x[:, 2 * rank :] = joined(ups[2], 1)
+    for out, low in ((down_x, 1), (down_y, 3)):
+        near, away = joined(downs[low + 1], low)
+        out[:, : 2 * rank] = downs[low] + near
+        out[:, 2 * rank :] = away
+
+
+def join_body(matrix, *refs):
+    refs[-1][...] = split_dot(
+        matrix[...], jnp.concatenate([r[...] for r in refs[:-1]], axis=0)
+    )
+
+
+def below_body(first, second, *refs):
+    out = refs[-1]
+    out[...] = split_dot(
+        first[...], jnp.concatenate([r[...] for r in refs[:2]], axis=0)
+    ) + split_dot(second[...], jnp.concatenate([r[...] for r in refs[2:-1]], axis=0))
+
+
+def end_body(matrix, before, *refs):
+    refs[-1][...] = before[...] + split_dot(
+        matrix[...], jnp.concatenate([r[...] for r in refs[:-1]], axis=0)
+    )
+
+
+def pack_width(bit, rank):
+    return (7 if bit % 2 else 5) * rank
 
 
 def out_body(
@@ -286,26 +316,25 @@
     some, width = back.shape[0], back.shape[1]
     height = far0.shape[1]
     top = top_ref[...]
-    leaf = pl.program_id(0) * some
     at = [turned(row_ref, part, height) for part in (0, 3, 1, 2)]
 
-    def pick(refs, spans, k):
-        chosen = refs[-1][k]
-        for ref, (start, _) in zip(refs[-2::-1], spans[:0:-1]):
-            chosen = jnp.where(leaf < start, ref[k], chosen)
-        return chosen
-
-    for k in range(some):
-        difference = (rest[k] - split_dot(paths[k], top)).astype(narrow)
-        matching = jnp.concatenate([back[k, pl.ds(a, height), :] for a in at], axis=0)
-        change = narrow_dot(matching, difference)
-        near = pick((near0, near1, near2, near3), PIECES, k)
-        far = pick((far0, far1), GROUPS, k)
-        for j, a in enumerate(at):
-            block = far if j == 3 else near[j * height : (j + 1) * height]
-            out[pl.ds(pl.multiple_of(k * width + a, height), height), :] = (
-                block.astype(wide) - change[j * height : (j + 1) * height]
-            )
+    def leaves_of(near, far):
+        for k in range(some):
+            difference = (rest[k] - split_dot(paths[k], top)).astype(narrow)
+            matching = jnp.concatenate([back[k, pl.ds(a, height), :] for a in at], axis=0)
+            change = narrow_dot(matching, difference)
+            for j, a in enumerate(at):
+                block = far[k] if j == 3 else near[k, j * height : (j + 1) * height, :]
+                out[pl.ds(pl.multiple_of(k * width + a, height), height), :] = (
+                    block.astype(wide) - change[j * height : (j + 1) * height]
+                )
+
+    for step, near in enumerate((near0, near1, near2, near3)):
+        far = (far0, far1)[step // 2]
+
+        @pl.when(pl.program_id(0) == step)
+        def _(near=near, far=far):
+            leaves_of(near, far)
 
 
 def out_call(row, top, paths, rest, back, nears, fars):
@@ -353,11 +382,14 @@
     reduce_mat = exact("ik,ij->kj", basis, inv)
     up_mat = exact("kl,lj->kj", coarse, reduce_mat)
     down_mat = inv - exact("ik,kj->ij", back, reduce_mat)
+    swaps = [
+        (i, i ^ (2 * stride)) for stride in (2, 8) for i in range(stride, total, 2 * stride)
+    ]
+    swapped = lax.ppermute(up_mat, "leaf", swaps)
     halves = [
-        jnp.concatenate([up_mat, down_mat[s : s + rank], back[s : s + rank]], axis=1)
+        jnp.concatenate([up_mat, down_mat[s : s + rank], back[s : s + rank], swapped], axis=1)
         for s in (0, rank)
     ]
-    mine = halves[0].shape[1]
     upper, message, size = inv[rank:], inv[:rank], 0
     for bit in reversed(range(depth)):
         stride = 1 << bit
@@ -368,12 +400,13 @@
         got = lax.ppermute(message, "leaf", pairs)
         if bit == 0:
             return got, upper, halves[1]
+        mine, next_mine = pack_width(bit, rank), pack_width(bit - 1, rank)
         held = size + mine if size else 2 * rank
         upper, message = kernel_call(
-            functools.partial(spread_body, size, bit),
+            functools.partial(spread_body, size, mine, next_mine, bit),
             [
                 jax.ShapeDtypeStruct((rank, held), wide),
-                jax.ShapeDtypeStruct((rank, max(held, mine)), wide),
+                jax.ShapeDtypeStruct((rank, max(held, next_mine)), wide),
             ],
             10**6,
             (spot, got, upper, *halves),
@@ -424,13 +457,13 @@
         top_inv[0], top_basis[0], top_back[0], top_coarse[0], row, depth
     )
     square = (rank, rank)
-    up_own, up_sib, down_own, down_sib = kernel_call(
+    up_first, down_first, up_x, down_x, down_y = kernel_call(
         top_body,
-        [jax.ShapeDtypeStruct((n, *square), wide) for n in (depth - 1, depth - 1, depth, depth)],
+        [jax.ShapeDtypeStruct((rank, n * rank), wide) for n in (2, 2, 4, 4, 4)],
         10**8,
         (row, got, upper, own_half),
         scalars=1,
-        scratch_shapes=[pltpu.VMEM((rank, upper.shape[1] + own_half.shape[1]), wide)],
+        scratch_shapes=[pltpu.VMEM((rank, upper.shape[1] + pack_width(0, rank)), wide)],
     )
     ups, paths = kernel_call(
         prepare_body,
@@ -467,9 +500,11 @@
         room=12,
     )
     final = lax.optimization_barrier(
-        (far[1], parts[2:], ups, early, up_own, up_sib, down_own, down_sib, paths)
-    )
-    last_far, last_parts, ups, early, up_own, up_sib, down_own, down_sib, paths = final
+        (far[1], parts[2:], ups, early, up_first, down_first, up_x, down_x, down_y, paths)
+    )
+    (
+        last_far, last_parts, ups, early, up_first, down_first, up_x, down_x, down_y, paths
+    ) = final
     *last, late, current = kernel_call(
         last_body,
         far_shapes(GROUPS[1][1], height, rank, columns)
@@ -496,19 +531,19 @@
         room=12,
     )
 
-    top = None
-    for level in range(depth):
-        mask = 1 << level
-        if level in (2, 4):
-            mask |= mask >> 1
-        pairs = [(i, i ^ mask) for i in range(leaf_total)]
-        partner = lax.ppermute(current, "leaf", pairs)
-        known = close_dot(down_own[level], current)
-        top = known if top is None else top + known
-        top = top + close_dot(down_sib[level], partner)
-        if level < depth - 1:
-            before = close_dot(up_own[level], current)
-            current = before + close_dot(up_sib[level], partner)
+    def partners(value, masks):
+        return [lax.ppermute(value, "leaf", [(i, i ^ m) for i in range(leaf_total)]) for m in masks]
+
+    tall = jax.ShapeDtypeStruct((rank, columns), wide)
+    first_pair = [current, *partners(current, (1,))]
+    current = kernel_call(join_body, tall, 10**7, (up_first, *first_pair), room=6)
+    along_x = [current, *partners(current, (2, 4, 6))]
+    current = kernel_call(join_body, tall, 2 * 10**7, (up_x, *along_x), room=6)
+    along_y = [current, *partners(current, (8, 16, 24))]
+    below = kernel_call(
+        below_body, tall, 10**7, (down_first, down_x, *first_pair, *along_x), room=6
+    )
+    top = kernel_call(end_body, tall, 10**7, (down_y, below, *along_y), room=6)
     return out_call(row, top, paths, rest, leaf_back, nears, (first[0], last[0]))
 
 

time: 126 us -> 132 us (1.048)
  starting transfers between devices: 31.4 us -> 36.9 us
  matrix products: 6.16 us -> 3.84 us
  Pallas kernels: 25.6 us -> 27 us
    ppermute x5 -> x8, waiting for transfers between devices: 16.2 us -> 5.5 us  [the longest x7 5.5 us: partners(): lax.ppermute(value, 'leaf', [(i, i ^ m) for i in range(leaf_total)])]
    ppermute x5, waiting for transfers between devices: 20.6 us -> 30.7 us  [top_factors(): got = lax.ppermute(message, 'leaf', pairs)]
    ppermute x5 -> x8, starting transfers between devices: 2.95 us -> 9.1 us  [the longest x7 8.43 us: partners(): lax.ppermute(value, 'leaf', [(i, i ^ m) for i in range(leaf_total)])]
    ppermute x2, waiting for transfers between devices: 0.01 us -> 4.05 us  [solve(): lax.ppermute(two, 'rhs', behind)]
    dot_general x18 -> x0, matrix products: 3.16 us -> none  [close_dot(): jnp.dot(a, b, precision=lax.Precision.HIGH, preferred_element_type=wide)]
    ppermute x2, waiting for transfers between devices: 3.6 us -> 1.44 us  [solve(): lax.ppermute(one, 'rhs', ahead)]
    ppermute x4, starting transfers between devices: 11.7 us -> 9.72 us  [solve(): right = [lax.ppermute(a, 'rhs', behind) for a in own]]
    ppermute x4, starting transfers between devices: 2.46 us -> 4.19 us  [solve(): left = [lax.ppermute(a, 'rhs', ahead) for a in own]]
  transfers between devices with their start and end apart: 22 -> 25, of which waited for: 14 -> 13; matrix products, arithmetic and copies ran while one was open for 5% -> 2% of each run, Pallas kernels for 14% -> 14%
where the time goes in v5:
time: 132 us; the launch traced here: 131 us
  waiting for transfers between devices  60.2 us (46%)
  starting transfers between devices  36.9 us (28%)
  Pallas kernels  27 us (20%)
  matrix products  3.84 us (3%)
  local copies, waits for them, and re-layouts  2.8 us (2%)
    ppermute x5, waiting for transfers between devices, top_factors(): got = lax.ppermute(message, 'leaf', pairs)  30.7 us
    pallas_call x15, Pallas kernels, kernel_call(): pl.pallas_call(body, out_shape=out_shape, cost_estimate=pl.CostEstimate(f...  17.3 us
    ppermute x4, waiting for transfers between devices, solve(): left = [lax.ppermute(a, 'rhs', ahead) for a in own]  11.4 us
    ppermute x4, starting transfers between devices, solve(): right = [lax.ppermute(a, 'rhs', behind) for a in own]  9.72 us
    ppermute x7, starting transfers between devices, partners(): lax.ppermute(value, 'leaf', [(i, i ^ m) for i in range(leaf_total)])  8.43 us
    ppermute x5, starting transfers between devices, top_factors(): got = lax.ppermute(message, 'leaf', pairs)  7.22 us
    ppermute x4, waiting for transfers between devices, solve(): right = [lax.ppermute(a, 'rhs', behind) for a in own]  7.2 us
    ppermute x2, starting transfers between devices, solve(): lax.ppermute(two, 'rhs', behind)  6.65 us
  transfers between devices with their start and end apart: 25, of which 13 were waited for; matrix products, arithmetic and copies ran while one was open for 2% of the time, Pallas kernels for 14%

profile of v5, /device:TPU:0, one launch (start us, length us, event | category | flops | bytes accessed | tf_op | source)
XLA Modules:
  0.0 131.3 jit_solution(8185602887534266250)
XLA Ops:
  8.6 5.4 %collective-permute-done.12.got = f32[128,256]{1,0:T(8,128)S(1)} collective-permute-done((f32[128,256]{1,0:T(8,128)S(1)}, f32[128,256]{1,0:T(8,128)S(1)}, u32[]{:S(2)}, u32[]{:S(2)}) %collective-permute-start.12) | collective-permute-done | bytes 131104 | tf_op jit(solution)/shard_map/ppermute | solution.py:400
  14.6 2.0 %collective-permute-start.14 = (f32[128,896]{1,0:T(8,128)S(1)}, f32[128,896]{1,0:T(8,128)S(1)}, u32[]{:S(2)}, u32[]{:S(2)}) collective-permute-start(f32[128,896]{1,0:T(8,128)S(1)} %get-tuple-element.63), channel_id=1, source_target_pairs={{0,32},{32,0},{64,96},{96,64},{1,33},{33,1},{65,97},{97,65},{2,34}... | collective-permute-start | bytes 1376264 | tf_op jit(solution)/shard_map/ppermute | solution.py:400
  16.6 8.4 %collective-permute-done.14.got = f32[128,896]{1,0:T(8,128)S(1)} collective-permute-done((f32[128,896]{1,0:T(8,128)S(1)}, f32[128,896]{1,0:T(8,128)S(1)}, u32[]{:S(2)}, u32[]{:S(2)}) %collective-permute-start.14) | collective-permute-done | bytes 458784 | tf_op jit(solution)/shard_map/ppermute | solution.py:400
  25.6 1.9 %collective-permute-start.15 = (f32[128,1152]{1,0:T(8,128)S(1)}, f32[128,1152]{1,0:T(8,128)S(1)}, u32[]{:S(2)}, u32[]{:S(2)}) collective-permute-start(f32[128,1152]{1,0:T(8,128)S(1)} %get-tuple-element.65), channel_id=1, source_target_pairs={{0,16},{16,0},{32,48},{48,32},{64,80},{80,64},{96,112},{112,96},{1... | collective-permute-start | bytes 1769480 | tf_op jit(solution)/shard_map/ppermute | solution.py:400
  27.6 11.4 %collective-permute-done.15.got = f32[128,1152]{1,0:T(8,128)S(1)} collective-permute-done((f32[128,1152]{1,0:T(8,128)S(1)}, f32[128,1152]{1,0:T(8,128)S(1)}, u32[]{:S(2)}, u32[]{:S(2)}) %collective-permute-start.15) | collective-permute-done | bytes 589856 | tf_op jit(solution)/shard_map/ppermute | solution.py:400
  41.6 4.2 %collective-permute-start.10 = (bf16[4,128,512]{2,1,0:T(8,128)(2,1)S(1)}, bf16[4,128,512]{2,1,0:T(8,128)(2,1)S(1)}, u32[]{:S(2)}, u32[]{:S(2)}) collective-permute-start(bf16[4,128,512]{2,1,0:T(8,128)(2,1)S(1)} %slice.42), channel_id=1, source_target_pairs={{0,3},{1,0},{2,1},{3,2},{4,7},{5,4},{6,5},{7,6},{8,11},{9,8},{10,9... | collective-permute-start | bytes 1572872 | tf_op jit(solution)/shard_map/ppermute | solution.py:449
  46.1 3.3 %collective-permute-start.8 = (bf16[4,128,512]{2,1,0:T(8,128)(2,1)S(1)}, bf16[4,128,512]{2,1,0:T(8,128)(2,1)S(1)}, u32[]{:S(2)}, u32[]{:S(2)}) collective-permute-start(bf16[4,128,512]{2,1,0:T(8,128)(2,1)S(1)} %get-tuple-element.101), channel_id=1, source_target_pairs={{0,3},{1,0},{2,1},{3,2},{4,7},{5,4},{6,5},{7,6},{8,11},{9,8},{10,9... | collective-permute-start | bytes 1572872 | tf_op jit(solution)/shard_map/ppermute | solution.py:449
  49.4 5.6 %collective-permute-done.16.got = f32[128,1792]{1,0:T(8,128)S(1)} collective-permute-done((f32[128,1792]{1,0:T(8,128)S(1)}, f32[128,1792]{1,0:T(8,128)S(1)}, u32[]{:S(2)}, u32[]{:S(2)}) %collective-permute-start.16) | collective-permute-done | bytes 917536 | tf_op jit(solution)/shard_map/ppermute | solution.py:400
  55.8 2.1 %collective-permute-start.5 = (bf16[4,128,512]{2,1,0:T(8,128)(2,1)S(1)}, bf16[4,128,512]{2,1,0:T(8,128)(2,1)S(1)}, u32[]{:S(2)}, u32[]{:S(2)}) collective-permute-start(bf16[4,128,512]{2,1,0:T(8,128)(2,1)S(1)} %get-tuple-element.102), channel_id=1, source_target_pairs={{0,1},{1,2},{2,3},{3,0},{4,5},{5,6},{6,7},{7,4},{8,9},{9,10},{10,1... | collective-permute-start | bytes 1572872 | tf_op jit(solution)/shard_map/ppermute | solution.py:448
  57.9 2.2 %collective-permute-start.2 = (bf16[4,128,512]{2,1,0:T(8,128)(2,1)S(1)}, bf16[4,128,512]{2,1,0:T(8,128)(2,1)S(1)}, u32[]{:S(2)}, u32[]{:S(2)}) collective-permute-start(bf16[4,128,512]{2,1,0:T(8,128)(2,1)S(1)} %get-tuple-element.102), channel_id=1, source_target_pairs={{0,3},{1,0},{2,1},{3,2},{4,7},{5,4},{6,5},{7,6},{8,11},{9,8},{10,9... | collective-permute-start | bytes 1572872 | tf_op jit(solution)/shard_map/ppermute | solution.py:449
  60.1 2.2 %collective-permute-done.11.left = bf16[4,128,512]{2,1,0:T(8,128)(2,1)S(1)} collective-permute-done((bf16[4,128,512]{2,1,0:T(8,128)(2,1)S(1)}, bf16[4,128,512]{2,1,0:T(8,128)(2,1)S(1)}, u32[]{:S(2)}, u32[]{:S(2)}) %collective-permute-start.11) | collective-permute-done | bytes 524320 | tf_op jit(solution)/shard_map/ppermute | solution.py:448
  62.3 2.0 %collective-permute-start = (bf16[4,128,512]{2,1,0:T(8,128)(2,1)S(1)}, bf16[4,128,512]{2,1,0:T(8,128)(2,1)S(1)}, u32[]{:S(2)}, u32[]{:S(2)}) collective-permute-start(bf16[4,128,512]{2,1,0:T(8,128)(2,1)S(1)} %get-tuple-element.103), channel_id=1, source_target_pairs={{0,1},{1,2},{2,3},{3,0},{4,5},{5,6},{6,7},{7,4},{8,9},{9,10},{10,1... | collective-permute-start | bytes 1572872 | tf_op jit(solution)/shard_map/ppermute | solution.py:448
  64.3 9.2 %collective-permute-done.5.left = bf16[4,128,512]{2,1,0:T(8,128)(2,1)S(1)} collective-permute-done((bf16[4,128,512]{2,1,0:T(8,128)(2,1)S(1)}, bf16[4,128,512]{2,1,0:T(8,128)(2,1)S(1)}, u32[]{:S(2)}, u32[]{:S(2)}) %collective-permute-start.5) | collective-permute-done | bytes 524320 | tf_op jit(solution)/shard_map/ppermute | solution.py:448
  73.5 3.2 %collective-permute-start.9 = (bf16[4,128,512]{2,1,0:T(8,128)(2,1)S(1)}, bf16[4,128,512]{2,1,0:T(8,128)(2,1)S(1)}, u32[]{:S(2)}, u32[]{:S(2)}) collective-permute-start(bf16[4,128,512]{2,1,0:T(8,128)(2,1)S(1)} %collective-permute-done.8.right), channel_id=1, source_target_pairs={{0,3},{1,0},{2,1},{3,2},{4,7},{5,4},{6,5},{7,6},{8,11},{9,8},{10,9... | collective-permute-start | bytes 1572872 | tf_op jit(solution)/shard_map/ppermute | solution.py:452
  76.8 7.2 %collective-permute-done.4.right = bf16[4,128,512]{2,1,0:T(8,128)(2,1)S(1)} collective-permute-done((bf16[4,128,512]{2,1,0:T(8,128)(2,1)S(1)}, bf16[4,128,512]{2,1,0:T(8,128)(2,1)S(1)}, u32[]{:S(2)}, u32[]{:S(2)}) %collective-permute-start.4) | collective-permute-done | bytes 524320 | tf_op jit(solution)/shard_map/ppermute | solution.py:449
  84.0 3.4 %collective-permute-start.3 = (bf16[4,128,512]{2,1,0:T(8,128)(2,1)S(1)}, bf16[4,128,512]{2,1,0:T(8,128)(2,1)S(1)}, u32[]{:S(2)}, u32[]{:S(2)}) collective-permute-start(bf16[4,128,512]{2,1,0:T(8,128)(2,1)S(1)} %collective-permute-done.2.right), channel_id=1, source_target_pairs={{0,3},{1,0},{2,1},{3,2},{4,7},{5,4},{6,5},{7,6},{8,11},{9,8},{10,9... | collective-permute-start | bytes 1572872 | tf_op jit(solution)/shard_map/ppermute | solution.py:452
  87.4 2.7 %shard_map.129 = (f32[8,128,256]{2,1,0:T(8,128)S(1)}, f32[16,128,128]{2,1,0:T(8,128)S(1)}) custom-call(f32[15,256,256]{2,1,0:T(8,128)S(1)} %copy-done.4, f32[15,256,128]{2,1,0:T(8,128)S(1)} %copy-done.6, f32[15,256,128]{2,1,0:T(8,128)S(1)} %copy-done.5, f32[15,128,128]{2,1,0:T(8,128)S(1)} %copy-done.8), custom_call_target="tpu_custom_call" | custom-call | flops 800000000 | bytes 8847360 | tf_op jit(solution)/shard_map/pallas_call | solution.py:45
  97.5 2.4 %shard_map.133 = (f32[7,128,128]{2,1,0:T(8,128)S(1)}, f32[7,256,128]{2,1,0:T(8,128)S(1)}) custom-call(f32[8,128,128]{2,1,0:T(8,128)S(1)} %get-tuple-element.61.lead, f32[15,256,256]{2,1,0:T(8,128)S(1)} %copy-done.4, f32[15,256,128]{2,1,0:T(8,128)S(1)} %copy-done.6, f32[15,256,128]{2,1,0:T(8,128)S(1)} %copy-done.5, f32[15,128,128]{2,1,0:T(8,128)S(1)} %copy-done.8), custom_call_target="tpu_custom_call" | custom-call | flops 700000000 | bytes 9371648 | tf_op jit(solution)/shard_map/pallas_call | solution.py:45
  101.7 4.0 %collective-permute-done.3.far_b = bf16[4,128,512]{2,1,0:T(8,128)(2,1)S(1)} collective-permute-done((bf16[4,128,512]{2,1,0:T(8,128)(2,1)S(1)}, bf16[4,128,512]{2,1,0:T(8,128)(2,1)S(1)}, u32[]{:S(2)}, u32[]{:S(2)}) %collective-permute-start.3) | collective-permute-done | bytes 524320 | tf_op jit(solution)/shard_map/ppermute | solution.py:452
  106.8 2.2 %shard_map.139 = (bf16[8,128,128]{2,1,0:T(8,128)(2,1)S(1)}, f32[8,128,128]{2,1,0:T(8,128)S(1)}, f32[8,128,128]{2,1,0:T(8,128)S(1)}, f32[7,128,128]{2,1,0:T(8,128)S(1)}, f32[128,128]{1,0:T(8,128)S(1)}) custom-call(s32[2]{0:T(128)S(1)} %pad_add_fusion.row_ref.spot, bf16[4,128,512]{2,1,0:T(8,128)(2,1)S(1)} %collective-permute-done.1.far_a, ...), custom_call_target="tpu_custom_call" | custom-call | flops 400000000 | bytes 8323080 | tf_op jit(solution)/shard_map/pallas_call | solution.py:45
  111.2 3.5 %collective-permute-start.20 = (f32[128,128]{1,0:T(8,128)S(1)}, f32[128,128]{1,0:T(8,128)S(1)}, u32[]{:S(2)}, u32[]{:S(2)}) collective-permute-start(f32[128,128]{1,0:T(8,128)S(1)} %shard_map.140.refs_2_.refs_0_), channel_id=1, source_target_pairs={{0,16},{4,20},{8,24},{12,28},{16,0},{20,4},{24,8},{28,12},{32,48},... | collective-permute-start | bytes 196616 | tf_op jit(solution)/shard_map/ppermute | solution.py:535
  114.7 2.8 %collective-permute-done.21.refs_5_.refs_3_ = f32[128,128]{1,0:T(8,128)S(1)} collective-permute-done((f32[128,128]{1,0:T(8,128)S(1)}, f32[128,128]{1,0:T(8,128)S(1)}, u32[]{:S(2)}, u32[]{:S(2)}) %collective-permute-start.21) | collective-permute-done | bytes 65568 | tf_op jit(solution)/shard_map/ppermute | solution.py:535
  121.3 2.0 %collective-permute-start.22 = (f32[128,128]{1,0:T(8,128)S(1)}, f32[128,128]{1,0:T(8,128)S(1)}, u32[]{:S(2)}, u32[]{:S(2)}) collective-permute-start(f32[128,128]{1,0:T(8,128)S(1)} %shard_map.142.refs_0_), channel_id=1, source_target_pairs={{0,32},{4,36},{8,40},{12,44},{16,48},{20,52},{24,56},{28,60},{32,0... | collective-permute-start | bytes 196616 | tf_op jit(solution)/shard_map/ppermute | solution.py:535
  126.9 4.4 %leaf_result.1 = f32[8192,128]{1,0:T(8,128)} custom-call(s32[2]{0:T(128)S(1)} %pad_add_fusion.row_ref.spot, f32[128,128]{1,0:T(8,128)S(1)} %shard_map.143.top_ref, f32[16,128,128]{2,1,0:T(8,128)S(1)} %get-tuple-element.89.paths, f32[16,128,128]{2,1,0:T(8,128)S(1)} %shard_map.145.rest, bf16[16,512,128]{2,1,0:T(8,128)(2,1)S(1)} %copy-done.9, ...), custom_call_target="tpu_custom_call" | custom-call | tf_op jit(solution)/shard_map/leaf_result/pallas_call | solution.py:354
  (78 shorter events, 33.1 us)
Async XLA Ops:
  4.0 4.6 %collective-permute-start.13 = (f32[128,256]{1,0:T(8,128)S(1)}, f32[128,256]{1,0:T(8,128)S(1)}, u32[]{:S(2)}, u32[]{:S(2)}) collective-permute-start(f32[128,256]{1,0:T(8,128)S(1)} %convolution_bitcast_fusion.1), channel_id=1, source_target_pairs={{8,24},{24,8},{40,56},{56,40},{72,88},{88,72},{104,120},{120,104},... | collective-permute-start | bytes 393224 | tf_op jit(solution)/shard_map/ppermute | solution.py:388
  5.7 8.4 %collective-permute-start.12 = (f32[128,256]{1,0:T(8,128)S(1)}, f32[128,256]{1,0:T(8,128)S(1)}, u32[]{:S(2)}, u32[]{:S(2)}) collective-permute-start(f32[128,256]{1,0:T(8,128)S(1)} %get-tuple-element.109), channel_id=1, source_target_pairs={{64,0},{65,1},{66,2},{67,3}} | collective-permute-start | bytes 393224 | tf_op jit(solution)/shard_map/ppermute | solution.py:400
  14.6 10.4 %collective-permute-start.14 = (f32[128,896]{1,0:T(8,128)S(1)}, f32[128,896]{1,0:T(8,128)S(1)}, u32[]{:S(2)}, u32[]{:S(2)}) collective-permute-start(f32[128,896]{1,0:T(8,128)S(1)} %get-tuple-element.63), channel_id=1, source_target_pairs={{0,32},{32,0},{64,96},{96,64},{1,33},{33,1},{65,97},{97,65},{2,34}... | collective-permute-start | bytes 1376264 | tf_op jit(solution)/shard_map/ppermute | solution.py:400
  25.6 13.3 %collective-permute-start.15 = (f32[128,1152]{1,0:T(8,128)S(1)}, f32[128,1152]{1,0:T(8,128)S(1)}, u32[]{:S(2)}, u32[]{:S(2)}) collective-permute-start(f32[128,1152]{1,0:T(8,128)S(1)} %get-tuple-element.65), channel_id=1, source_target_pairs={{0,16},{16,0},{32,48},{48,32},{64,80},{80,64},{96,112},{112,96},{1... | collective-permute-start | bytes 1769480 | tf_op jit(solution)/shard_map/ppermute | solution.py:400
  39.7 15.3 %collective-permute-start.16 = (f32[128,1792]{1,0:T(8,128)S(1)}, f32[128,1792]{1,0:T(8,128)S(1)}, u32[]{:S(2)}, u32[]{:S(2)}) collective-permute-start(f32[128,1792]{1,0:T(8,128)S(1)} %get-tuple-element.67), channel_id=1, source_target_pairs={{0,8},{8,0},{16,24},{24,16},{32,40},{40,32},{48,56},{56,48},{64,72... | collective-permute-start | bytes 2752520 | tf_op jit(solution)/shard_map/ppermute | solution.py:400
  41.6 14.2 %collective-permute-start.10 = (bf16[4,128,512]{2,1,0:T(8,128)(2,1)S(1)}, bf16[4,128,512]{2,1,0:T(8,128)(2,1)S(1)}, u32[]{:S(2)}, u32[]{:S(2)}) collective-permute-start(bf16[4,128,512]{2,1,0:T(8,128)(2,1)S(1)} %slice.42), channel_id=1, source_target_pairs={{0,3},{1,0},{2,1},{3,2},{4,7},{5,4},{6,5},{7,6},{8,11},{9,8},{10,9... | collective-permute-start | bytes 1572872 | tf_op jit(solution)/shard_map/ppermute | solution.py:449
  45.8 12.1 %collective-permute-start.6 = (bf16[4,128,512]{2,1,0:T(8,128)(2,1)S(1)}, bf16[4,128,512]{2,1,0:T(8,128)(2,1)S(1)}, u32[]{:S(2)}, u32[]{:S(2)}) collective-permute-start(bf16[4,128,512]{2,1,0:T(8,128)(2,1)S(1)} %slice.42), channel_id=1, source_target_pairs={{0,1},{1,2},{2,3},{3,0},{4,5},{5,6},{6,7},{7,4},{8,9},{9,10},{10,1... | collective-permute-start | bytes 1572872 | tf_op jit(solution)/shard_map/ppermute | solution.py:448
  46.0 16.3 %collective-permute-start.11 = (bf16[4,128,512]{2,1,0:T(8,128)(2,1)S(1)}, bf16[4,128,512]{2,1,0:T(8,128)(2,1)S(1)}, u32[]{:S(2)}, u32[]{:S(2)}) collective-permute-start(bf16[4,128,512]{2,1,0:T(8,128)(2,1)S(1)} %get-tuple-element.101), channel_id=1, source_target_pairs={{0,1},{1,2},{2,3},{3,0},{4,5},{5,6},{6,7},{7,4},{8,9},{9,10},{10,1... | collective-permute-start | bytes 1572872 | tf_op jit(solution)/shard_map/ppermute | solution.py:448
  46.1 16.2 %collective-permute-start.8 = (bf16[4,128,512]{2,1,0:T(8,128)(2,1)S(1)}, bf16[4,128,512]{2,1,0:T(8,128)(2,1)S(1)}, u32[]{:S(2)}, u32[]{:S(2)}) collective-permute-start(bf16[4,128,512]{2,1,0:T(8,128)(2,1)S(1)} %get-tuple-element.101), channel_id=1, source_target_pairs={{0,3},{1,0},{2,1},{3,2},{4,7},{5,4},{6,5},{7,6},{8,11},{9,8},{10,9... | collective-permute-start | bytes 1572872 | tf_op jit(solution)/shard_map/ppermute | solution.py:449
  55.7 44.2 %collective-permute-start.17 = (f32[128,2688]{1,0:T(8,128)S(1)}, f32[128,2688]{1,0:T(8,128)S(1)}, u32[]{:S(2)}, u32[]{:S(2)}) collective-permute-start(f32[128,2688]{1,0:T(8,128)S(1)} %get-tuple-element.69), channel_id=1, source_target_pairs={{0,4},{4,0},{8,12},{12,8},{16,20},{20,16},{24,28},{28,24},{32,36},... | collective-permute-start | bytes 4128776 | tf_op jit(solution)/shard_map/ppermute | solution.py:400
  55.8 17.7 %collective-permute-start.5 = (bf16[4,128,512]{2,1,0:T(8,128)(2,1)S(1)}, bf16[4,128,512]{2,1,0:T(8,128)(2,1)S(1)}, u32[]{:S(2)}, u32[]{:S(2)}) collective-permute-start(bf16[4,128,512]{2,1,0:T(8,128)(2,1)S(1)} %get-tuple-element.102), channel_id=1, source_target_pairs={{0,1},{1,2},{2,3},{3,0},{4,5},{5,6},{6,7},{7,4},{8,9},{9,10},{10,1... | collective-permute-start | bytes 1572872 | tf_op jit(solution)/shard_map/ppermute | solution.py:448
  57.9 15.6 %collective-permute-start.2 = (bf16[4,128,512]{2,1,0:T(8,128)(2,1)S(1)}, bf16[4,128,512]{2,1,0:T(8,128)(2,1)S(1)}, u32[]{:S(2)}, u32[]{:S(2)}) collective-permute-start(bf16[4,128,512]{2,1,0:T(8,128)(2,1)S(1)} %get-tuple-element.102), channel_id=1, source_target_pairs={{0,3},{1,0},{2,1},{3,2},{4,7},{5,4},{6,5},{7,6},{8,11},{9,8},{10,9... | collective-permute-start | bytes 1572872 | tf_op jit(solution)/shard_map/ppermute | solution.py:449
  62.3 21.7 %collective-permute-start.4 = (bf16[4,128,512]{2,1,0:T(8,128)(2,1)S(1)}, bf16[4,128,512]{2,1,0:T(8,128)(2,1)S(1)}, u32[]{:S(2)}, u32[]{:S(2)}) collective-permute-start(bf16[4,128,512]{2,1,0:T(8,128)(2,1)S(1)} %get-tuple-element.103), channel_id=1, source_target_pairs={{0,3},{1,0},{2,1},{3,2},{4,7},{5,4},{6,5},{7,6},{8,11},{9,8},{10,9... | collective-permute-start | bytes 1572872 | tf_op jit(solution)/shard_map/ppermute | solution.py:449
  62.3 25.1 %collective-permute-start = (bf16[4,128,512]{2,1,0:T(8,128)(2,1)S(1)}, bf16[4,128,512]{2,1,0:T(8,128)(2,1)S(1)}, u32[]{:S(2)}, u32[]{:S(2)}) collective-permute-start(bf16[4,128,512]{2,1,0:T(8,128)(2,1)S(1)} %get-tuple-element.103), channel_id=1, source_target_pairs={{0,1},{1,2},{2,3},{3,0},{4,5},{5,6},{6,7},{7,4},{8,9},{9,10},{10,1... | collective-permute-start | bytes 1572872 | tf_op jit(solution)/shard_map/ppermute | solution.py:448
  73.5 22.5 %collective-permute-start.7 = (bf16[4,128,512]{2,1,0:T(8,128)(2,1)S(1)}, bf16[4,128,512]{2,1,0:T(8,128)(2,1)S(1)}, u32[]{:S(2)}, u32[]{:S(2)}) collective-permute-start(bf16[4,128,512]{2,1,0:T(8,128)(2,1)S(1)} %collective-permute-done.6.left), channel_id=1, source_target_pairs={{0,1},{1,2},{2,3},{3,0},{4,5},{5,6},{6,7},{7,4},{8,9},{9,10},{10,1... | collective-permute-start | bytes 1572872 | tf_op jit(solution)/shard_map/ppermute | solution.py:452
  73.5 22.5 %collective-permute-start.9 = (bf16[4,128,512]{2,1,0:T(8,128)(2,1)S(1)}, bf16[4,128,512]{2,1,0:T(8,128)(2,1)S(1)}, u32[]{:S(2)}, u32[]{:S(2)}) collective-permute-start(bf16[4,128,512]{2,1,0:T(8,128)(2,1)S(1)} %collective-permute-done.8.right), channel_id=1, source_target_pairs={{0,3},{1,0},{2,1},{3,2},{4,7},{5,4},{6,5},{7,6},{8,11},{9,8},{10,9... | collective-permute-start | bytes 1572872 | tf_op jit(solution)/shard_map/ppermute | solution.py:452
  84.0 21.8 %collective-permute-start.3 = (bf16[4,128,512]{2,1,0:T(8,128)(2,1)S(1)}, bf16[4,128,512]{2,1,0:T(8,128)(2,1)S(1)}, u32[]{:S(2)}, u32[]{:S(2)}) collective-permute-start(bf16[4,128,512]{2,1,0:T(8,128)(2,1)S(1)} %collective-permute-done.2.right), channel_id=1, source_target_pairs={{0,3},{1,0},{2,1},{3,2},{4,7},{5,4},{6,5},{7,6},{8,11},{9,8},{10,9... | collective-permute-start | bytes 1572872 | tf_op jit(solution)/shard_map/ppermute | solution.py:452
  87.4 19.4 %collective-permute-start.1 = (bf16[4,128,512]{2,1,0:T(8,128)(2,1)S(1)}, bf16[4,128,512]{2,1,0:T(8,128)(2,1)S(1)}, u32[]{:S(2)}, u32[]{:S(2)}) collective-permute-start(bf16[4,128,512]{2,1,0:T(8,128)(2,1)S(1)} %collective-permute-done.left), channel_id=1, source_target_pairs={{0,1},{1,2},{2,3},{3,0},{4,5},{5,6},{6,7},{7,4},{8,9},{9,10},{10,1... | collective-permute-start | bytes 1572872 | tf_op jit(solution)/shard_map/ppermute | solution.py:452
  110.5 7.0 %collective-permute-start.21 = (f32[128,128]{1,0:T(8,128)S(1)}, f32[128,128]{1,0:T(8,128)S(1)}, u32[]{:S(2)}, u32[]{:S(2)}) collective-permute-start(f32[128,128]{1,0:T(8,128)S(1)} %shard_map.140.refs_2_.refs_0_), channel_id=1, source_target_pairs={{0,24},{4,28},{8,16},{12,20},{16,8},{20,12},{24,0},{28,4},{32,56},... | collective-permute-start | bytes 196616 | tf_op jit(solution)/shard_map/ppermute | solution.py:535
  111.2 6.3 %collective-permute-start.20 = (f32[128,128]{1,0:T(8,128)S(1)}, f32[128,128]{1,0:T(8,128)S(1)}, u32[]{:S(2)}, u32[]{:S(2)}) collective-permute-start(f32[128,128]{1,0:T(8,128)S(1)} %shard_map.140.refs_2_.refs_0_), channel_id=1, source_target_pairs={{0,16},{4,20},{8,24},{12,28},{16,0},{20,4},{24,8},{28,12},{32,48},... | collective-permute-start | bytes 196616 | tf_op jit(solution)/shard_map/ppermute | solution.py:535
  114.7 4.3 %collective-permute-start.19 = (f32[128,128]{1,0:T(8,128)S(1)}, f32[128,128]{1,0:T(8,128)S(1)}, u32[]{:S(2)}, u32[]{:S(2)}) collective-permute-start(f32[128,128]{1,0:T(8,128)S(1)} %shard_map.140.refs_2_.refs_0_), channel_id=1, source_target_pairs={{0,8},{4,12},{8,0},{12,4},{16,24},{20,28},{24,16},{28,20},{32,40},... | collective-permute-start | bytes 196616 | tf_op jit(solution)/shard_map/ppermute | solution.py:535
  119.2 7.4 %collective-permute-start.24 = (f32[128,128]{1,0:T(8,128)S(1)}, f32[128,128]{1,0:T(8,128)S(1)}, u32[]{:S(2)}, u32[]{:S(2)}) collective-permute-start(f32[128,128]{1,0:T(8,128)S(1)} %shard_map.142.refs_0_), channel_id=1, source_target_pairs={{0,96},{4,100},{8,104},{12,108},{16,112},{20,116},{24,120},{28,124... | collective-permute-start | bytes 196616 | tf_op jit(solution)/shard_map/ppermute | solution.py:535
  120.7 5.9 %collective-permute-start.23 = (f32[128,128]{1,0:T(8,128)S(1)}, f32[128,128]{1,0:T(8,128)S(1)}, u32[]{:S(2)}, u32[]{:S(2)}) collective-permute-start(f32[128,128]{1,0:T(8,128)S(1)} %shard_map.142.refs_0_), channel_id=1, source_target_pairs={{0,64},{4,68},{8,72},{12,76},{16,80},{20,84},{24,88},{28,92},{32,9... | collective-permute-start | bytes 196616 | tf_op jit(solution)/shard_map/ppermute | solution.py:535
  121.3 5.3 %collective-permute-start.22 = (f32[128,128]{1,0:T(8,128)S(1)}, f32[128,128]{1,0:T(8,128)S(1)}, u32[]{:S(2)}, u32[]{:S(2)}) collective-permute-start(f32[128,128]{1,0:T(8,128)S(1)} %shard_map.142.refs_0_), channel_id=1, source_target_pairs={{0,32},{4,36},{8,40},{12,44},{16,48},{20,52},{24,56},{28,60},{32,0... | collective-permute-start | bytes 196616 | tf_op jit(solution)/shard_map/ppermute | solution.py:535
  (12 other events, 273.1 us)

commit v6 on v5

--- a/solution.py
+++ b/solution.py
@@ -11,7 +11,7 @@
 wide = jnp.float32
 narrow = jnp.bfloat16
 
-GROUPS = ((0, 8), (8, 8))
+GROUPS = (tuple(range(8)), (8, 9, 12, 13), (10, 11, 14, 15))
 PIECES = ((0, 4), (4, 4), (8, 4), (12, 4))
 MERGED = (0, 1, 2, 3, 8, 9, 12)
 LATE = (4, 5, 6, 7, 10, 11, 13, 14)
@@ -110,32 +110,33 @@
 def far_leaves(
     group, row_ref, far_a, far_b, rhs, basis, coarse, part_a, part_b, vals, proj, lead
 ):
-    start, count = GROUPS[group]
+    leaves = GROUPS[group]
     height, width = far_a.shape[1], far_a.shape[2]
-    half = count // 2
+    half = len(leaves) // 2
     at = turned(row_ref, 2, height)
-    for k in range(count):
-        leaf = start + k
+    for k, leaf in enumerate(leaves):
         rows = far_a[k] if k < half else far_b[k - half]
         got = narrow_dot(rows, rhs[leaf * width : (leaf + 1) * width, :])
         vals[k] = got.astype(narrow)
-    for k in range(count):
-        before = part_a[k] if k < half else part_b[k - half]
+    for k, leaf in enumerate(leaves):
+        before = (part_a if k < half else part_b)[leaf % 4]
         proj[k] = before + lax.dot_general(
-            basis[start + k, pl.ds(at, height), :], vals[k], FRONT, preferred_element_type=wide
+            basis[leaf, pl.ds(at, height), :], vals[k], FRONT, preferred_element_type=wide
         )
-    for k in range(count):
-        lead[k] = split_dot(coarse[start + k], proj[k])
+    for k, leaf in enumerate(leaves):
+        lead[k] = split_dot(coarse[leaf], proj[k])
 
 
 def last_body(
-    row_ref, far_a, far_b, rhs, basis, coarse, part_a, part_b, ups, early,
+    row_ref, far_a, far_b, rhs, basis, coarse, part_a, part_b, lead1, ups, early,
     vals, proj, lead, late, up,
 ):
     far_leaves(
-        1, row_ref, far_a, far_b, rhs, basis, coarse, part_a, part_b, vals, proj, lead
-    )
-    value = {8 + k: (lead, k) for k in range(8)}
+        2, row_ref, far_a, far_b, rhs, basis, coarse, part_a, part_b, vals, proj, lead
+    )
+    value = {
+        leaf: (ref, k) for g, ref in ((1, lead1), (2, lead)) for k, leaf in enumerate(GROUPS[g])
+    }
     for k, node in enumerate(MERGED):
         value[16 + node] = (early, k)
     for k, node in enumerate(LATE):
@@ -192,8 +193,10 @@
                 paths[2 * node + k] = value[2 * node + k]
 
 
-def late_body(lead, late, early, inv, basis, back, base):
-    value = {8 + k: (lead, k) for k in range(8)}
+def late_body(lead1, lead2, late, early, inv, basis, back, base):
+    value = {
+        leaf: (ref, k) for g, ref in ((1, lead1), (2, lead2)) for k, leaf in enumerate(GROUPS[g])
+    }
     for k, node in enumerate(MERGED):
         value[16 + node] = (early, k)
     for k, node in enumerate(LATE[:-1]):
@@ -208,13 +211,17 @@
         base[k] -= split_dot(back[node], reduced[k])
 
 
-def known_body(base0, base1, back, proj0, proj1, rest):
+def known_body(base0, base1, back, proj0, proj1, proj2, rest):
     rank = proj0.shape[1]
     known = {}
     for base, nodes in ((base0, MERGED), (base1, LATE)):
         for k, node in enumerate(nodes):
             known[node] = (base, k)
-    projs = [(proj, k) for proj in (proj0, proj1) for k in range(proj.shape[0])]
+    projs = {
+        leaf: (ref, k)
+        for ref, leaves in zip((proj0, proj1, proj2), GROUPS)
+        for k, leaf in enumerate(leaves)
+    }
     part = {30: None}
     for node in reversed(range(15)):
         ref, at = known[node]
@@ -300,76 +307,55 @@
     ) + split_dot(second[...], jnp.concatenate([r[...] for r in refs[2:-1]], axis=0))
 
 
-def end_body(matrix, before, *refs):
-    refs[-1][...] = before[...] + split_dot(
-        matrix[...], jnp.concatenate([r[...] for r in refs[:-1]], axis=0)
-    )
-
-
 def pack_width(bit, rank):
     return (7 if bit % 2 else 5) * rank
 
 
 def out_body(
-    row_ref, top_ref, paths, rest, back, near0, near1, near2, near3, far0, far1, out
+    row_ref, down_y, below, here, one, two, three, paths, rest, back,
+    near0, near1, near2, near3, far0, far1, far2, out, blocks, sent,
 ):
-    some, width = back.shape[0], back.shape[1]
+    leaves, width = back.shape[0], back.shape[1]
     height = far0.shape[1]
-    top = top_ref[...]
+    along = jnp.concatenate([here[...], one[...], two[...], three[...]], axis=0)
+    top = below[...] + split_dot(down_y[...], along)
     at = [turned(row_ref, part, height) for part in (0, 3, 1, 2)]
-
-    def leaves_of(near, far):
-        for k in range(some):
-            difference = (rest[k] - split_dot(paths[k], top)).astype(narrow)
-            matching = jnp.concatenate([back[k, pl.ds(a, height), :] for a in at], axis=0)
-            change = narrow_dot(matching, difference)
-            for j, a in enumerate(at):
-                block = far[k] if j == 3 else near[k, j * height : (j + 1) * height, :]
-                out[pl.ds(pl.multiple_of(k * width + a, height), height), :] = (
-                    block.astype(wide) - change[j * height : (j + 1) * height]
-                )
-
-    for step, near in enumerate((near0, near1, near2, near3)):
-        far = (far0, far1)[step // 2]
-
-        @pl.when(pl.program_id(0) == step)
-        def _(near=near, far=far):
-            leaves_of(near, far)
-
-
-def out_call(row, top, paths, rest, back, nears, fars):
-    leaves, width, rank = back.shape
-    height, columns = fars[0].shape[1:]
-    some = 4
-
-    def at(shape):
-        return pl.BlockSpec(shape, lambda i, row: (i,) + (0,) * (len(shape) - 1))
-
-    def within(shape, span):
-        first, most = span[0] // some, span[1] // some - 1
-        return pl.BlockSpec(
-            shape, lambda i, row: (jnp.clip(i - first, 0, most),) + (0,) * (len(shape) - 1)
+    spans = zip(PIECES, (near0, near1, near2, near3))
+    nears = [(ref, k) for (_, count), ref in spans for k in range(count)]
+    fars = {
+        leaf: (ref, k)
+        for ref, group in zip((far0, far1, far2), GROUPS)
+        for k, leaf in enumerate(group)
+    }
+    copies = [
+        pltpu.make_async_copy(
+            blocks.at[leaf], out.at[pl.ds(leaf * width, width), :], sent.at[leaf]
         )
-
-    return pl.pallas_call(
-        out_body,
-        grid_spec=pltpu.PrefetchScalarGridSpec(
-            num_scalar_prefetch=1,
-            grid=(leaves // some,),
-            in_specs=[
-                pl.BlockSpec(top.shape, lambda i, row: (0, 0)),
-                at((some, rank, rank)),
-                at((some, rank, columns)),
-                at((some, width, rank)),
-                *[within((some, 3 * height, columns), span) for span in PIECES],
-                *[within((some, height, columns), span) for span in GROUPS],
-            ],
-            out_specs=at((some * width, columns)),
-        ),
-        out_shape=jax.ShapeDtypeStruct((leaves * width, columns), wide),
-        compiler_params=pltpu.CompilerParams(vmem_limit_bytes=8 * 1024 * 1024),
-        name="leaf_result",
-    )(row, top, paths, rest, back, *nears, *fars)
+        for leaf in range(leaves)
+    ]
+    rank, some = top.shape[0], 4
+    for leaf in range(leaves):
+        k = leaf % some
+        if k == 0:
+            these = paths[leaf : leaf + some].reshape(some * rank, rank)
+            down = split_dot(these, top)
+        difference = (rest[leaf] - down[k * rank : (k + 1) * rank]).astype(narrow)
+        matching = jnp.concatenate([back[leaf, pl.ds(a, height), :] for a in at], axis=0)
+        change = narrow_dot(matching, difference)
+        near, far = nears[leaf], fars[leaf]
+        for j, a in enumerate(at):
+            if j == 3:
+                block = far[0][far[1]]
+            else:
+                block = near[0][near[1], j * height : (j + 1) * height, :]
+            blocks[leaf, pl.ds(a, height), :] = (
+                block.astype(wide) - change[j * height : (j + 1) * height]
+            )
+        if leaf:
+            copies[leaf - 1].start()
+    copies[-1].start()
+    for copy in copies:
+        copy.wait()
 
 
 def exact(eq, a, b):
@@ -430,7 +416,7 @@
     top_back,
     top_coarse,
 ):
-    leaf_count, height, _ = leaf_inv.shape
+    leaf_count, height, width = leaf_inv.shape
     rank, columns = leaf_basis.shape[2], rhs_cols.shape[1]
     position = lax.axis_index("leaf")
     leaf_total = lax.axis_size("leaf")
@@ -447,7 +433,7 @@
             whole, own[0], row = lax.optimization_barrier((whole, own[0], row))
     left = [lax.ppermute(a, "rhs", ahead) for a in own]
     right = [lax.ppermute(a, "rhs", behind) for a in own]
-    pairs = ((left[0], right[1]), (left[2], right[3]))
+    pairs = ((left[0], right[1]), (left[2][:2], right[3][:2]), (left[2][2:], right[3][2:]))
     far = [
         (lax.ppermute(one, "rhs", ahead), lax.ppermute(two, "rhs", behind))
         for one, two in pairs
@@ -484,9 +470,16 @@
     shared = (rhs_cols, leaf_basis, leaf_coarse)
     first = kernel_call(
         functools.partial(far_leaves, 0),
-        far_shapes(GROUPS[0][1], height, rank, columns),
+        far_shapes(len(GROUPS[0]), height, rank, columns),
         3 * 10**8,
         (row, *far[0], *shared, *parts[:2]),
+        scalars=1,
+    )
+    second = kernel_call(
+        functools.partial(far_leaves, 1),
+        far_shapes(len(GROUPS[1]), height, rank, columns),
+        15 * 10**7,
+        (row, *far[1], *shared, *parts[2:]),
         scalars=1,
     )
     early, early_base = kernel_call(
@@ -500,34 +493,34 @@
         room=12,
     )
     final = lax.optimization_barrier(
-        (far[1], parts[2:], ups, early, up_first, down_first, up_x, down_x, down_y, paths)
+        (far[2], parts[2:], second[2], ups, early, up_first, down_first, up_x, down_x, down_y, paths)
     )
     (
-        last_far, last_parts, ups, early, up_first, down_first, up_x, down_x, down_y, paths
+        last_far, last_parts, second_lead, ups, early, up_first, down_first, up_x, down_x, down_y, paths
     ) = final
     *last, late, current = kernel_call(
         last_body,
-        far_shapes(GROUPS[1][1], height, rank, columns)
+        far_shapes(len(GROUPS[2]), height, rank, columns)
         + [
             jax.ShapeDtypeStruct((len(LATE) - 1, rank, columns), wide),
             jax.ShapeDtypeStruct((rank, columns), wide),
         ],
         4 * 10**8,
-        (row, *last_far, *shared, *last_parts, ups, early),
+        (row, *last_far, *shared, *last_parts, second_lead, ups, early),
         scalars=1,
     )
     late_base = kernel_call(
         late_body,
         jax.ShapeDtypeStruct((len(LATE), 2 * rank, columns), wide),
         6 * 10**8,
-        (last[2], late, early, mid_inv, mid_basis, mid_back),
+        (second_lead, last[2], late, early, mid_inv, mid_basis, mid_back),
         room=12,
     )
     rest = kernel_call(
         known_body,
         jax.ShapeDtypeStruct((leaf_count, rank, columns), wide),
         4 * 10**8,
-        (early_base, late_base, mid_back, first[1], last[1]),
+        (early_base, late_base, mid_back, first[1], second[1], last[1]),
         room=12,
     )
 
@@ -543,8 +536,31 @@
     below = kernel_call(
         below_body, tall, 10**7, (down_first, down_x, *first_pair, *along_x), room=6
     )
-    top = kernel_call(end_body, tall, 10**7, (down_y, below, *along_y), room=6)
-    return out_call(row, top, paths, rest, leaf_back, nears, (first[0], last[0]))
+    return kernel_call(
+        out_body,
+        jax.ShapeDtypeStruct((leaf_count * width, columns), wide),
+        10**9,
+        (
+            row,
+            down_y,
+            below,
+            *along_y,
+            paths,
+            rest,
+            leaf_back,
+            *nears,
+            first[0],
+            second[0],
+            last[0],
+        ),
+        scalars=1,
+        room=12,
+        out_specs=pl.BlockSpec(memory_space=pl.ANY),
+        scratch_shapes=[
+            pltpu.VMEM((leaf_count, width, columns), wide),
+            pltpu.SemaphoreType.DMA((leaf_count,)),
+        ],
+    )
 
 
 def solution(mesh):

time: 132 us -> 136 us (1.030)
  waiting for transfers between devices: 60.2 us -> 63.9 us
    ppermute x4, starting transfers between devices: 9.72 us -> 15 us  [solve(): right = [lax.ppermute(a, 'rhs', behind) for a in own]]
    ppermute x4, waiting for transfers between devices: 11.4 us -> 16.3 us  [solve(): left = [lax.ppermute(a, 'rhs', ahead) for a in own]]
    pallas_call x15 -> x16, Pallas kernels: 17.3 us -> 21.7 us  [kernel_call(): pl.pallas_call(body, out_shape=out_shape, cost_estimate=pl.CostEstimate(f...]
    pallas_call x1 -> x0, Pallas kernels: 4.4 us -> none  [out_call(): pl.pallas_call(out_body, grid_spec=pltpu.PrefetchScalarGridSpec(num_scala...]
    ppermute x4, starting transfers between devices: 4.19 us -> 0.08 us  [solve(): left = [lax.ppermute(a, 'rhs', ahead) for a in own]]
    ppermute x2 -> x3, starting transfers between devices: 6.65 us -> 3.7 us  [solve(): lax.ppermute(two, 'rhs', behind)]
    ppermute x2 -> x3, starting transfers between devices: 0.01 us -> 2.38 us  [solve(): lax.ppermute(one, 'rhs', ahead)]
    ppermute x2 -> x3, waiting for transfers between devices: 1.44 us -> 0.01 us  [solve(): lax.ppermute(one, 'rhs', ahead)]
  transfers between devices with their start and end apart: 25 -> 27, of which waited for: 13 -> 12; matrix products, arithmetic and copies ran while one was open for 2% -> 2% of each run, Pallas kernels for 14% -> 14%
where the time goes in v6:
time: 136 us
  waiting for transfers between devices  63.9 us (47%)
  starting transfers between devices  37.4 us (28%)
  Pallas kernels  27 us (20%)
  matrix products  3.84 us (3%)
  local copies, waits for them, and re-layouts  2.87 us (2%)
    ppermute x5, waiting for transfers between devices, top_factors(): got = lax.ppermute(message, 'leaf', pairs)  30.7 us
    pallas_call x16, Pallas kernels, kernel_call(): pl.pallas_call(body, out_shape=out_shape, cost_estimate=pl.CostEstimate(f...  21.7 us
    ppermute x4, waiting for transfers between devices, solve(): left = [lax.ppermute(a, 'rhs', ahead) for a in own]  16.3 us
    ppermute x4, starting transfers between devices, solve(): right = [lax.ppermute(a, 'rhs', behind) for a in own]  15 us
    ppermute x7, starting transfers between devices, partners(): lax.ppermute(value, 'leaf', [(i, i ^ m) for i in range(leaf_total)])  8.42 us
    ppermute x4, waiting for transfers between devices, solve(): right = [lax.ppermute(a, 'rhs', behind) for a in own]  7.28 us
    ppermute x5, starting transfers between devices, top_factors(): got = lax.ppermute(message, 'leaf', pairs)  7.22 us
    pallas_call x4, Pallas kernels, near_call(): pl.pallas_call(near_body, grid_spec=pltpu.PrefetchScalarGridSpec(num_scal...  5.32 us
  transfers between devices with their start and end apart: 27, of which 12 were waited for; matrix products, arithmetic and copies ran while one was open for 2% of the time, Pallas kernels for 14%

profile of v6, /device:TPU:0, one launch (start us, length us, event | category | flops | bytes accessed | tf_op | source)
XLA Modules:
  0.0 135.9 jit_solution(3568107915627622249)
XLA Ops:
  8.6 5.4 %collective-permute-done.14.got = f32[128,256]{1,0:T(8,128)S(1)} collective-permute-done((f32[128,256]{1,0:T(8,128)S(1)}, f32[128,256]{1,0:T(8,128)S(1)}, u32[]{:S(2)}, u32[]{:S(2)}) %collective-permute-start.14) | collective-permute-done | bytes 131104 | tf_op jit(solution)/shard_map/ppermute | solution.py:386
  14.6 2.0 %collective-permute-start.16 = (f32[128,896]{1,0:T(8,128)S(1)}, f32[128,896]{1,0:T(8,128)S(1)}, u32[]{:S(2)}, u32[]{:S(2)}) collective-permute-start(f32[128,896]{1,0:T(8,128)S(1)} %get-tuple-element.68), channel_id=1, source_target_pairs={{0,32},{32,0},{64,96},{96,64},{1,33},{33,1},{65,97},{97,65},{2,34}... | collective-permute-start | bytes 1376264 | tf_op jit(solution)/shard_map/ppermute | solution.py:386
  16.6 8.4 %collective-permute-done.16.got = f32[128,896]{1,0:T(8,128)S(1)} collective-permute-done((f32[128,896]{1,0:T(8,128)S(1)}, f32[128,896]{1,0:T(8,128)S(1)}, u32[]{:S(2)}, u32[]{:S(2)}) %collective-permute-start.16) | collective-permute-done | bytes 458784 | tf_op jit(solution)/shard_map/ppermute | solution.py:386
  25.6 1.9 %collective-permute-start.17 = (f32[128,1152]{1,0:T(8,128)S(1)}, f32[128,1152]{1,0:T(8,128)S(1)}, u32[]{:S(2)}, u32[]{:S(2)}) collective-permute-start(f32[128,1152]{1,0:T(8,128)S(1)} %get-tuple-element.70), channel_id=1, source_target_pairs={{0,16},{16,0},{32,48},{48,32},{64,80},{80,64},{96,112},{112,96},{1... | collective-permute-start | bytes 1769480 | tf_op jit(solution)/shard_map/ppermute | solution.py:386
  27.6 11.4 %collective-permute-done.17.got = f32[128,1152]{1,0:T(8,128)S(1)} collective-permute-done((f32[128,1152]{1,0:T(8,128)S(1)}, f32[128,1152]{1,0:T(8,128)S(1)}, u32[]{:S(2)}, u32[]{:S(2)}) %collective-permute-start.17) | collective-permute-done | bytes 589856 | tf_op jit(solution)/shard_map/ppermute | solution.py:386
  41.6 4.2 %collective-permute-start.12 = (bf16[4,128,512]{2,1,0:T(8,128)(2,1)S(1)}, bf16[4,128,512]{2,1,0:T(8,128)(2,1)S(1)}, u32[]{:S(2)}, u32[]{:S(2)}) collective-permute-start(bf16[4,128,512]{2,1,0:T(8,128)(2,1)S(1)} %slice.54), channel_id=1, source_target_pairs={{0,3},{1,0},{2,1},{3,2},{4,7},{5,4},{6,5},{7,6},{8,11},{9,8},{10,9... | collective-permute-start | bytes 1572872 | tf_op jit(solution)/shard_map/ppermute | solution.py:435
  46.1 3.3 %collective-permute-start.2 = (bf16[4,128,512]{2,1,0:T(8,128)(2,1)S(1)}, bf16[4,128,512]{2,1,0:T(8,128)(2,1)S(1)}, u32[]{:S(2)}, u32[]{:S(2)}) collective-permute-start(bf16[4,128,512]{2,1,0:T(8,128)(2,1)S(1)} %get-tuple-element.110), channel_id=1, source_target_pairs={{0,3},{1,0},{2,1},{3,2},{4,7},{5,4},{6,5},{7,6},{8,11},{9,8},{10,9... | collective-permute-start | bytes 1572872 | tf_op jit(solution)/shard_map/ppermute | solution.py:435
  49.4 5.6 %collective-permute-done.18.got = f32[128,1792]{1,0:T(8,128)S(1)} collective-permute-done((f32[128,1792]{1,0:T(8,128)S(1)}, f32[128,1792]{1,0:T(8,128)S(1)}, u32[]{:S(2)}, u32[]{:S(2)}) %collective-permute-start.18) | collective-permute-done | bytes 917536 | tf_op jit(solution)/shard_map/ppermute | solution.py:386
  55.8 4.2 %collective-permute-start.10 = (bf16[4,128,512]{2,1,0:T(8,128)(2,1)S(1)}, bf16[4,128,512]{2,1,0:T(8,128)(2,1)S(1)}, u32[]{:S(2)}, u32[]{:S(2)}) collective-permute-start(bf16[4,128,512]{2,1,0:T(8,128)(2,1)S(1)} %get-tuple-element.109), channel_id=1, source_target_pairs={{0,3},{1,0},{2,1},{3,2},{4,7},{5,4},{6,5},{7,6},{8,11},{9,8},{10,9... | collective-permute-start | bytes 1572872 | tf_op jit(solution)/shard_map/ppermute | solution.py:435
  61.8 3.2 %collective-permute-start.4 = (bf16[4,128,512]{2,1,0:T(8,128)(2,1)S(1)}, bf16[4,128,512]{2,1,0:T(8,128)(2,1)S(1)}, u32[]{:S(2)}, u32[]{:S(2)}) collective-permute-start(bf16[4,128,512]{2,1,0:T(8,128)(2,1)S(1)} %get-tuple-element.111), channel_id=1, source_target_pairs={{0,3},{1,0},{2,1},{3,2},{4,7},{5,4},{6,5},{7,6},{8,11},{9,8},{10,9... | collective-permute-start | bytes 1572872 | tf_op jit(solution)/shard_map/ppermute | solution.py:435
  65.1 7.3 %collective-permute-done.10.right = bf16[4,128,512]{2,1,0:T(8,128)(2,1)S(1)} collective-permute-done((bf16[4,128,512]{2,1,0:T(8,128)(2,1)S(1)}, bf16[4,128,512]{2,1,0:T(8,128)(2,1)S(1)}, u32[]{:S(2)}, u32[]{:S(2)}) %collective-permute-start.10) | collective-permute-done | bytes 524320 | tf_op jit(solution)/shard_map/ppermute | solution.py:435
  72.7 3.3 %collective-permute-done.left = bf16[4,128,512]{2,1,0:T(8,128)(2,1)S(1)} collective-permute-done((bf16[4,128,512]{2,1,0:T(8,128)(2,1)S(1)}, bf16[4,128,512]{2,1,0:T(8,128)(2,1)S(1)}, u32[]{:S(2)}, u32[]{:S(2)}) %collective-permute-start) | collective-permute-done | bytes 524320 | tf_op jit(solution)/shard_map/ppermute | solution.py:434
  76.1 11.2 %collective-permute-done.5.left = bf16[4,128,512]{2,1,0:T(8,128)(2,1)S(1)} collective-permute-done((bf16[4,128,512]{2,1,0:T(8,128)(2,1)S(1)}, bf16[4,128,512]{2,1,0:T(8,128)(2,1)S(1)}, u32[]{:S(2)}, u32[]{:S(2)}) %collective-permute-start.5) | collective-permute-done | bytes 524320 | tf_op jit(solution)/shard_map/ppermute | solution.py:434
  87.3 2.0 %collective-permute-start.6 = (bf16[2,128,512]{2,1,0:T(8,128)(2,1)S(1)}, bf16[2,128,512]{2,1,0:T(8,128)(2,1)S(1)}, u32[]{:S(2)}, u32[]{:S(2)}) collective-permute-start(bf16[2,128,512]{2,1,0:T(8,128)(2,1)S(1)} %get-tuple-element.114), channel_id=1, source_target_pairs={{0,1},{1,2},{2,3},{3,0},{4,5},{5,6},{6,7},{7,4},{8,9},{9,10},{10,1... | collective-permute-start | bytes 786440 | tf_op jit(solution)/shard_map/ppermute | solution.py:438
  89.3 2.7 %shard_map.130 = (f32[8,128,256]{2,1,0:T(8,128)S(1)}, f32[16,128,128]{2,1,0:T(8,128)S(1)}) custom-call(f32[15,256,256]{2,1,0:T(8,128)S(1)} %copy-done.4, f32[15,256,128]{2,1,0:T(8,128)S(1)} %copy-done.6, f32[15,256,128]{2,1,0:T(8,128)S(1)} %copy-done.5, f32[15,128,128]{2,1,0:T(8,128)S(1)} %copy-done.8), custom_call_target="tpu_custom_call" | custom-call | flops 800000000 | bytes 8847360 | tf_op jit(solution)/shard_map/pallas_call | solution.py:45
  94.8 5.1 %collective-permute-done.7.far_b = bf16[2,128,512]{2,1,0:T(8,128)(2,1)S(1)} collective-permute-done((bf16[2,128,512]{2,1,0:T(8,128)(2,1)S(1)}, bf16[2,128,512]{2,1,0:T(8,128)(2,1)S(1)}, u32[]{:S(2)}, u32[]{:S(2)}) %collective-permute-start.7) | collective-permute-done | bytes 262176 | tf_op jit(solution)/shard_map/ppermute | solution.py:438
  99.9 3.7 %collective-permute-start.3 = (bf16[2,128,512]{2,1,0:T(8,128)(2,1)S(1)}, bf16[2,128,512]{2,1,0:T(8,128)(2,1)S(1)}, u32[]{:S(2)}, u32[]{:S(2)}) collective-permute-start(bf16[2,128,512]{2,1,0:T(8,128)(2,1)S(1)} %get-tuple-element.113), channel_id=1, source_target_pairs={{0,3},{1,0},{2,1},{3,2},{4,7},{5,4},{6,5},{7,6},{8,11},{9,8},{10,9... | collective-permute-start | bytes 786440 | tf_op jit(solution)/shard_map/ppermute | solution.py:438
  109.0 2.4 %shard_map.134 = (f32[7,128,128]{2,1,0:T(8,128)S(1)}, f32[7,256,128]{2,1,0:T(8,128)S(1)}) custom-call(f32[8,128,128]{2,1,0:T(8,128)S(1)} %get-tuple-element.66.lead, f32[15,256,256]{2,1,0:T(8,128)S(1)} %copy-done.4, f32[15,256,128]{2,1,0:T(8,128)S(1)} %copy-done.6, f32[15,256,128]{2,1,0:T(8,128)S(1)} %copy-done.5, f32[15,128,128]{2,1,0:T(8,128)S(1)} %copy-done.8), custom_call_target="tpu_custom_call" | custom-call | flops 700000000 | bytes 9371648 | tf_op jit(solution)/shard_map/pallas_call | solution.py:45
  113.3 2.0 %shard_map.140 = (bf16[4,128,128]{2,1,0:T(8,128)(2,1)S(1)}, f32[4,128,128]{2,1,0:T(8,128)S(1)}, f32[4,128,128]{2,1,0:T(8,128)S(1)}, f32[7,128,128]{2,1,0:T(8,128)S(1)}, f32[128,128]{1,0:T(8,128)S(1)}) custom-call(s32[2]{0:T(128)S(1)} %pad_add_fusion.row_ref.spot, bf16[2,128,512]{2,1,0:T(8,128)(2,1)S(1)} %collective-permute-done.1.far_a, ...), custom_call_target="tpu_custom_call" | custom-call | flops 400000000 | bytes 8060936 | tf_op jit(solution)/shard_map/pallas_call | solution.py:45
  116.9 2.1 %collective-permute-start.22 = (f32[128,128]{1,0:T(8,128)S(1)}, f32[128,128]{1,0:T(8,128)S(1)}, u32[]{:S(2)}, u32[]{:S(2)}) collective-permute-start(f32[128,128]{1,0:T(8,128)S(1)} %shard_map.141.refs_2_.refs_0_), channel_id=1, source_target_pairs={{0,16},{4,20},{8,24},{12,28},{16,0},{20,4},{24,8},{28,12},{32,48},... | collective-permute-start | bytes 196616 | tf_op jit(solution)/shard_map/ppermute | solution.py:528
  119.0 2.0 %collective-permute-start.21 = (f32[128,128]{1,0:T(8,128)S(1)}, f32[128,128]{1,0:T(8,128)S(1)}, u32[]{:S(2)}, u32[]{:S(2)}) collective-permute-start(f32[128,128]{1,0:T(8,128)S(1)} %shard_map.141.refs_2_.refs_0_), channel_id=1, source_target_pairs={{0,8},{4,12},{8,0},{12,4},{16,24},{20,28},{24,16},{28,20},{32,40},... | collective-permute-start | bytes 196616 | tf_op jit(solution)/shard_map/ppermute | solution.py:528
  121.0 2.7 %collective-permute-done.23.refs_5_.refs_3_ = f32[128,128]{1,0:T(8,128)S(1)} collective-permute-done((f32[128,128]{1,0:T(8,128)S(1)}, f32[128,128]{1,0:T(8,128)S(1)}, u32[]{:S(2)}, u32[]{:S(2)}) %collective-permute-start.23) | collective-permute-done | bytes 65568 | tf_op jit(solution)/shard_map/ppermute | solution.py:528
  126.7 2.0 %collective-permute-start.24 = (f32[128,128]{1,0:T(8,128)S(1)}, f32[128,128]{1,0:T(8,128)S(1)}, u32[]{:S(2)}, u32[]{:S(2)}) collective-permute-start(f32[128,128]{1,0:T(8,128)S(1)} %shard_map.143.here), channel_id=1, source_target_pairs={{0,32},{4,36},{8,40},{12,44},{16,48},{20,52},{24,56},{28,60},{32,0... | collective-permute-start | bytes 196616 | tf_op jit(solution)/shard_map/ppermute | solution.py:528
  132.0 3.7 %shard_map.146 = f32[8192,128]{1,0:T(8,128)} custom-call(s32[2]{0:T(128)S(1)} %pad_add_fusion.row_ref.spot, f32[128,512]{1,0:T(8,128)S(1)} %get-tuple-element.82.down_y, f32[128,128]{1,0:T(8,128)S(1)} %shard_map.142.below, f32[128,128]{1,0:T(8,128)S(1)} %shard_map.143.here, f32[128,128]{1,0:T(8,128)S(1)} %collective-permute-done.24.one, ...), custom_call_target="tpu_custom_call" | custom-call | flops 1000000000 | bytes 6881288 | tf_op jit(solution)/shard_map/pallas_call | solution.py:45
  (84 shorter events, 33.4 us)
Async XLA Ops:
  5.7 8.4 %collective-permute-start.14 = (f32[128,256]{1,0:T(8,128)S(1)}, f32[128,256]{1,0:T(8,128)S(1)}, u32[]{:S(2)}, u32[]{:S(2)}) collective-permute-start(f32[128,256]{1,0:T(8,128)S(1)} %get-tuple-element.121), channel_id=1, source_target_pairs={{64,0},{65,1},{66,2},{67,3}} | collective-permute-start | bytes 393224 | tf_op jit(solution)/shard_map/ppermute | solution.py:386
  14.6 10.4 %collective-permute-start.16 = (f32[128,896]{1,0:T(8,128)S(1)}, f32[128,896]{1,0:T(8,128)S(1)}, u32[]{:S(2)}, u32[]{:S(2)}) collective-permute-start(f32[128,896]{1,0:T(8,128)S(1)} %get-tuple-element.68), channel_id=1, source_target_pairs={{0,32},{32,0},{64,96},{96,64},{1,33},{33,1},{65,97},{97,65},{2,34}... | collective-permute-start | bytes 1376264 | tf_op jit(solution)/shard_map/ppermute | solution.py:386
  25.6 13.3 %collective-permute-start.17 = (f32[128,1152]{1,0:T(8,128)S(1)}, f32[128,1152]{1,0:T(8,128)S(1)}, u32[]{:S(2)}, u32[]{:S(2)}) collective-permute-start(f32[128,1152]{1,0:T(8,128)S(1)} %get-tuple-element.70), channel_id=1, source_target_pairs={{0,16},{16,0},{32,48},{48,32},{64,80},{80,64},{96,112},{112,96},{1... | collective-permute-start | bytes 1769480 | tf_op jit(solution)/shard_map/ppermute | solution.py:386
  39.7 15.3 %collective-permute-start.18 = (f32[128,1792]{1,0:T(8,128)S(1)}, f32[128,1792]{1,0:T(8,128)S(1)}, u32[]{:S(2)}, u32[]{:S(2)}) collective-permute-start(f32[128,1792]{1,0:T(8,128)S(1)} %get-tuple-element.72), channel_id=1, source_target_pairs={{0,8},{8,0},{16,24},{24,16},{32,40},{40,32},{48,56},{56,48},{64,72... | collective-permute-start | bytes 2752520 | tf_op jit(solution)/shard_map/ppermute | solution.py:386
  41.6 14.2 %collective-permute-start.12 = (bf16[4,128,512]{2,1,0:T(8,128)(2,1)S(1)}, bf16[4,128,512]{2,1,0:T(8,128)(2,1)S(1)}, u32[]{:S(2)}, u32[]{:S(2)}) collective-permute-start(bf16[4,128,512]{2,1,0:T(8,128)(2,1)S(1)} %slice.54), channel_id=1, source_target_pairs={{0,3},{1,0},{2,1},{3,2},{4,7},{5,4},{6,5},{7,6},{8,11},{9,8},{10,9... | collective-permute-start | bytes 1572872 | tf_op jit(solution)/shard_map/ppermute | solution.py:435
  45.8 14.3 %collective-permute-start.8 = (bf16[4,128,512]{2,1,0:T(8,128)(2,1)S(1)}, bf16[4,128,512]{2,1,0:T(8,128)(2,1)S(1)}, u32[]{:S(2)}, u32[]{:S(2)}) collective-permute-start(bf16[4,128,512]{2,1,0:T(8,128)(2,1)S(1)} %slice.54), channel_id=1, source_target_pairs={{0,1},{1,2},{2,3},{3,0},{4,5},{5,6},{6,7},{7,4},{8,9},{9,10},{10,1... | collective-permute-start | bytes 1572872 | tf_op jit(solution)/shard_map/ppermute | solution.py:434
  46.0 15.8 %collective-permute-start.13 = (bf16[4,128,512]{2,1,0:T(8,128)(2,1)S(1)}, bf16[4,128,512]{2,1,0:T(8,128)(2,1)S(1)}, u32[]{:S(2)}, u32[]{:S(2)}) collective-permute-start(bf16[4,128,512]{2,1,0:T(8,128)(2,1)S(1)} %get-tuple-element.109), channel_id=1, source_target_pairs={{0,1},{1,2},{2,3},{3,0},{4,5},{5,6},{6,7},{7,4},{8,9},{9,10},{10,1... | collective-permute-start | bytes 1572872 | tf_op jit(solution)/shard_map/ppermute | solution.py:434
  46.1 15.7 %collective-permute-start.2 = (bf16[4,128,512]{2,1,0:T(8,128)(2,1)S(1)}, bf16[4,128,512]{2,1,0:T(8,128)(2,1)S(1)}, u32[]{:S(2)}, u32[]{:S(2)}) collective-permute-start(bf16[4,128,512]{2,1,0:T(8,128)(2,1)S(1)} %get-tuple-element.110), channel_id=1, source_target_pairs={{0,3},{1,0},{2,1},{3,2},{4,7},{5,4},{6,5},{7,6},{8,11},{9,8},{10,9... | collective-permute-start | bytes 1572872 | tf_op jit(solution)/shard_map/ppermute | solution.py:435
  55.7 55.7 %collective-permute-start.19 = (f32[128,2688]{1,0:T(8,128)S(1)}, f32[128,2688]{1,0:T(8,128)S(1)}, u32[]{:S(2)}, u32[]{:S(2)}) collective-permute-start(f32[128,2688]{1,0:T(8,128)S(1)} %get-tuple-element.74), channel_id=1, source_target_pairs={{0,4},{4,0},{8,12},{12,8},{16,20},{20,16},{24,28},{28,24},{32,36},... | collective-permute-start | bytes 4128776 | tf_op jit(solution)/shard_map/ppermute | solution.py:386
  55.8 16.5 %collective-permute-start.10 = (bf16[4,128,512]{2,1,0:T(8,128)(2,1)S(1)}, bf16[4,128,512]{2,1,0:T(8,128)(2,1)S(1)}, u32[]{:S(2)}, u32[]{:S(2)}) collective-permute-start(bf16[4,128,512]{2,1,0:T(8,128)(2,1)S(1)} %get-tuple-element.109), channel_id=1, source_target_pairs={{0,3},{1,0},{2,1},{3,2},{4,7},{5,4},{6,5},{7,6},{8,11},{9,8},{10,9... | collective-permute-start | bytes 1572872 | tf_op jit(solution)/shard_map/ppermute | solution.py:435
  60.1 16.0 %collective-permute-start = (bf16[4,128,512]{2,1,0:T(8,128)(2,1)S(1)}, bf16[4,128,512]{2,1,0:T(8,128)(2,1)S(1)}, u32[]{:S(2)}, u32[]{:S(2)}) collective-permute-start(bf16[4,128,512]{2,1,0:T(8,128)(2,1)S(1)} %get-tuple-element.111), channel_id=1, source_target_pairs={{0,1},{1,2},{2,3},{3,0},{4,5},{5,6},{6,7},{7,4},{8,9},{9,10},{10,1... | collective-permute-start | bytes 1572872 | tf_op jit(solution)/shard_map/ppermute | solution.py:434
  61.8 25.5 %collective-permute-start.5 = (bf16[4,128,512]{2,1,0:T(8,128)(2,1)S(1)}, bf16[4,128,512]{2,1,0:T(8,128)(2,1)S(1)}, u32[]{:S(2)}, u32[]{:S(2)}) collective-permute-start(bf16[4,128,512]{2,1,0:T(8,128)(2,1)S(1)} %get-tuple-element.110), channel_id=1, source_target_pairs={{0,1},{1,2},{2,3},{3,0},{4,5},{5,6},{6,7},{7,4},{8,9},{9,10},{10,1... | collective-permute-start | bytes 1572872 | tf_op jit(solution)/shard_map/ppermute | solution.py:434
  61.8 25.5 %collective-permute-start.4 = (bf16[4,128,512]{2,1,0:T(8,128)(2,1)S(1)}, bf16[4,128,512]{2,1,0:T(8,128)(2,1)S(1)}, u32[]{:S(2)}, u32[]{:S(2)}) collective-permute-start(bf16[4,128,512]{2,1,0:T(8,128)(2,1)S(1)} %get-tuple-element.111), channel_id=1, source_target_pairs={{0,3},{1,0},{2,1},{3,2},{4,7},{5,4},{6,5},{7,6},{8,11},{9,8},{10,9... | collective-permute-start | bytes 1572872 | tf_op jit(solution)/shard_map/ppermute | solution.py:435
  72.4 35.2 %collective-permute-start.9 = (bf16[4,128,512]{2,1,0:T(8,128)(2,1)S(1)}, bf16[4,128,512]{2,1,0:T(8,128)(2,1)S(1)}, u32[]{:S(2)}, u32[]{:S(2)}) collective-permute-start(bf16[4,128,512]{2,1,0:T(8,128)(2,1)S(1)} %collective-permute-done.8.left), channel_id=1, source_target_pairs={{0,1},{1,2},{2,3},{3,0},{4,5},{5,6},{6,7},{7,4},{8,9},{9,10},{10,1... | collective-permute-start | bytes 1572872 | tf_op jit(solution)/shard_map/ppermute | solution.py:438
  76.1 31.5 %collective-permute-start.11 = (bf16[4,128,512]{2,1,0:T(8,128)(2,1)S(1)}, bf16[4,128,512]{2,1,0:T(8,128)(2,1)S(1)}, u32[]{:S(2)}, u32[]{:S(2)}) collective-permute-start(bf16[4,128,512]{2,1,0:T(8,128)(2,1)S(1)} %collective-permute-done.10.right), channel_id=1, source_target_pairs={{0,3},{1,0},{2,1},{3,2},{4,7},{5,4},{6,5},{7,6},{8,11},{9,8},{10,9... | collective-permute-start | bytes 1572872 | tf_op jit(solution)/shard_map/ppermute | solution.py:438
  87.3 12.6 %collective-permute-start.7 = (bf16[2,128,512]{2,1,0:T(8,128)(2,1)S(1)}, bf16[2,128,512]{2,1,0:T(8,128)(2,1)S(1)}, u32[]{:S(2)}, u32[]{:S(2)}) collective-permute-start(bf16[2,128,512]{2,1,0:T(8,128)(2,1)S(1)} %get-tuple-element.112), channel_id=1, source_target_pairs={{0,3},{1,0},{2,1},{3,2},{4,7},{5,4},{6,5},{7,6},{8,11},{9,8},{10,9... | collective-permute-start | bytes 786440 | tf_op jit(solution)/shard_map/ppermute | solution.py:438
  87.3 16.3 %collective-permute-start.6 = (bf16[2,128,512]{2,1,0:T(8,128)(2,1)S(1)}, bf16[2,128,512]{2,1,0:T(8,128)(2,1)S(1)}, u32[]{:S(2)}, u32[]{:S(2)}) collective-permute-start(bf16[2,128,512]{2,1,0:T(8,128)(2,1)S(1)} %get-tuple-element.114), channel_id=1, source_target_pairs={{0,1},{1,2},{2,3},{3,0},{4,5},{5,6},{6,7},{7,4},{8,9},{9,10},{10,1... | collective-permute-start | bytes 786440 | tf_op jit(solution)/shard_map/ppermute | solution.py:438
  99.9 13.4 %collective-permute-start.3 = (bf16[2,128,512]{2,1,0:T(8,128)(2,1)S(1)}, bf16[2,128,512]{2,1,0:T(8,128)(2,1)S(1)}, u32[]{:S(2)}, u32[]{:S(2)}) collective-permute-start(bf16[2,128,512]{2,1,0:T(8,128)(2,1)S(1)} %get-tuple-element.113), channel_id=1, source_target_pairs={{0,3},{1,0},{2,1},{3,2},{4,7},{5,4},{6,5},{7,6},{8,11},{9,8},{10,9... | collective-permute-start | bytes 786440 | tf_op jit(solution)/shard_map/ppermute | solution.py:438
  103.6 9.7 %collective-permute-start.1 = (bf16[2,128,512]{2,1,0:T(8,128)(2,1)S(1)}, bf16[2,128,512]{2,1,0:T(8,128)(2,1)S(1)}, u32[]{:S(2)}, u32[]{:S(2)}) collective-permute-start(bf16[2,128,512]{2,1,0:T(8,128)(2,1)S(1)} %get-tuple-element.115), channel_id=1, source_target_pairs={{0,1},{1,2},{2,3},{3,0},{4,5},{5,6},{6,7},{7,4},{8,9},{9,10},{10,1... | collective-permute-start | bytes 786440 | tf_op jit(solution)/shard_map/ppermute | solution.py:438
  116.8 6.8 %collective-permute-start.23 = (f32[128,128]{1,0:T(8,128)S(1)}, f32[128,128]{1,0:T(8,128)S(1)}, u32[]{:S(2)}, u32[]{:S(2)}) collective-permute-start(f32[128,128]{1,0:T(8,128)S(1)} %shard_map.141.refs_2_.refs_0_), channel_id=1, source_target_pairs={{0,24},{4,28},{8,16},{12,20},{16,8},{20,12},{24,0},{28,4},{32,56},... | collective-permute-start | bytes 196616 | tf_op jit(solution)/shard_map/ppermute | solution.py:528
  116.9 6.8 %collective-permute-start.22 = (f32[128,128]{1,0:T(8,128)S(1)}, f32[128,128]{1,0:T(8,128)S(1)}, u32[]{:S(2)}, u32[]{:S(2)}) collective-permute-start(f32[128,128]{1,0:T(8,128)S(1)} %shard_map.141.refs_2_.refs_0_), channel_id=1, source_target_pairs={{0,16},{4,20},{8,24},{12,28},{16,0},{20,4},{24,8},{28,12},{32,48},... | collective-permute-start | bytes 196616 | tf_op jit(solution)/shard_map/ppermute | solution.py:528
  124.5 7.5 %collective-permute-start.26 = (f32[128,128]{1,0:T(8,128)S(1)}, f32[128,128]{1,0:T(8,128)S(1)}, u32[]{:S(2)}, u32[]{:S(2)}) collective-permute-start(f32[128,128]{1,0:T(8,128)S(1)} %shard_map.143.here), channel_id=1, source_target_pairs={{0,96},{4,100},{8,104},{12,108},{16,112},{20,116},{24,120},{28,124... | collective-permute-start | bytes 196616 | tf_op jit(solution)/shard_map/ppermute | solution.py:528
  126.0 6.0 %collective-permute-start.25 = (f32[128,128]{1,0:T(8,128)S(1)}, f32[128,128]{1,0:T(8,128)S(1)}, u32[]{:S(2)}, u32[]{:S(2)}) collective-permute-start(f32[128,128]{1,0:T(8,128)S(1)} %shard_map.143.here), channel_id=1, source_target_pairs={{0,64},{4,68},{8,72},{12,76},{16,80},{20,84},{24,88},{28,92},{32,9... | collective-permute-start | bytes 196616 | tf_op jit(solution)/shard_map/ppermute | solution.py:528
  126.7 5.3 %collective-permute-start.24 = (f32[128,128]{1,0:T(8,128)S(1)}, f32[128,128]{1,0:T(8,128)S(1)}, u32[]{:S(2)}, u32[]{:S(2)}) collective-permute-start(f32[128,128]{1,0:T(8,128)S(1)} %shard_map.143.here), channel_id=1, source_target_pairs={{0,32},{4,36},{8,40},{12,44},{16,48},{20,52},{24,56},{28,60},{32,0... | collective-permute-start | bytes 196616 | tf_op jit(solution)/shard_map/ppermute | solution.py:528
  (14 other events, 214.0 us)

commit v7 on v6

--- a/solution.py
+++ b/solution.py
@@ -11,7 +11,7 @@
 wide = jnp.float32
 narrow = jnp.bfloat16
 
-GROUPS = (tuple(range(8)), (8, 9, 12, 13), (10, 11, 14, 15))
+GROUPS = ((0, 8), (8, 8))
 PIECES = ((0, 4), (4, 4), (8, 4), (12, 4))
 MERGED = (0, 1, 2, 3, 8, 9, 12)
 LATE = (4, 5, 6, 7, 10, 11, 13, 14)
@@ -110,33 +110,32 @@
 def far_leaves(
     group, row_ref, far_a, far_b, rhs, basis, coarse, part_a, part_b, vals, proj, lead
 ):
-    leaves = GROUPS[group]
+    start, count = GROUPS[group]
     height, width = far_a.shape[1], far_a.shape[2]
-    half = len(leaves) // 2
+    half = count // 2
     at = turned(row_ref, 2, height)
-    for k, leaf in enumerate(leaves):
+    for k in range(count):
+        leaf = start + k
         rows = far_a[k] if k < half else far_b[k - half]
         got = narrow_dot(rows, rhs[leaf * width : (leaf + 1) * width, :])
         vals[k] = got.astype(narrow)
-    for k, leaf in enumerate(leaves):
-        before = (part_a if k < half else part_b)[leaf % 4]
+    for k in range(count):
+        before = part_a[k] if k < half else part_b[k - half]
         proj[k] = before + lax.dot_general(
-            basis[leaf, pl.ds(at, height), :], vals[k], FRONT, preferred_element_type=wide
+            basis[start + k, pl.ds(at, height), :], vals[k], FRONT, preferred_element_type=wide
         )
-    for k, leaf in enumerate(leaves):
-        lead[k] = split_dot(coarse[leaf], proj[k])
+    for k in range(count):
+        lead[k] = split_dot(coarse[start + k], proj[k])
 
 
 def last_body(
-    row_ref, far_a, far_b, rhs, basis, coarse, part_a, part_b, lead1, ups, early,
+    row_ref, far_a, far_b, rhs, basis, coarse, part_a, part_b, ups, early,
     vals, proj, lead, late, up,
 ):
     far_leaves(
-        2, row_ref, far_a, far_b, rhs, basis, coarse, part_a, part_b, vals, proj, lead
-    )
-    value = {
-        leaf: (ref, k) for g, ref in ((1, lead1), (2, lead)) for k, leaf in enumerate(GROUPS[g])
-    }
+        1, row_ref, far_a, far_b, rhs, basis, coarse, part_a, part_b, vals, proj, lead
+    )
+    value = {8 + k: (lead, k) for k in range(8)}
     for k, node in enumerate(MERGED):
         value[16 + node] = (early, k)
     for k, node in enumerate(LATE):
@@ -193,10 +192,8 @@
                 paths[2 * node + k] = value[2 * node + k]
 
 
-def late_body(lead1, lead2, late, early, inv, basis, back, base):
-    value = {
-        leaf: (ref, k) for g, ref in ((1, lead1), (2, lead2)) for k, leaf in enumerate(GROUPS[g])
-    }
+def late_body(lead, late, early, inv, basis, back, base):
+    value = {8 + k: (lead, k) for k in range(8)}
     for k, node in enumerate(MERGED):
         value[16 + node] = (early, k)
     for k, node in enumerate(LATE[:-1]):
@@ -211,17 +208,13 @@
         base[k] -= split_dot(back[node], reduced[k])
 
 
-def known_body(base0, base1, back, proj0, proj1, proj2, rest):
+def known_body(base0, base1, back, proj0, proj1, rest):
     rank = proj0.shape[1]
     known = {}
     for base, nodes in ((base0, MERGED), (base1, LATE)):
         for k, node in enumerate(nodes):
             known[node] = (base, k)
-    projs = {
-        leaf: (ref, k)
-        for ref, leaves in zip((proj0, proj1, proj2), GROUPS)
-        for k, leaf in enumerate(leaves)
-    }
+    projs = [(proj, k) for proj in (proj0, proj1) for k in range(proj.shape[0])]
     part = {30: None}
     for node in reversed(range(15)):
         ref, at = known[node]
@@ -313,7 +306,7 @@
 
 def out_body(
     row_ref, down_y, below, here, one, two, three, paths, rest, back,
-    near0, near1, near2, near3, far0, far1, far2, out, blocks, sent,
+    near0, near1, near2, near3, far0, far1, out, blocks, sent,
 ):
     leaves, width = back.shape[0], back.shape[1]
     height = far0.shape[1]
@@ -322,24 +315,15 @@
     at = [turned(row_ref, part, height) for part in (0, 3, 1, 2)]
     spans = zip(PIECES, (near0, near1, near2, near3))
     nears = [(ref, k) for (_, count), ref in spans for k in range(count)]
-    fars = {
-        leaf: (ref, k)
-        for ref, group in zip((far0, far1, far2), GROUPS)
-        for k, leaf in enumerate(group)
-    }
+    fars = [(ref, k) for (_, count), ref in zip(GROUPS, (far0, far1)) for k in range(count)]
     copies = [
         pltpu.make_async_copy(
             blocks.at[leaf], out.at[pl.ds(leaf * width, width), :], sent.at[leaf]
         )
         for leaf in range(leaves)
     ]
-    rank, some = top.shape[0], 4
     for leaf in range(leaves):
-        k = leaf % some
-        if k == 0:
-            these = paths[leaf : leaf + some].reshape(some * rank, rank)
-            down = split_dot(these, top)
-        difference = (rest[leaf] - down[k * rank : (k + 1) * rank]).astype(narrow)
+        difference = (rest[leaf] - split_dot(paths[leaf], top)).astype(narrow)
         matching = jnp.concatenate([back[leaf, pl.ds(a, height), :] for a in at], axis=0)
         change = narrow_dot(matching, difference)
         near, far = nears[leaf], fars[leaf]
@@ -351,9 +335,7 @@
             blocks[leaf, pl.ds(a, height), :] = (
                 block.astype(wide) - change[j * height : (j + 1) * height]
             )
-        if leaf:
-            copies[leaf - 1].start()
-    copies[-1].start()
+        copies[leaf].start()
     for copy in copies:
         copy.wait()
 
@@ -433,7 +415,7 @@
             whole, own[0], row = lax.optimization_barrier((whole, own[0], row))
     left = [lax.ppermute(a, "rhs", ahead) for a in own]
     right = [lax.ppermute(a, "rhs", behind) for a in own]
-    pairs = ((left[0], right[1]), (left[2][:2], right[3][:2]), (left[2][2:], right[3][2:]))
+    pairs = ((left[0], right[1]), (left[2], right[3]))
     far = [
         (lax.ppermute(one, "rhs", ahead), lax.ppermute(two, "rhs", behind))
         for one, two in pairs
@@ -470,16 +452,9 @@
     shared = (rhs_cols, leaf_basis, leaf_coarse)
     first = kernel_call(
         functools.partial(far_leaves, 0),
-        far_shapes(len(GROUPS[0]), height, rank, columns),
+        far_shapes(GROUPS[0][1], height, rank, columns),
         3 * 10**8,
         (row, *far[0], *shared, *parts[:2]),
-        scalars=1,
-    )
-    second = kernel_call(
-        functools.partial(far_leaves, 1),
-        far_shapes(len(GROUPS[1]), height, rank, columns),
-        15 * 10**7,
-        (row, *far[1], *shared, *parts[2:]),
         scalars=1,
     )
     early, early_base = kernel_call(
@@ -493,34 +468,34 @@
         room=12,
     )
     final = lax.optimization_barrier(
-        (far[2], parts[2:], second[2], ups, early, up_first, down_first, up_x, down_x, down_y, paths)
+        (far[1], parts[2:], ups, early, up_first, down_first, up_x, down_x, down_y, paths)
     )
     (
-        last_far, last_parts, second_lead, ups, early, up_first, down_first, up_x, down_x, down_y, paths
+        last_far, last_parts, ups, early, up_first, down_first, up_x, down_x, down_y, paths
     ) = final
     *last, late, current = kernel_call(
         last_body,
-        far_shapes(len(GROUPS[2]), height, rank, columns)
+        far_shapes(GROUPS[1][1], height, rank, columns)
         + [
             jax.ShapeDtypeStruct((len(LATE) - 1, rank, columns), wide),
             jax.ShapeDtypeStruct((rank, columns), wide),
         ],
         4 * 10**8,
-        (row, *last_far, *shared, *last_parts, second_lead, ups, early),
+        (row, *last_far, *shared, *last_parts, ups, early),
         scalars=1,
     )
     late_base = kernel_call(
         late_body,
         jax.ShapeDtypeStruct((len(LATE), 2 * rank, columns), wide),
         6 * 10**8,
-        (second_lead, last[2], late, early, mid_inv, mid_basis, mid_back),
+        (last[2], late, early, mid_inv, mid_basis, mid_back),
         room=12,
     )
     rest = kernel_call(
         known_body,
         jax.ShapeDtypeStruct((leaf_count, rank, columns), wide),
         4 * 10**8,
-        (early_base, late_base, mid_back, first[1], second[1], last[1]),
+        (early_base, late_base, mid_back, first[1], last[1]),
         room=12,
     )
 
@@ -550,7 +525,6 @@
             leaf_back,
             *nears,
             first[0],
-            second[0],
             last[0],
         ),
         scalars=1,

time: 136 us -> 131 us (0.963)
  waiting for transfers between devices: 63.9 us -> 60.2 us
    ppermute x4, starting transfers between devices: 15 us -> 9.72 us  [solve(): right = [lax.ppermute(a, 'rhs', behind) for a in own]]
    ppermute x4, waiting for transfers between devices: 16.3 us -> 11.4 us  [solve(): left = [lax.ppermute(a, 'rhs', ahead) for a in own]]
    ppermute x4, starting transfers between devices: 0.08 us -> 4.19 us  [solve(): left = [lax.ppermute(a, 'rhs', ahead) for a in own]]
    ppermute x3 -> x2, starting transfers between devices: 3.7 us -> 6.65 us  [solve(): lax.ppermute(two, 'rhs', behind)]
    ppermute x3 -> x2, starting transfers between devices: 2.38 us -> 0.01 us  [solve(): lax.ppermute(one, 'rhs', ahead)]
    ppermute x3 -> x2, waiting for transfers between devices: 0.01 us -> 1.44 us  [solve(): lax.ppermute(one, 'rhs', ahead)]
    pallas_call x16 -> x15, Pallas kernels: 21.7 us -> 20.6 us  [kernel_call(): pl.pallas_call(body, out_shape=out_shape, cost_estimate=pl.CostEstimate(f...]
    ppermute x3 -> x2, waiting for transfers between devices: 5.14 us -> 4.06 us  [solve(): lax.ppermute(two, 'rhs', behind)]
  transfers between devices with their start and end apart: 27 -> 25, of which waited for: 12 -> 13; matrix products, arithmetic and copies ran while one was open for 2% -> 2% of each run, Pallas kernels for 14% -> 14%
where the time goes in v7:
time: 131 us; the launch traced here: 130 us
  waiting for transfers between devices  60.2 us (46%)
  starting transfers between devices  36.9 us (28%)
  Pallas kernels  25.9 us (20%)
  matrix products  3.84 us (3%)
  local copies, waits for them, and re-layouts  2.8 us (2%)
    ppermute x5, waiting for transfers between devices, top_factors(): got = lax.ppermute(message, 'leaf', pairs)  30.7 us
    pallas_call x15, Pallas kernels, kernel_call(): pl.pallas_call(body, out_shape=out_shape, cost_estimate=pl.CostEstimate(f...  20.6 us
    ppermute x4, waiting for transfers between devices, solve(): left = [lax.ppermute(a, 'rhs', ahead) for a in own]  11.4 us
    ppermute x4, starting transfers between devices, solve(): right = [lax.ppermute(a, 'rhs', behind) for a in own]  9.72 us
    ppermute x7, starting transfers between devices, partners(): lax.ppermute(value, 'leaf', [(i, i ^ m) for i in range(leaf_total)])  8.43 us
    ppermute x5, starting transfers between devices, top_factors(): got = lax.ppermute(message, 'leaf', pairs)  7.22 us
    ppermute x4, waiting for transfers between devices, solve(): right = [lax.ppermute(a, 'rhs', behind) for a in own]  7.2 us
    ppermute x2, starting transfers between devices, solve(): lax.ppermute(two, 'rhs', behind)  6.65 us
  transfers between devices with their start and end apart: 25, of which 13 were waited for; matrix products, arithmetic and copies ran while one was open for 2% of the time, Pallas kernels for 14%

profile of v7, /device:TPU:0, one launch (start us, length us, event | category | flops | bytes accessed | tf_op | source)
XLA Modules:
  0.0 130.4 jit_solution(16368155297456551005)
XLA Ops:
  8.6 5.4 %collective-permute-done.12.got = f32[128,256]{1,0:T(8,128)S(1)} collective-permute-done((f32[128,256]{1,0:T(8,128)S(1)}, f32[128,256]{1,0:T(8,128)S(1)}, u32[]{:S(2)}, u32[]{:S(2)}) %collective-permute-start.12) | collective-permute-done | bytes 131104 | tf_op jit(solution)/shard_map/ppermute | solution.py:368
  14.6 2.0 %collective-permute-start.14 = (f32[128,896]{1,0:T(8,128)S(1)}, f32[128,896]{1,0:T(8,128)S(1)}, u32[]{:S(2)}, u32[]{:S(2)}) collective-permute-start(f32[128,896]{1,0:T(8,128)S(1)} %get-tuple-element.63), channel_id=1, source_target_pairs={{0,32},{32,0},{64,96},{96,64},{1,33},{33,1},{65,97},{97,65},{2,34}... | collective-permute-start | bytes 1376264 | tf_op jit(solution)/shard_map/ppermute | solution.py:368
  16.6 8.4 %collective-permute-done.14.got = f32[128,896]{1,0:T(8,128)S(1)} collective-permute-done((f32[128,896]{1,0:T(8,128)S(1)}, f32[128,896]{1,0:T(8,128)S(1)}, u32[]{:S(2)}, u32[]{:S(2)}) %collective-permute-start.14) | collective-permute-done | bytes 458784 | tf_op jit(solution)/shard_map/ppermute | solution.py:368
  25.6 1.9 %collective-permute-start.15 = (f32[128,1152]{1,0:T(8,128)S(1)}, f32[128,1152]{1,0:T(8,128)S(1)}, u32[]{:S(2)}, u32[]{:S(2)}) collective-permute-start(f32[128,1152]{1,0:T(8,128)S(1)} %get-tuple-element.65), channel_id=1, source_target_pairs={{0,16},{16,0},{32,48},{48,32},{64,80},{80,64},{96,112},{112,96},{1... | collective-permute-start | bytes 1769480 | tf_op jit(solution)/shard_map/ppermute | solution.py:368
  27.6 11.4 %collective-permute-done.15.got = f32[128,1152]{1,0:T(8,128)S(1)} collective-permute-done((f32[128,1152]{1,0:T(8,128)S(1)}, f32[128,1152]{1,0:T(8,128)S(1)}, u32[]{:S(2)}, u32[]{:S(2)}) %collective-permute-start.15) | collective-permute-done | bytes 589856 | tf_op jit(solution)/shard_map/ppermute | solution.py:368
  41.6 4.2 %collective-permute-start.10 = (bf16[4,128,512]{2,1,0:T(8,128)(2,1)S(1)}, bf16[4,128,512]{2,1,0:T(8,128)(2,1)S(1)}, u32[]{:S(2)}, u32[]{:S(2)}) collective-permute-start(bf16[4,128,512]{2,1,0:T(8,128)(2,1)S(1)} %slice.42), channel_id=1, source_target_pairs={{0,3},{1,0},{2,1},{3,2},{4,7},{5,4},{6,5},{7,6},{8,11},{9,8},{10,9... | collective-permute-start | bytes 1572872 | tf_op jit(solution)/shard_map/ppermute | solution.py:417
  46.1 3.3 %collective-permute-start.8 = (bf16[4,128,512]{2,1,0:T(8,128)(2,1)S(1)}, bf16[4,128,512]{2,1,0:T(8,128)(2,1)S(1)}, u32[]{:S(2)}, u32[]{:S(2)}) collective-permute-start(bf16[4,128,512]{2,1,0:T(8,128)(2,1)S(1)} %get-tuple-element.101), channel_id=1, source_target_pairs={{0,3},{1,0},{2,1},{3,2},{4,7},{5,4},{6,5},{7,6},{8,11},{9,8},{10,9... | collective-permute-start | bytes 1572872 | tf_op jit(solution)/shard_map/ppermute | solution.py:417
  49.4 5.6 %collective-permute-done.16.got = f32[128,1792]{1,0:T(8,128)S(1)} collective-permute-done((f32[128,1792]{1,0:T(8,128)S(1)}, f32[128,1792]{1,0:T(8,128)S(1)}, u32[]{:S(2)}, u32[]{:S(2)}) %collective-permute-start.16) | collective-permute-done | bytes 917536 | tf_op jit(solution)/shard_map/ppermute | solution.py:368
  55.8 2.1 %collective-permute-start.5 = (bf16[4,128,512]{2,1,0:T(8,128)(2,1)S(1)}, bf16[4,128,512]{2,1,0:T(8,128)(2,1)S(1)}, u32[]{:S(2)}, u32[]{:S(2)}) collective-permute-start(bf16[4,128,512]{2,1,0:T(8,128)(2,1)S(1)} %get-tuple-element.102), channel_id=1, source_target_pairs={{0,1},{1,2},{2,3},{3,0},{4,5},{5,6},{6,7},{7,4},{8,9},{9,10},{10,1... | collective-permute-start | bytes 1572872 | tf_op jit(solution)/shard_map/ppermute | solution.py:416
  57.9 2.2 %collective-permute-start.2 = (bf16[4,128,512]{2,1,0:T(8,128)(2,1)S(1)}, bf16[4,128,512]{2,1,0:T(8,128)(2,1)S(1)}, u32[]{:S(2)}, u32[]{:S(2)}) collective-permute-start(bf16[4,128,512]{2,1,0:T(8,128)(2,1)S(1)} %get-tuple-element.102), channel_id=1, source_target_pairs={{0,3},{1,0},{2,1},{3,2},{4,7},{5,4},{6,5},{7,6},{8,11},{9,8},{10,9... | collective-permute-start | bytes 1572872 | tf_op jit(solution)/shard_map/ppermute | solution.py:417
  60.1 2.2 %collective-permute-done.11.left = bf16[4,128,512]{2,1,0:T(8,128)(2,1)S(1)} collective-permute-done((bf16[4,128,512]{2,1,0:T(8,128)(2,1)S(1)}, bf16[4,128,512]{2,1,0:T(8,128)(2,1)S(1)}, u32[]{:S(2)}, u32[]{:S(2)}) %collective-permute-start.11) | collective-permute-done | bytes 524320 | tf_op jit(solution)/shard_map/ppermute | solution.py:416
  62.3 2.0 %collective-permute-start = (bf16[4,128,512]{2,1,0:T(8,128)(2,1)S(1)}, bf16[4,128,512]{2,1,0:T(8,128)(2,1)S(1)}, u32[]{:S(2)}, u32[]{:S(2)}) collective-permute-start(bf16[4,128,512]{2,1,0:T(8,128)(2,1)S(1)} %get-tuple-element.103), channel_id=1, source_target_pairs={{0,1},{1,2},{2,3},{3,0},{4,5},{5,6},{6,7},{7,4},{8,9},{9,10},{10,1... | collective-permute-start | bytes 1572872 | tf_op jit(solution)/shard_map/ppermute | solution.py:416
  64.3 9.2 %collective-permute-done.5.left = bf16[4,128,512]{2,1,0:T(8,128)(2,1)S(1)} collective-permute-done((bf16[4,128,512]{2,1,0:T(8,128)(2,1)S(1)}, bf16[4,128,512]{2,1,0:T(8,128)(2,1)S(1)}, u32[]{:S(2)}, u32[]{:S(2)}) %collective-permute-start.5) | collective-permute-done | bytes 524320 | tf_op jit(solution)/shard_map/ppermute | solution.py:416
  73.5 3.2 %collective-permute-start.9 = (bf16[4,128,512]{2,1,0:T(8,128)(2,1)S(1)}, bf16[4,128,512]{2,1,0:T(8,128)(2,1)S(1)}, u32[]{:S(2)}, u32[]{:S(2)}) collective-permute-start(bf16[4,128,512]{2,1,0:T(8,128)(2,1)S(1)} %collective-permute-done.8.right), channel_id=1, source_target_pairs={{0,3},{1,0},{2,1},{3,2},{4,7},{5,4},{6,5},{7,6},{8,11},{9,8},{10,9... | collective-permute-start | bytes 1572872 | tf_op jit(solution)/shard_map/ppermute | solution.py:420
  76.8 7.2 %collective-permute-done.4.right = bf16[4,128,512]{2,1,0:T(8,128)(2,1)S(1)} collective-permute-done((bf16[4,128,512]{2,1,0:T(8,128)(2,1)S(1)}, bf16[4,128,512]{2,1,0:T(8,128)(2,1)S(1)}, u32[]{:S(2)}, u32[]{:S(2)}) %collective-permute-start.4) | collective-permute-done | bytes 524320 | tf_op jit(solution)/shard_map/ppermute | solution.py:417
  84.0 3.4 %collective-permute-start.3 = (bf16[4,128,512]{2,1,0:T(8,128)(2,1)S(1)}, bf16[4,128,512]{2,1,0:T(8,128)(2,1)S(1)}, u32[]{:S(2)}, u32[]{:S(2)}) collective-permute-start(bf16[4,128,512]{2,1,0:T(8,128)(2,1)S(1)} %collective-permute-done.2.right), channel_id=1, source_target_pairs={{0,3},{1,0},{2,1},{3,2},{4,7},{5,4},{6,5},{7,6},{8,11},{9,8},{10,9... | collective-permute-start | bytes 1572872 | tf_op jit(solution)/shard_map/ppermute | solution.py:420
  87.4 2.7 %shard_map.129 = (f32[8,128,256]{2,1,0:T(8,128)S(1)}, f32[16,128,128]{2,1,0:T(8,128)S(1)}) custom-call(f32[15,256,256]{2,1,0:T(8,128)S(1)} %copy-done.4, f32[15,256,128]{2,1,0:T(8,128)S(1)} %copy-done.6, f32[15,256,128]{2,1,0:T(8,128)S(1)} %copy-done.5, f32[15,128,128]{2,1,0:T(8,128)S(1)} %copy-done.8), custom_call_target="tpu_custom_call" | custom-call | flops 800000000 | bytes 8847360 | tf_op jit(solution)/shard_map/pallas_call | solution.py:45
  97.4 2.4 %shard_map.133 = (f32[7,128,128]{2,1,0:T(8,128)S(1)}, f32[7,256,128]{2,1,0:T(8,128)S(1)}) custom-call(f32[8,128,128]{2,1,0:T(8,128)S(1)} %get-tuple-element.61.lead, f32[15,256,256]{2,1,0:T(8,128)S(1)} %copy-done.4, f32[15,256,128]{2,1,0:T(8,128)S(1)} %copy-done.6, f32[15,256,128]{2,1,0:T(8,128)S(1)} %copy-done.5, f32[15,128,128]{2,1,0:T(8,128)S(1)} %copy-done.8), custom_call_target="tpu_custom_call" | custom-call | flops 700000000 | bytes 9371648 | tf_op jit(solution)/shard_map/pallas_call | solution.py:45
  101.7 4.1 %collective-permute-done.3.far_b = bf16[4,128,512]{2,1,0:T(8,128)(2,1)S(1)} collective-permute-done((bf16[4,128,512]{2,1,0:T(8,128)(2,1)S(1)}, bf16[4,128,512]{2,1,0:T(8,128)(2,1)S(1)}, u32[]{:S(2)}, u32[]{:S(2)}) %collective-permute-start.3) | collective-permute-done | bytes 524320 | tf_op jit(solution)/shard_map/ppermute | solution.py:420
  106.8 2.2 %shard_map.139 = (bf16[8,128,128]{2,1,0:T(8,128)(2,1)S(1)}, f32[8,128,128]{2,1,0:T(8,128)S(1)}, f32[8,128,128]{2,1,0:T(8,128)S(1)}, f32[7,128,128]{2,1,0:T(8,128)S(1)}, f32[128,128]{1,0:T(8,128)S(1)}) custom-call(s32[2]{0:T(128)S(1)} %pad_add_fusion.row_ref.spot, bf16[4,128,512]{2,1,0:T(8,128)(2,1)S(1)} %collective-permute-done.1.far_a, ...), custom_call_target="tpu_custom_call" | custom-call | flops 400000000 | bytes 8323080 | tf_op jit(solution)/shard_map/pallas_call | solution.py:45
  111.2 3.5 %collective-permute-start.20 = (f32[128,128]{1,0:T(8,128)S(1)}, f32[128,128]{1,0:T(8,128)S(1)}, u32[]{:S(2)}, u32[]{:S(2)}) collective-permute-start(f32[128,128]{1,0:T(8,128)S(1)} %shard_map.140.refs_2_.refs_0_), channel_id=1, source_target_pairs={{0,16},{4,20},{8,24},{12,28},{16,0},{20,4},{24,8},{28,12},{32,48},... | collective-permute-start | bytes 196616 | tf_op jit(solution)/shard_map/ppermute | solution.py:503
  114.7 2.8 %collective-permute-done.21.refs_5_.refs_3_ = f32[128,128]{1,0:T(8,128)S(1)} collective-permute-done((f32[128,128]{1,0:T(8,128)S(1)}, f32[128,128]{1,0:T(8,128)S(1)}, u32[]{:S(2)}, u32[]{:S(2)}) %collective-permute-start.21) | collective-permute-done | bytes 65568 | tf_op jit(solution)/shard_map/ppermute | solution.py:503
  121.3 2.0 %collective-permute-start.22 = (f32[128,128]{1,0:T(8,128)S(1)}, f32[128,128]{1,0:T(8,128)S(1)}, u32[]{:S(2)}, u32[]{:S(2)}) collective-permute-start(f32[128,128]{1,0:T(8,128)S(1)} %shard_map.142.here), channel_id=1, source_target_pairs={{0,32},{4,36},{8,40},{12,44},{16,48},{20,52},{24,56},{28,60},{32,0... | collective-permute-start | bytes 196616 | tf_op jit(solution)/shard_map/ppermute | solution.py:503
  126.7 3.5 %shard_map.145 = f32[8192,128]{1,0:T(8,128)} custom-call(s32[2]{0:T(128)S(1)} %pad_add_fusion.row_ref.spot, f32[128,512]{1,0:T(8,128)S(1)} %get-tuple-element.77.down_y, f32[128,128]{1,0:T(8,128)S(1)} %shard_map.141.below, f32[128,128]{1,0:T(8,128)S(1)} %shard_map.142.here, f32[128,128]{1,0:T(8,128)S(1)} %collective-permute-done.22.one, ...), custom_call_target="tpu_custom_call" | custom-call | flops 1000000000 | bytes 6881288 | tf_op jit(solution)/shard_map/pallas_call | solution.py:45
  (77 shorter events, 32.9 us)
Async XLA Ops:
  4.0 4.6 %collective-permute-start.13 = (f32[128,256]{1,0:T(8,128)S(1)}, f32[128,256]{1,0:T(8,128)S(1)}, u32[]{:S(2)}, u32[]{:S(2)}) collective-permute-start(f32[128,256]{1,0:T(8,128)S(1)} %convolution_bitcast_fusion.1), channel_id=1, source_target_pairs={{8,24},{24,8},{40,56},{56,40},{72,88},{88,72},{104,120},{120,104},... | collective-permute-start | bytes 393224 | tf_op jit(solution)/shard_map/ppermute | solution.py:356
  5.7 8.4 %collective-permute-start.12 = (f32[128,256]{1,0:T(8,128)S(1)}, f32[128,256]{1,0:T(8,128)S(1)}, u32[]{:S(2)}, u32[]{:S(2)}) collective-permute-start(f32[128,256]{1,0:T(8,128)S(1)} %get-tuple-element.109), channel_id=1, source_target_pairs={{64,0},{65,1},{66,2},{67,3}} | collective-permute-start | bytes 393224 | tf_op jit(solution)/shard_map/ppermute | solution.py:368
  14.6 10.4 %collective-permute-start.14 = (f32[128,896]{1,0:T(8,128)S(1)}, f32[128,896]{1,0:T(8,128)S(1)}, u32[]{:S(2)}, u32[]{:S(2)}) collective-permute-start(f32[128,896]{1,0:T(8,128)S(1)} %get-tuple-element.63), channel_id=1, source_target_pairs={{0,32},{32,0},{64,96},{96,64},{1,33},{33,1},{65,97},{97,65},{2,34}... | collective-permute-start | bytes 1376264 | tf_op jit(solution)/shard_map/ppermute | solution.py:368
  25.6 13.3 %collective-permute-start.15 = (f32[128,1152]{1,0:T(8,128)S(1)}, f32[128,1152]{1,0:T(8,128)S(1)}, u32[]{:S(2)}, u32[]{:S(2)}) collective-permute-start(f32[128,1152]{1,0:T(8,128)S(1)} %get-tuple-element.65), channel_id=1, source_target_pairs={{0,16},{16,0},{32,48},{48,32},{64,80},{80,64},{96,112},{112,96},{1... | collective-permute-start | bytes 1769480 | tf_op jit(solution)/shard_map/ppermute | solution.py:368
  39.7 15.3 %collective-permute-start.16 = (f32[128,1792]{1,0:T(8,128)S(1)}, f32[128,1792]{1,0:T(8,128)S(1)}, u32[]{:S(2)}, u32[]{:S(2)}) collective-permute-start(f32[128,1792]{1,0:T(8,128)S(1)} %get-tuple-element.67), channel_id=1, source_target_pairs={{0,8},{8,0},{16,24},{24,16},{32,40},{40,32},{48,56},{56,48},{64,72... | collective-permute-start | bytes 2752520 | tf_op jit(solution)/shard_map/ppermute | solution.py:368
  41.6 14.2 %collective-permute-start.10 = (bf16[4,128,512]{2,1,0:T(8,128)(2,1)S(1)}, bf16[4,128,512]{2,1,0:T(8,128)(2,1)S(1)}, u32[]{:S(2)}, u32[]{:S(2)}) collective-permute-start(bf16[4,128,512]{2,1,0:T(8,128)(2,1)S(1)} %slice.42), channel_id=1, source_target_pairs={{0,3},{1,0},{2,1},{3,2},{4,7},{5,4},{6,5},{7,6},{8,11},{9,8},{10,9... | collective-permute-start | bytes 1572872 | tf_op jit(solution)/shard_map/ppermute | solution.py:417
  45.8 12.1 %collective-permute-start.6 = (bf16[4,128,512]{2,1,0:T(8,128)(2,1)S(1)}, bf16[4,128,512]{2,1,0:T(8,128)(2,1)S(1)}, u32[]{:S(2)}, u32[]{:S(2)}) collective-permute-start(bf16[4,128,512]{2,1,0:T(8,128)(2,1)S(1)} %slice.42), channel_id=1, source_target_pairs={{0,1},{1,2},{2,3},{3,0},{4,5},{5,6},{6,7},{7,4},{8,9},{9,10},{10,1... | collective-permute-start | bytes 1572872 | tf_op jit(solution)/shard_map/ppermute | solution.py:416
  46.0 16.3 %collective-permute-start.11 = (bf16[4,128,512]{2,1,0:T(8,128)(2,1)S(1)}, bf16[4,128,512]{2,1,0:T(8,128)(2,1)S(1)}, u32[]{:S(2)}, u32[]{:S(2)}) collective-permute-start(bf16[4,128,512]{2,1,0:T(8,128)(2,1)S(1)} %get-tuple-element.101), channel_id=1, source_target_pairs={{0,1},{1,2},{2,3},{3,0},{4,5},{5,6},{6,7},{7,4},{8,9},{9,10},{10,1... | collective-permute-start | bytes 1572872 | tf_op jit(solution)/shard_map/ppermute | solution.py:416
  46.1 16.2 %collective-permute-start.8 = (bf16[4,128,512]{2,1,0:T(8,128)(2,1)S(1)}, bf16[4,128,512]{2,1,0:T(8,128)(2,1)S(1)}, u32[]{:S(2)}, u32[]{:S(2)}) collective-permute-start(bf16[4,128,512]{2,1,0:T(8,128)(2,1)S(1)} %get-tuple-element.101), channel_id=1, source_target_pairs={{0,3},{1,0},{2,1},{3,2},{4,7},{5,4},{6,5},{7,6},{8,11},{9,8},{10,9... | collective-permute-start | bytes 1572872 | tf_op jit(solution)/shard_map/ppermute | solution.py:417
  55.7 44.1 %collective-permute-start.17 = (f32[128,2688]{1,0:T(8,128)S(1)}, f32[128,2688]{1,0:T(8,128)S(1)}, u32[]{:S(2)}, u32[]{:S(2)}) collective-permute-start(f32[128,2688]{1,0:T(8,128)S(1)} %get-tuple-element.69), channel_id=1, source_target_pairs={{0,4},{4,0},{8,12},{12,8},{16,20},{20,16},{24,28},{28,24},{32,36},... | collective-permute-start | bytes 4128776 | tf_op jit(solution)/shard_map/ppermute | solution.py:368
  55.8 17.7 %collective-permute-start.5 = (bf16[4,128,512]{2,1,0:T(8,128)(2,1)S(1)}, bf16[4,128,512]{2,1,0:T(8,128)(2,1)S(1)}, u32[]{:S(2)}, u32[]{:S(2)}) collective-permute-start(bf16[4,128,512]{2,1,0:T(8,128)(2,1)S(1)} %get-tuple-element.102), channel_id=1, source_target_pairs={{0,1},{1,2},{2,3},{3,0},{4,5},{5,6},{6,7},{7,4},{8,9},{9,10},{10,1... | collective-permute-start | bytes 1572872 | tf_op jit(solution)/shard_map/ppermute | solution.py:416
  57.9 15.6 %collective-permute-start.2 = (bf16[4,128,512]{2,1,0:T(8,128)(2,1)S(1)}, bf16[4,128,512]{2,1,0:T(8,128)(2,1)S(1)}, u32[]{:S(2)}, u32[]{:S(2)}) collective-permute-start(bf16[4,128,512]{2,1,0:T(8,128)(2,1)S(1)} %get-tuple-element.102), channel_id=1, source_target_pairs={{0,3},{1,0},{2,1},{3,2},{4,7},{5,4},{6,5},{7,6},{8,11},{9,8},{10,9... | collective-permute-start | bytes 1572872 | tf_op jit(solution)/shard_map/ppermute | solution.py:417
  62.3 21.7 %collective-permute-start.4 = (bf16[4,128,512]{2,1,0:T(8,128)(2,1)S(1)}, bf16[4,128,512]{2,1,0:T(8,128)(2,1)S(1)}, u32[]{:S(2)}, u32[]{:S(2)}) collective-permute-start(bf16[4,128,512]{2,1,0:T(8,128)(2,1)S(1)} %get-tuple-element.103), channel_id=1, source_target_pairs={{0,3},{1,0},{2,1},{3,2},{4,7},{5,4},{6,5},{7,6},{8,11},{9,8},{10,9... | collective-permute-start | bytes 1572872 | tf_op jit(solution)/shard_map/ppermute | solution.py:417
  62.3 25.1 %collective-permute-start = (bf16[4,128,512]{2,1,0:T(8,128)(2,1)S(1)}, bf16[4,128,512]{2,1,0:T(8,128)(2,1)S(1)}, u32[]{:S(2)}, u32[]{:S(2)}) collective-permute-start(bf16[4,128,512]{2,1,0:T(8,128)(2,1)S(1)} %get-tuple-element.103), channel_id=1, source_target_pairs={{0,1},{1,2},{2,3},{3,0},{4,5},{5,6},{6,7},{7,4},{8,9},{9,10},{10,1... | collective-permute-start | bytes 1572872 | tf_op jit(solution)/shard_map/ppermute | solution.py:416
  73.5 22.5 %collective-permute-start.7 = (bf16[4,128,512]{2,1,0:T(8,128)(2,1)S(1)}, bf16[4,128,512]{2,1,0:T(8,128)(2,1)S(1)}, u32[]{:S(2)}, u32[]{:S(2)}) collective-permute-start(bf16[4,128,512]{2,1,0:T(8,128)(2,1)S(1)} %collective-permute-done.6.left), channel_id=1, source_target_pairs={{0,1},{1,2},{2,3},{3,0},{4,5},{5,6},{6,7},{7,4},{8,9},{9,10},{10,1... | collective-permute-start | bytes 1572872 | tf_op jit(solution)/shard_map/ppermute | solution.py:420
  73.5 22.5 %collective-permute-start.9 = (bf16[4,128,512]{2,1,0:T(8,128)(2,1)S(1)}, bf16[4,128,512]{2,1,0:T(8,128)(2,1)S(1)}, u32[]{:S(2)}, u32[]{:S(2)}) collective-permute-start(bf16[4,128,512]{2,1,0:T(8,128)(2,1)S(1)} %collective-permute-done.8.right), channel_id=1, source_target_pairs={{0,3},{1,0},{2,1},{3,2},{4,7},{5,4},{6,5},{7,6},{8,11},{9,8},{10,9... | collective-permute-start | bytes 1572872 | tf_op jit(solution)/shard_map/ppermute | solution.py:420
  84.0 21.8 %collective-permute-start.3 = (bf16[4,128,512]{2,1,0:T(8,128)(2,1)S(1)}, bf16[4,128,512]{2,1,0:T(8,128)(2,1)S(1)}, u32[]{:S(2)}, u32[]{:S(2)}) collective-permute-start(bf16[4,128,512]{2,1,0:T(8,128)(2,1)S(1)} %collective-permute-done.2.right), channel_id=1, source_target_pairs={{0,3},{1,0},{2,1},{3,2},{4,7},{5,4},{6,5},{7,6},{8,11},{9,8},{10,9... | collective-permute-start | bytes 1572872 | tf_op jit(solution)/shard_map/ppermute | solution.py:420
  87.4 19.4 %collective-permute-start.1 = (bf16[4,128,512]{2,1,0:T(8,128)(2,1)S(1)}, bf16[4,128,512]{2,1,0:T(8,128)(2,1)S(1)}, u32[]{:S(2)}, u32[]{:S(2)}) collective-permute-start(bf16[4,128,512]{2,1,0:T(8,128)(2,1)S(1)} %collective-permute-done.left), channel_id=1, source_target_pairs={{0,1},{1,2},{2,3},{3,0},{4,5},{5,6},{6,7},{7,4},{8,9},{9,10},{10,1... | collective-permute-start | bytes 1572872 | tf_op jit(solution)/shard_map/ppermute | solution.py:420
  110.5 7.0 %collective-permute-start.21 = (f32[128,128]{1,0:T(8,128)S(1)}, f32[128,128]{1,0:T(8,128)S(1)}, u32[]{:S(2)}, u32[]{:S(2)}) collective-permute-start(f32[128,128]{1,0:T(8,128)S(1)} %shard_map.140.refs_2_.refs_0_), channel_id=1, source_target_pairs={{0,24},{4,28},{8,16},{12,20},{16,8},{20,12},{24,0},{28,4},{32,56},... | collective-permute-start | bytes 196616 | tf_op jit(solution)/shard_map/ppermute | solution.py:503
  111.2 6.3 %collective-permute-start.20 = (f32[128,128]{1,0:T(8,128)S(1)}, f32[128,128]{1,0:T(8,128)S(1)}, u32[]{:S(2)}, u32[]{:S(2)}) collective-permute-start(f32[128,128]{1,0:T(8,128)S(1)} %shard_map.140.refs_2_.refs_0_), channel_id=1, source_target_pairs={{0,16},{4,20},{8,24},{12,28},{16,0},{20,4},{24,8},{28,12},{32,48},... | collective-permute-start | bytes 196616 | tf_op jit(solution)/shard_map/ppermute | solution.py:503
  114.7 4.3 %collective-permute-start.19 = (f32[128,128]{1,0:T(8,128)S(1)}, f32[128,128]{1,0:T(8,128)S(1)}, u32[]{:S(2)}, u32[]{:S(2)}) collective-permute-start(f32[128,128]{1,0:T(8,128)S(1)} %shard_map.140.refs_2_.refs_0_), channel_id=1, source_target_pairs={{0,8},{4,12},{8,0},{12,4},{16,24},{20,28},{24,16},{28,20},{32,40},... | collective-permute-start | bytes 196616 | tf_op jit(solution)/shard_map/ppermute | solution.py:503
  119.2 7.5 %collective-permute-start.24 = (f32[128,128]{1,0:T(8,128)S(1)}, f32[128,128]{1,0:T(8,128)S(1)}, u32[]{:S(2)}, u32[]{:S(2)}) collective-permute-start(f32[128,128]{1,0:T(8,128)S(1)} %shard_map.142.here), channel_id=1, source_target_pairs={{0,96},{4,100},{8,104},{12,108},{16,112},{20,116},{24,120},{28,124... | collective-permute-start | bytes 196616 | tf_op jit(solution)/shard_map/ppermute | solution.py:503
  120.7 6.0 %collective-permute-start.23 = (f32[128,128]{1,0:T(8,128)S(1)}, f32[128,128]{1,0:T(8,128)S(1)}, u32[]{:S(2)}, u32[]{:S(2)}) collective-permute-start(f32[128,128]{1,0:T(8,128)S(1)} %shard_map.142.here), channel_id=1, source_target_pairs={{0,64},{4,68},{8,72},{12,76},{16,80},{20,84},{24,88},{28,92},{32,9... | collective-permute-start | bytes 196616 | tf_op jit(solution)/shard_map/ppermute | solution.py:503
  121.3 5.3 %collective-permute-start.22 = (f32[128,128]{1,0:T(8,128)S(1)}, f32[128,128]{1,0:T(8,128)S(1)}, u32[]{:S(2)}, u32[]{:S(2)}) collective-permute-start(f32[128,128]{1,0:T(8,128)S(1)} %shard_map.142.here), channel_id=1, source_target_pairs={{0,32},{4,36},{8,40},{12,44},{16,48},{20,52},{24,56},{28,60},{32,0... | collective-permute-start | bytes 196616 | tf_op jit(solution)/shard_map/ppermute | solution.py:503
  (12 other events, 272.8 us)
